TPU v7x, 256 devices: a whole 4x4x8 slice. The times are simulated.
256 devices in a mesh: dp: 64 (over z, y, core), query: 4 (over x).
Axes of the slice: x: 4, y: 4, z: 8, core: 2. Of those that a mesh axis runs over, the one named last changes fastest.
Arguments:
- sensors: bfloat16 [24576, 4096], P('dp'), may hold values from -8 to 8
- query_index: int32 [2, 8192], P(None, 'query'), may hold values from 0 to 127
- targets: bfloat16 [24576, 8192], P('dp', 'query'), may hold values from -6 to 6
- w_one: bfloat16 [4096, 1024], P(None, 'query'), may hold values from -0.09375 to 0.09375
- b_one: float32 [1024], P('query'), may hold values from -3 to 3
- w_two: bfloat16 [1024, 512], P('query'), may hold values from -0.1875 to 0.1875
- b_two: float32 [512], replicated, may hold values from -3 to 3
- v_one: float32 [2, 512], replicated, may hold values from -4 to 4
- c_one: float32 [512], replicated, may hold values from -3 to 3
- v_two: bfloat16 [512, 512], replicated, may hold values from -0.25 to 0.25
- c_two: float32 [512], replicated, may hold values from -3 to 3
- v_three: bfloat16 [512, 512], replicated, may hold values from -0.25 to 0.25
- c_three: float32 [512], replicated, may hold values from -3 to 3
Outputs:
- loss: float32 [], replicated
- grad_w_one: float32 [4096, 1024], P('dp', 'query')
- grad_b_one: float32 [1024], P('query')
- grad_w_two: float32 [1024, 512], P('query', 'dp')
- grad_b_two: float32 [512], replicated
- grad_v_one: float32 [2, 512], replicated
- grad_c_one: float32 [512], replicated
- grad_v_two: float32 [512, 512], replicated
- grad_c_two: float32 [512], replicated
- grad_v_three: float32 [512, 512], replicated
- grad_c_three: float32 [512], replicated
All inputs are finite; a program needn't handle non-finite values.
Results may differ from a plain program's by a relative error of at most 0.00075.
Values may be sent and summed in bfloat16 or wider, within the bound.
No kernel may reach another device: no remote copies, remote signals or barrier semaphores. Data moves between devices by JAX's collectives and lax.ppermute only.
A program may use at most 128 MiB of HBM per device.

v0:
```python
import functools
import math

import jax
import jax.numpy as jnp
from jax import lax
from jax.experimental import pallas as pl
from jax.experimental.pallas import tpu as pltpu
from jax.sharding import Mesh
from jax.sharding import PartitionSpec as P


GRID = 128
DP = ("z", "y", "c")
ALL = ("z", "y", "c", "query")


def shift(x, axis, k):
    n = lax.axis_size(axis)
    return lax.ppermute(x, axis, [(i, (i + k) % n) for i in range(n)])


def part(x, i):
    return lax.dynamic_index_in_dim(x, i, 0, False)


def scattered_sum(chunks, axis):
    n, i = lax.axis_size(axis), lax.axis_index(axis)
    arrived = [shift(part(chunks, (i + k) % n), axis, k) for k in range(1, n)]
    total = part(chunks, i)
    for a in arrived:
        total = total + a
    return total


def exchanged(x, axis):
    return lax.all_to_all(x, axis, 0, 0, tiled=True)


def told_to_all(x, axis):
    return exchanged(jnp.broadcast_to(x[None], (lax.axis_size(axis), *x.shape)), axis)


def other_core(x):
    return lax.ppermute(x, "c", [(0, 1), (1, 0)])


def contract_rows(left, right, precision=None):
    return lax.dot_general(
        left,
        right,
        (((0,), (0,)), ((), ())),
        precision=precision,
        preferred_element_type=jnp.float32,
    )


def contract_cols(left, right, precision=None):
    return lax.dot_general(
        left,
        right,
        (((1,), (1,)), ((), ())),
        precision=precision,
        preferred_element_type=jnp.float32,
    )


def trunk_forward(coords, v_one, c_one, v_two, c_two, v_three, c_three):
    first_act = jnp.tanh(
        coords[0][:, None] * v_one[0][None, :] + coords[1][:, None] * v_one[1][None, :] + c_one
    )
    first_b = first_act.astype(jnp.bfloat16)
    second_act = jnp.tanh(jnp.dot(first_b, v_two, preferred_element_type=jnp.float32) + c_two)
    second_b = second_act.astype(jnp.bfloat16)
    basis_full = jnp.dot(second_b, v_three, preferred_element_type=jnp.float32) + c_three
    return basis_full.astype(jnp.bfloat16)


def back_kernel(core, coords, misfit, coeffs, rows_in, v_two, v_three, mine, give, acc3, acc2, accs, *, inv_scale):
    step = pl.program_id(0)

    @pl.when(step == 0)
    def _():
        acc3[...] = jnp.zeros_like(acc3)
        acc2[...] = jnp.zeros_like(acc2)
        accs[...] = jnp.zeros_like(accs)

    points = coords[...].T
    x, y = points[:, 0:1], points[:, 1:2]
    first = jnp.tanh(x * rows_in[0:1, :] + y * rows_in[1:2, :] + rows_in[2:3, :])
    first_b = first.astype(jnp.bfloat16)
    second = jnp.tanh(jnp.dot(first_b, v_two[...], preferred_element_type=jnp.float32) + rows_in[3:4, :])
    second_b = second.astype(jnp.bfloat16)
    grad = contract_rows(misfit[...], coeffs[...]) * inv_scale
    grad_b = grad.astype(jnp.bfloat16)
    acc3[...] += contract_rows(second_b, grad_b)
    accs[4:5, :] += jnp.sum(grad, axis=0, keepdims=True)
    grad = contract_cols(grad_b, v_three[...]) * (1.0 - second * second)
    grad_b = grad.astype(jnp.bfloat16)
    acc2[...] += contract_rows(first_b, grad_b)
    accs[3:4, :] += jnp.sum(grad, axis=0, keepdims=True)
    grad = contract_cols(grad_b, v_two[...]) * (1.0 - first * first)
    accs[2:3, :] += jnp.sum(grad, axis=0, keepdims=True)
    accs[0:1, :] += jnp.sum(x * grad, axis=0, keepdims=True)
    accs[1:2, :] += jnp.sum(y * grad, axis=0, keepdims=True)

    rows = acc3.shape[0]

    @pl.when(step == pl.num_programs(0) - 1)
    def _():
        mine[rows:, :] = accs[...]
        give[rows:, :] = accs[...]

        @pl.when(core[0] == 0)
        def _():
            mine[:rows, :] = acc3[...]
            give[:rows, :] = acc2[...]

        @pl.when(core[0] != 0)
        def _():
            mine[:rows, :] = acc2[...]
            give[:rows, :] = acc3[...]


def trunk_backward(core, coords, misfit_b, coeffs_b, v_one, c_one, v_two, c_two, v_three, inv_scale):
    queries = misfit_b.shape[1]
    funcs, basis = coeffs_b.shape
    trunk = v_two.shape[0]
    block = 512

    def whole(*shape):
        return pl.BlockSpec(shape, lambda i, core: (0,) * len(shape))

    rows_in = jnp.concatenate([v_one, c_one[None], c_two[None], jnp.zeros((4, trunk), jnp.float32)])
    out = jax.ShapeDtypeStruct((trunk + 8, basis), jnp.float32)
    return pl.pallas_call(
        functools.partial(back_kernel, inv_scale=inv_scale),
        grid_spec=pltpu.PrefetchScalarGridSpec(
            num_scalar_prefetch=1,
            grid=(queries // block,),
            in_specs=[
                pl.BlockSpec((8, block), lambda i, core: (0, i)),
                pl.BlockSpec((funcs, block), lambda i, core: (0, i)),
                whole(funcs, basis),
                whole(8, trunk),
                whole(trunk, trunk),
                whole(trunk, basis),
            ],
            out_specs=[whole(trunk + 8, basis), whole(trunk + 8, basis)],
            scratch_shapes=[
                pltpu.VMEM((trunk, basis), jnp.float32),
                pltpu.VMEM((trunk, trunk), jnp.float32),
                pltpu.VMEM((8, basis), jnp.float32),
            ],
        ),
        out_shape=[out, out],
        cost_estimate=pl.CostEstimate(flops=12 * queries * trunk * basis, bytes_accessed=8_000_000, transcendentals=2 * queries * trunk),
        compiler_params=pltpu.CompilerParams(vmem_limit_bytes=60 * 2**20),
        name="trunk_backward",
    )(core.reshape(1), coords, misfit_b, coeffs_b, rows_in, v_two, v_three)


def scaled(x, axes=None):
    top = jnp.max(jnp.abs(x), axis=axes, keepdims=True)
    e = jnp.clip(jnp.floor(jnp.log2(jnp.maximum(top, 1e-30))), -100.0, 127.0) - 14.0
    return x * jnp.exp2(-e), e


def power(e):
    return jnp.exp2(e.astype(jnp.float32))


def summed_in_pairs(x, axis):
    n, k = lax.axis_size(axis), 1
    while k < n:
        x = x + lax.ppermute(x, axis, [(i, i ^ k) for i in range(n)])
        k *= 2
    return x


def with_tail(out, j, big_e, piece, piece_e):
    rows, w = out.shape[1] - 8, out.shape[2]
    out[j, rows:, :] = jnp.zeros((8, w), jnp.float32)
    out[j, rows : rows + 1, : piece.shape[1]] = piece
    out[j, rows + 1 : rows + 2, :] = jnp.broadcast_to(big_e, (1, w))
    out[j, rows + 2 : rows + 3, :] = jnp.broadcast_to(piece_e, (1, w))


def plane_messages(mine, got, late, n):
    w = mine.shape[1]
    rows = mine.shape[0] - 8
    per = n // 8
    k = w // per

    def body(mine, got, late, out):
        big, big_e = scaled(mine[:rows, :] + got[:rows, :])
        small, small_e = scaled(mine[rows:, :] + got[rows:, :] + late[...], 1)
        out[:, : rows // n, :] = big.reshape(n, rows // n, w)
        for j in range(n):
            i, at = j // per, j % per * k
            with_tail(out, j, big_e, small[i : i + 1, at : at + k], small_e[i : i + 1])

    out = pl.pallas_call(
        body,
        out_shape=jax.ShapeDtypeStruct((n, rows // n + 8, w), jnp.float32),
        compiler_params=pltpu.CompilerParams(vmem_limit_bytes=12 * 2**20),
        name="plane_messages",
    )(mine, got, late)
    return out.astype(jnp.float16)


def total_message(both, side):
    rows, w = both.shape[0] - 8, both.shape[1]

    def body(both, out):
        big, big_e = scaled(both[:rows, :])
        small, small_e = scaled(both[rows : rows + 1, :side])
        out[0, :rows, :] = big
        with_tail(out, 0, big_e, small, small_e)

    out = pl.pallas_call(
        body,
        out_shape=jax.ShapeDtypeStruct((1, rows + 8, w), jnp.float32),
        compiler_params=pltpu.CompilerParams(vmem_limit_bytes=12 * 2**20),
        name="total_message",
    )(both)
    return out[0].astype(jnp.float16)


def z_messages(core, w_one_part, got, w_two_part, b_one_row):
    nz, _, rows, w = w_one_part.shape
    m = w_two_part.shape[1]

    def body(core, part, got, two, bias, out):
        one, one_e = scaled(part[:, 0] + got[...])
        two, two_e = scaled(two[...])
        bias, bias_e = scaled(bias[...])
        out[:, :rows, :] = one
        out[:, rows : rows + m, :] = two
        for j in range(nz):
            out[j, rows + m :, :] = jnp.zeros((8, w), jnp.float32)
            for i, row in enumerate((bias, bias_e, two_e, one_e)):
                out[j, rows + m + i : rows + m + i + 1, :] = jnp.broadcast_to(row.reshape(1, -1), (1, w))

    out = pl.pallas_call(
        body,
        grid_spec=pltpu.PrefetchScalarGridSpec(
            num_scalar_prefetch=1,
            grid=(1,),
            in_specs=[
                pl.BlockSpec((nz, 1, rows, w), lambda i, core: (0, core[0], 0, 0)),
                pl.BlockSpec((nz, rows, w), lambda i, core: (0, 0, 0)),
                pl.BlockSpec((nz, m, w), lambda i, core: (0, 0, 0)),
                pl.BlockSpec((1, w), lambda i, core: (0, 0)),
            ],
            out_specs=pl.BlockSpec((nz, rows + m + 8, w), lambda i, core: (0, 0, 0)),
        ),
        out_shape=jax.ShapeDtypeStruct((nz, rows + m + 8, w), jnp.float32),
        compiler_params=pltpu.CompilerParams(vmem_limit_bytes=12 * 2**20),
        name="z_messages",
    )(core.reshape(1), w_one_part, got, w_two_part, b_one_row)
    return out.astype(jnp.float16)


def read(got, rows, side):
    big = got[:, :rows].astype(jnp.float32) * power(got[:, rows + 1 : rows + 2, :1])
    small = got[:, rows, :side].astype(jnp.float32) * power(got[:, rows + 2, :1])
    return big, small


def finished(core, got, other, side):
    n, rows, w = got.shape[0], got.shape[1] - 8, got.shape[2]
    per = n // 8

    def body(core, got, other, one, two, v_one, c_one, c_two, c_three, b_two, loss):
        def put(zero, last):
            for x, out in ((zero, one), (last, two)):
                out[...] = (x[:, :rows, :] * jnp.exp2(x[:, rows + 1 : rows + 2, :])).reshape(n * rows, w)
            small = zero[:, rows : rows + 1, :side] * jnp.exp2(zero[:, rows + 2 : rows + 3, :side])
            more = last[:, rows : rows + 1, :side] * jnp.exp2(last[:, rows + 2 : rows + 3, :side])
            both = small + more
            for p in range(per):
                at = slice(p * side, (p + 1) * side)
                v_one[0:1, at] = small[p]
                v_one[1:2, at] = small[per + p]
                c_one[:, at] = small[2 * per + p]
                c_two[:, at] = small[3 * per + p]
                c_three[:, at] = small[4 * per + p]
                b_two[:, at] = both[5 * per + p]
                loss[:, at] = both[6 * per + p]

        @pl.when(core[0] == 0)
        def _():
            put(got, other)

        @pl.when(core[0] != 0)
        def _():
            put(other, got)

    def whole(*shape):
        return pl.BlockSpec(shape, lambda i, core: (0,) * len(shape))

    shapes = [(n * rows, w), (n * rows, w), (2, w)] + [(1, w)] * 5
    return pl.pallas_call(
        body,
        grid_spec=pltpu.PrefetchScalarGridSpec(
            num_scalar_prefetch=1,
            grid=(1,),
            in_specs=[whole(*got.shape), whole(*got.shape)],
            out_specs=[whole(*shape) for shape in shapes],
        ),
        out_shape=[jax.ShapeDtypeStruct(shape, jnp.float32) for shape in shapes],
        compiler_params=pltpu.CompilerParams(vmem_limit_bytes=24 * 2**20),
        name="finished",
    )(core.reshape(1), got, other)


def z_finished(got, rows):
    nz, all_rows, w = got.shape
    m = all_rows - rows - 8

    def body(got, one, two, bias):
        def part(lo, hi, e):
            total = got[0, lo:hi, :] * jnp.exp2(got[0, e : e + 1, :])
            for j in range(1, nz):
                total = total + got[j, lo:hi, :] * jnp.exp2(got[j, e : e + 1, :])
            return total

        k = rows + m
        one[...] = part(0, rows, k + 3)
        two[...] = part(rows, k, k + 2)
        bias[...] = part(k, k + 1, k + 1)

    return pl.pallas_call(
        body,
        out_shape=[jax.ShapeDtypeStruct(shape, jnp.float32) for shape in ((rows, w), (m, w), (1, w))],
        compiler_params=pltpu.CompilerParams(vmem_limit_bytes=12 * 2**20),
        name="z_finished",
    )(got)


def sum_of_all(mine, give, late):
    w = mine.shape[1]
    rows = mine.shape[0] - 8
    n = lax.axis_size("y") * lax.axis_size("query")
    per, side = rows // n, 8 * w // n
    plane = ("y", "query")
    got = other_core(give)

    got = exchanged(plane_messages(mine, got, late, n), plane)
    big, small = read(got, per, side)
    big, small = jnp.sum(big, axis=0), jnp.sum(small, axis=0)
    both = jnp.concatenate([big, jnp.pad(small[None], ((0, 7), (0, w - side)))])
    both = summed_in_pairs(both, "z")
    got = told_to_all(total_message(both, side), plane)
    other = other_core(got)
    return finished(
        lax.axis_index("c"), got.astype(jnp.float32), other.astype(jnp.float32), side
    )


def local(
    sensors,
    query_index,
    targets,
    w_one,
    b_one,
    w_two,
    b_two,
    v_one,
    c_one,
    v_two,
    c_two,
    v_three,
    c_three,
):
    funcs, sensor_count = sensors.shape
    hidden_count, basis_count = w_two.shape
    query_rows = query_index.shape[1]
    nz, ny, nc, nx = (lax.axis_size(a) for a in ALL)
    count_all = funcs * nz * ny * nc * query_rows * nx
    grad_scale = 64.0 / math.sqrt(count_all)
    inv_scale = 1.0 / math.sqrt(basis_count)
    coords = query_index.astype(jnp.float32) / (GRID - 1)

    w_two_all = [w_two] + [shift(w_two, "query", k) for k in range(1, nx)]
    hidden = jnp.tanh(jnp.dot(sensors, w_one, preferred_element_type=jnp.float32) + b_one)
    hidden_b = hidden.astype(jnp.bfloat16)
    hidden_all = [hidden_b] + [shift(hidden_b, "query", k) for k in range(1, nx)]
    basis = trunk_forward(
        coords, v_one, c_one, v_two, c_two, v_three, c_three
    )

    rows_own = sensor_count // (nz * ny * nc)
    iy = lax.axis_index("y")
    sensors_late, _ = lax.optimization_barrier((sensors, hidden_b))
    columns = sensors_late.reshape(funcs, nz, ny, nc * rows_own)

    def columns_of(y):
        return lax.dynamic_index_in_dim(columns, y, 2, False).reshape(funcs, -1)

    sens_y = [columns_of(iy)] + [
        shift(columns_of((iy + k) % ny), "y", k) for k in range(1, ny)
    ]

    coeffs = b_two
    for h, w in zip(hidden_all, w_two_all):
        coeffs = coeffs + jnp.dot(h, w, preferred_element_type=jnp.float32)
    coeffs_b = coeffs.astype(jnp.bfloat16)
    prediction = contract_cols(coeffs_b, basis) * inv_scale
    misfit = prediction - targets.astype(jnp.float32)
    loss_part = jnp.sum(misfit * misfit)
    misfit_b = (misfit * grad_scale).astype(jnp.bfloat16)
    grad_part = jnp.dot(misfit_b, basis, preferred_element_type=jnp.float32) * inv_scale
    grad_own = exchanged(grad_part.reshape(nx, -1, basis_count), "query")
    grad_own = jnp.sum(grad_own, axis=0)
    b_two_part = jnp.sum(grad_own, axis=0)
    grad_coeffs_b = told_to_all(grad_own.astype(jnp.bfloat16), "query").reshape(funcs, basis_count)

    ic = lax.axis_index("c")
    mine, give = trunk_backward(
        ic, jnp.pad(coords, ((0, 6), (0, 0))), misfit_b, coeffs_b, v_one, c_one, v_two, c_two, v_three, inv_scale
    )
    late = jnp.stack([b_two_part, jnp.broadcast_to(loss_part, (basis_count,))])
    totals = sum_of_all(mine, give, jnp.pad(late, ((5, 1), (0, 0))))
    g_v_three, g_v_two, g_v_one, g_c_one, g_c_two, g_c_three, g_b_two, loss = totals

    grad_pre = contract_cols(grad_coeffs_b, w_two) * (1.0 - hidden * hidden)
    b_one_part = jnp.sum(grad_pre, axis=0)
    grad_pre_b = grad_pre.astype(jnp.bfloat16)

    pre_y = [grad_pre_b] + [shift(grad_pre_b, "y", k) for k in range(1, ny)]

    w_two_part = contract_rows(grad_coeffs_b, hidden_b)
    w_two_part = w_two_part.reshape(nz, ny, nc, -1, hidden_count)
    b_one_rows = jnp.pad(b_one_part[None], ((0, 7), (0, 0)))

    def with_bias(rows, n):
        rows = rows.reshape(n, -1, hidden_count)
        bias = jnp.broadcast_to(b_one_rows, (n, 8, hidden_count))
        return jnp.concatenate([rows, bias], axis=1)

    both = scattered_sum(with_bias(w_two_part.transpose(2, 0, 1, 3, 4), nc), "c")
    w_two_part, b_one_rows = both[:-8].reshape(nz, ny, -1, hidden_count), both[-8:]
    both = scattered_sum(with_bias(w_two_part.transpose(1, 0, 2, 3), ny), "y")
    w_two_part, b_one_row = both[:-8].reshape(nz, -1, hidden_count), both[-8:-7]

    w_one_part = contract_rows(sens_y[0], pre_y[0])
    for k in range(1, ny):
        w_one_part = w_one_part + contract_rows(sens_y[k], pre_y[k])
    w_one_part = w_one_part.reshape(nz, nc, rows_own, hidden_count)
    got = other_core(lax.dynamic_index_in_dim(w_one_part, 1 - ic, 1, False))
    sent = z_messages(ic, w_one_part, got, w_two_part, b_one_row)
    got = exchanged(sent, "z")
    grad_w_one, grad_w_two, grad_b_one = z_finished(got.astype(jnp.float32), rows_own)
    return (
        loss[0, 0] / count_all,
        grad_w_one,
        grad_b_one[0],
        grad_w_two.T,
        g_b_two[0],
        g_v_one,
        g_c_one[0],
        g_v_two,
        g_c_two[0],
        g_v_three,
        g_c_three[0],
    )


def solution(mesh):
    torus = Mesh(mesh.devices.reshape(8, 4, 2, mesh.shape["query"]), ALL)
    return jax.shard_map(
        local,
        mesh=torus,
        in_specs=(
            P(DP, None),
            P(None, "query"),
            P(DP, "query"),
            P(None, "query"),
            P("query"),
            P("query", None),
            P(),
            P(),
            P(),
            P(),
            P(),
            P(),
            P(),
        ),
        out_specs=(
            P(),
            P(DP, "query"),
            P("query"),
            P("query", DP),
            P(),
            P(),
            P(),
            P(),
            P(),
            P(),
            P(),
        ),
        check_vma=False,
    )
```

profile of v0, /device:TPU:1, one launch (start us, length us, event | category | flops | bytes accessed | tf_op | source)
XLA Modules:
  0.0 194.6 jit_solution(11040806325061641945)
XLA Ops:
  0.7 1.5 copy-done
  2.2 3.7 %fusion.40 = (bf16[384,256]{1,0:T(8,128)(2,1)S(1)}, f32[384,256]{1,0:T(8,128)}) fusion(f32[256]{0:T(256)} %param.17, bf16[384,4096]{1,0:T(8,128)(2,1)} %param.13, bf16[4096,256]{1,0:T(8,128)(2,1)S(1)} %copy-done), kind=kOutput, calls=%fused_computation.86 | convolution fusion | flops 805502976 | bytes 5833728 | tf_op jit(solution)/shard_map/dot_general | solution.py:387
  5.9 3.6 %collective-permute-start.2 = (bf16[384,256]{1,0:T(8,128)(2,1)S(1)}, bf16[384,256]{1,0:T(8,128)(2,1)}, u32[]{:S(2)}, u32[]{:S(2)}) collective-permute-start(bf16[384,256]{1,0:T(8,128)(2,1)S(1)} %get-tuple-element.58), channel_id=1, source_target_pairs={{0,2},{1,3},{2,0},{3,1},{4,6},{5,7},{6,4},{7,5},{8,10},{9,11},{10,... | collective-permute-start | bytes 589832 | tf_op jit(solution)/shard_map/ppermute | solution.py:20
  9.5 0.9 collective-permute-start.4
  10.3 1.2 collective-permute-start.3
  11.6 1.8 collective-permute-start.5
  13.4 5.0 %add_convert_fusion = bf16[2048,512]{1,0:T(8,128)(2,1)} fusion(bf16[512,512]{1,0:T(8,128)(2,1)S(1)} %copy-done.14, f32[512]{0:T(512)S(1)} %copy-done.15, bf16[512,512]{1,0:T(8,128)(2,1)} %v_two.1, f32[512]{0:T(512)S(1)} %copy-done.11, f32[512]{0:T(512)S(1)} %copy-done.12, f32[512]{0:T(512)S(1)} %bitcast.119, f32[2048]{0:T(1024)S(1)} %bitcast.114, ...), kind=kOutput, calls=%fused_computation | convolution fusion | flops 2156920832 | bytes 3172352 | tf_op jit(solution)/shard_map/dot_general | solution.py:75
  18.8 0.7 maximum_maximum_fusion.rows_in
  19.5 0.6 pad.17.coords
  20.3 1.4 fusion.41
  21.8 8.0 %collective-permute-done.5 = bf16[256,512]{1,0:T(8,128)(2,1)} collective-permute-done((bf16[256,512]{1,0:T(8,128)(2,1)S(1)}, bf16[256,512]{1,0:T(8,128)(2,1)}, u32[]{:S(2)}, u32[]{:S(2)}) %collective-permute-start.5) | collective-permute-done | bytes 262176 | tf_op jit(solution)/shard_map/ppermute | solution.py:20
  29.7 1.3 fusion.42
  31.1 1.2 fusion.8.coeffs
  32.3 1.8 multiply_reduce_fusion
  34.1 1.9 convolution_multiply_fusion
  36.0 4.6 %all-to-all-start = ((f32[4,96,512]{2,1,0:T(8,128)}), f32[4,96,512]{2,1,0:T(8,128)S(1)}, u32[]{:S(2)}, u32[]{:S(2)}) async-start(f32[4,96,512]{2,1,0:T(8,128)} %bitcast.109), calls=%async_computation | async-start | bytes 1572864 | tf_op jit(solution)/shard_map/all_to_all | solution.py:37
  40.6 12.9 %trunk_backward.1 = (f32[520,512]{1,0:T(8,128)}, f32[520,512]{1,0:T(8,128)}) custom-call(s32[1]{0:T(128)} %bitcast.core, f32[8,2048]{1,0:T(8,128)} %pad.17.coords, bf16[384,2048]{1,0:T(8,128)(2,1)} %copy-done.17, bf16[384,512]{1,0:T(8,128)(2,1)} %copy-done.7, f32[8,512]{1,0:T(8,128)} %maximum_maximum_fusion.rows_in, bf16[512,512]{1,0:T(8,128)(2,1)} %v_two.1, ...), custom_call_target="tpu_custom_call" | custom-call | flops 6442450944 | bytes 8000000 | tf_op jit(solution)/shard_map/trunk_backward/pallas_call | solution.py:136
  53.5 0.8 collective-permute-start.6
  54.3 4.6 %copy.30 = bf16[384,4096]{0,1:T(8,128)(2,1)} copy(bf16[384,4096]{1,0:T(8,128)(2,1)} %param.13) | data formatting | bytes 6291456 | tf_op jit(solution)/shard_map/optimization_barrier | solution.py:396
  59.0 0.8 broadcast_in_dim.46
  59.9 4.5 %all-to-all-start.3 = ((bf16[4,96,512]{2,1,0:T(8,128)(2,1)}), bf16[4,96,512]{2,1,0:T(8,128)(2,1)}, u32[]{:S(2)}, u32[]{:S(2)}) async-start(bf16[4,96,512]{2,1,0:T(8,128)(2,1)} %broadcast_in_dim.46), calls=%async_computation.3 | async-start | bytes 786432 | tf_op jit(solution)/shard_map/all_to_all | solution.py:37
  64.3 3.8 %constant_dynamic-slice_fusion.1 = (bf16[384,8,1,128]{0,3,2,1:T(8,128)(2,1)}, bf16[384,8,1,128]{0,3,2,1:T(8,128)(2,1)}, bf16[384,8,1,128]{0,3,2,1:T(8,128)(2,1)}, bf16[384,8,1,128]{0,3,2,1:T(8,128)(2,1)}) fusion(bf16[384,8,4,128]{0,3,2,1:T(8,128)(2,1)} %bitcast.101, s32[]{:T(128)S(6)} %select_n.58, s32[]{:T(128)S(6)} %select_n.60, s32[]{:T(128)S(6)} %select_n.56, ...), kind=kLoop, calls=%fused_computation.78 | loop fusion | bytes 6291472 | tf_op jit(solution)/shard_map/jit(dynamic_index_in_dim)/dynamic_slice | solution.py:400
  68.2 1.3 collective-permute-start.11
  69.4 1.4 collective-permute-start.15
  70.9 1.6 collective-permute-start.13
  72.5 0.7 pad_select_fusion.late
  73.2 2.0 %copy.31 = bf16[512,384]{1,0:T(8,128)(2,1)} copy(bf16[512,384]{0,1:T(8,128)(2,1)} %bitcast.20) | data formatting | bytes 786432 | tf_op jit(solution)/shard_map/dot_general | solution.py:49
  75.2 2.1 %fusion.37 = (f32[256]{0:T(256)S(1)}, bf16[384,256]{1,0:T(8,128)(2,1)}) fusion(f32[384,256]{1,0:T(8,128)} %get-tuple-element.59, bf16[384,512]{1,0:T(8,128)(2,1)} %bitcast.14, bf16[256,512]{1,0:T(8,128)(2,1)S(1)} %copy-done.4), kind=kOutput, calls=%fused_computation.83 | convolution fusion | flops 101154560 | bytes 1246208 | tf_op jit(solution)/shard_map/dot_general | solution.py:59
  77.3 0.4 collective-permute-start.12
  77.7 2.3 %collective-permute-start.16 = (bf16[384,256]{1,0:T(8,128)(2,1)}, bf16[384,256]{1,0:T(8,128)(2,1)}, u32[]{:S(2)}, u32[]{:S(2)}) collective-permute-start(bf16[384,256]{1,0:T(8,128)(2,1)} %get-tuple-element.50), channel_id=1, source_target_pairs={{0,24},{8,0},{16,8},{24,16},{1,25},{9,1},{17,9},{25,17},{2,26},{10... | collective-permute-start | bytes 589832 | tf_op jit(solution)/shard_map/ppermute | solution.py:20
  79.9 1.6 plane_messages.1
  81.5 1.0 convert_element_type.90
  82.5 4.4 %all-to-all-start.1 = ((f16[16,40,512]{2,1,0:T(8,128)(2,1)}), f16[16,40,512]{2,1,0:T(8,128)(2,1)}, u32[]{:S(2)}, u32[]{:S(2)}) async-start(f16[16,40,512]{2,1,0:T(8,128)(2,1)} %convert_element_type.90), calls=%async_computation.1 | async-start | bytes 1310720 | tf_op jit(solution)/shard_map/all_to_all | solution.py:37
  86.9 0.3 convolution_bitcast_fusion
  87.3 1.8 fusion.43
  89.1 28.4 %all-to-all-done.1 = f16[16,40,512]{2,1,0:T(8,128)(2,1)} async-done(((f16[16,40,512]{2,1,0:T(8,128)(2,1)}), f16[16,40,512]{2,1,0:T(8,128)(2,1)}, u32[]{:S(2)}, u32[]{:S(2)}) %all-to-all-start.1) | async-done | bytes 655392 | tf_op jit(solution)/shard_map/all_to_all | solution.py:37
  117.6 1.0 fusion.33
  118.6 0.9 slice_convert_fusion
  119.5 1.2 multiply_reduce_fusion.1
  120.8 1.6 collective-permute-start.14
  122.4 1.6 collective-permute-start.7
  124.0 1.6 convolution_add_fusion.1
  125.8 2.7 %collective-permute-start.18 = (f32[264,256]{1,0:T(8,128)S(1)}, f32[264,256]{1,0:T(8,128)}, u32[]{:S(2)}, u32[]{:S(2)}) collective-permute-start(f32[264,256]{1,0:T(8,128)S(1)} %fusion.11), channel_id=1, source_target_pairs={{0,4},{4,0},{1,5},{5,1},{2,6},{6,2},{3,7},{7,3},{8,12},{12,8},{9,1... | collective-permute-start | bytes 811016 | tf_op jit(solution)/shard_map/ppermute | solution.py:20
  128.5 3.3 %collective-permute-start.8 = (f32[40,512]{1,0:T(8,128)S(1)}, f32[40,512]{1,0:T(8,128)S(1)}, u32[]{:S(2)}, u32[]{:S(2)}) collective-permute-start(f32[40,512]{1,0:T(8,128)S(1)} %fusion.35), channel_id=1, source_target_pairs={{0,64},{32,96},{64,0},{96,32},{128,192},{160,224},{192,128},{224,1... | collective-permute-start | bytes 245768 | tf_op jit(solution)/shard_map/ppermute | solution.py:176
  131.8 1.6 fusion.44
  133.4 3.0 %collective-permute-done.8 = f32[40,512]{1,0:T(8,128)S(1)} collective-permute-done((f32[40,512]{1,0:T(8,128)S(1)}, f32[40,512]{1,0:T(8,128)S(1)}, u32[]{:S(2)}, u32[]{:S(2)}) %collective-permute-start.8) | collective-permute-done | bytes 81952 | tf_op jit(solution)/shard_map/ppermute | solution.py:176
  136.4 6.1 %collective-permute-start.9 = (f32[40,512]{1,0:T(8,128)S(1)}, f32[40,512]{1,0:T(8,128)S(1)}, u32[]{:S(2)}, u32[]{:S(2)}) collective-permute-start(f32[40,512]{1,0:T(8,128)S(1)} %add.168), channel_id=1, source_target_pairs={{0,128},{32,160},{64,192},{96,224},{128,0},{160,32},{192,64},{224,... | collective-permute-start | bytes 245768 | tf_op jit(solution)/shard_map/ppermute | solution.py:176
  142.5 1.6 fusion.5
  144.5 0.9 broadcast_in_dim.45
  145.4 5.6 %all-to-all-start.2 = ((f16[16,40,512]{2,1,0:T(8,128)(2,1)}), f16[16,40,512]{2,1,0:T(8,128)(2,1)}, u32[]{:S(2)}, u32[]{:S(2)}) async-start(f16[16,40,512]{2,1,0:T(8,128)(2,1)} %broadcast_in_dim.45), calls=%async_computation.2 | async-start | bytes 1310720 | tf_op jit(solution)/shard_map/all_to_all | solution.py:37
  151.0 1.1 fusion.14
  152.2 1.4 collective-permute-start.19
  153.6 2.4 %collective-permute-start.20 = (f32[72,256]{1,0:T(8,128)S(1)}, f32[72,256]{1,0:T(8,128)S(1)}, u32[]{:S(2)}, u32[]{:S(2)}) collective-permute-start(f32[72,256]{1,0:T(8,128)S(1)} %get-tuple-element.52), channel_id=1, source_target_pairs={{0,16},{8,24},{16,0},{24,8},{1,17},{9,25},{17,1},{25,9},{2,18},{10... | collective-permute-start | bytes 221192 | tf_op jit(solution)/shard_map/ppermute | solution.py:20
  156.0 1.2 collective-permute-start.21
  157.1 0.8 dynamic-slice_bitcast_fusion
  158.0 3.1 %collective-permute-start.17 = (f32[8,64,256]{2,1,0:T(8,128)}, f32[8,64,256]{2,1,0:T(8,128)}, u32[]{:S(2)}, u32[]{:S(2)}) collective-permute-start(f32[8,64,256]{2,1,0:T(8,128)} %dynamic-slice_bitcast_fusion), channel_id=1, source_target_pairs={{0,4},{4,0},{1,5},{5,1},{2,6},{6,2},{3,7},{7,3},{8,12},{12,8},{9,1... | collective-permute-start | bytes 1572872 | tf_op jit(solution)/shard_map/ppermute | solution.py:45
  161.1 4.0 %collective-permute-done.20 = f32[72,256]{1,0:T(8,128)S(1)} collective-permute-done((f32[72,256]{1,0:T(8,128)S(1)}, f32[72,256]{1,0:T(8,128)S(1)}, u32[]{:S(2)}, u32[]{:S(2)}) %collective-permute-start.20) | collective-permute-done | bytes 73760 | tf_op jit(solution)/shard_map/ppermute | solution.py:20
  165.1 1.9 collective-permute-start.10
  167.0 1.3 z_messages.1
  168.4 20.2 %all_to_all.25 = f16[8,80,256]{2,1,0:T(8,128)(2,1)S(1)} all-to-all(f16[8,80,256]{2,1,0:T(8,128)(2,1)S(1)} %convert_element_type.101), channel_id=1, replica_groups=mesh['z'=8,'y'=4,'c'=2,'query'=4] {'z'}, dimensions={0} | all-to-all | bytes 655360 | tf_op jit(solution)/shard_map/all_to_all | solution.py:37
  188.7 0.7 z_finished.1
  189.4 1.2 convert_element_type.97.got
  190.8 1.5 finished.1
  192.3 0.5 slice.47
  (88 shorter events, 2.0 us)
Async XLA Ops:
  0.6 1.6 copy-start
  0.7 9.7 %copy-start.4 = (bf16[256,512]{1,0:T(8,128)(2,1)S(1)}, bf16[256,512]{1,0:T(8,128)(2,1)}, u32[]{:S(2)}) copy-start(bf16[256,512]{1,0:T(8,128)(2,1)} %param.18) | copy-start | bytes 786436
  0.7 12.7 %copy-start.9 = (s32[2,2048]{1,0:T(2,128)S(1)}, s32[2,2048]{1,0:T(2,128)}, u32[]{:S(2)}) copy-start(s32[2,2048]{1,0:T(2,128)} %param.14) | copy-start | bytes 49156
  0.7 12.7 %copy-start.8 = (f32[2,512]{1,0:T(2,128)S(1)}, f32[2,512]{1,0:T(2,128)}, u32[]{:S(2)}) copy-start(f32[2,512]{1,0:T(2,128)} %param.20) | copy-start | bytes 12292
  0.7 12.7 %copy-start.12 = (f32[512]{0:T(512)S(1)}, f32[512]{0:T(512)}, u32[]{:S(2)}) copy-start(f32[512]{0:T(512)} %param.21) | copy-start | bytes 6148
  0.7 12.7 %copy-start.11 = (f32[512]{0:T(512)S(1)}, f32[512]{0:T(512)}, u32[]{:S(2)}) copy-start(f32[512]{0:T(512)} %param.23) | copy-start | bytes 6148
  0.7 12.7 %copy-start.14 = (bf16[512,512]{1,0:T(8,128)(2,1)S(1)}, bf16[512,512]{1,0:T(8,128)(2,1)}, u32[]{:S(2)}) copy-start(bf16[512,512]{1,0:T(8,128)(2,1)} %v_three.1) | copy-start | bytes 1572868
  0.7 12.7 %copy-start.15 = (f32[512]{0:T(512)S(1)}, f32[512]{0:T(512)}, u32[]{:S(2)}) copy-start(f32[512]{0:T(512)} %param.25) | copy-start | bytes 6148
  5.9 12.6 %copy-start.5 = (bf16[384,256]{1,0:T(8,128)(2,1)}, bf16[384,256]{1,0:T(8,128)(2,1)S(1)}, u32[]{:S(2)}) copy-start(bf16[384,256]{1,0:T(8,128)(2,1)S(1)} %get-tuple-element.58) | copy-start | bytes 589828
  5.9 14.2 %collective-permute-start.2 = (bf16[384,256]{1,0:T(8,128)(2,1)S(1)}, bf16[384,256]{1,0:T(8,128)(2,1)}, u32[]{:S(2)}, u32[]{:S(2)}) collective-permute-start(bf16[384,256]{1,0:T(8,128)(2,1)S(1)} %get-tuple-element.58), channel_id=1, source_target_pairs={{0,2},{1,3},{2,0},{3,1},{4,6},{5,7},{6,4},{7,5},{8,10},{9,11},{10,... | collective-permute-start | bytes 589832 | tf_op jit(solution)/shard_map/ppermute | solution.py:20
  9.5 12.3 %collective-permute-start.4 = (bf16[384,256]{1,0:T(8,128)(2,1)S(1)}, bf16[384,256]{1,0:T(8,128)(2,1)}, u32[]{:S(2)}, u32[]{:S(2)}) collective-permute-start(bf16[384,256]{1,0:T(8,128)(2,1)S(1)} %get-tuple-element.58), channel_id=1, source_target_pairs={{0,3},{1,0},{2,1},{3,2},{4,7},{5,4},{6,5},{7,6},{8,11},{9,8},{10,9... | collective-permute-start | bytes 589832 | tf_op jit(solution)/shard_map/ppermute | solution.py:20
  10.3 10.0 %collective-permute-start.3 = (bf16[256,512]{1,0:T(8,128)(2,1)S(1)}, bf16[256,512]{1,0:T(8,128)(2,1)}, u32[]{:S(2)}, u32[]{:S(2)}) collective-permute-start(bf16[256,512]{1,0:T(8,128)(2,1)S(1)} %copy-done.4), channel_id=1, source_target_pairs={{0,2},{1,3},{2,0},{3,1},{4,6},{5,7},{6,4},{7,5},{8,10},{9,11},{10,... | collective-permute-start | bytes 786440 | tf_op jit(solution)/shard_map/ppermute | solution.py:20
  11.6 18.2 %collective-permute-start.5 = (bf16[256,512]{1,0:T(8,128)(2,1)S(1)}, bf16[256,512]{1,0:T(8,128)(2,1)}, u32[]{:S(2)}, u32[]{:S(2)}) collective-permute-start(bf16[256,512]{1,0:T(8,128)(2,1)S(1)} %copy-done.4), channel_id=1, source_target_pairs={{0,3},{1,0},{2,1},{3,2},{4,7},{5,4},{6,5},{7,6},{8,11},{9,8},{10,9... | collective-permute-start | bytes 786440 | tf_op jit(solution)/shard_map/ppermute | solution.py:20
  13.3 17.7 %collective-permute-start = (bf16[384,256]{1,0:T(8,128)(2,1)S(1)}, bf16[384,256]{1,0:T(8,128)(2,1)}, u32[]{:S(2)}, u32[]{:S(2)}) collective-permute-start(bf16[384,256]{1,0:T(8,128)(2,1)S(1)} %get-tuple-element.58), channel_id=1, source_target_pairs={{0,1},{1,2},{2,3},{3,0},{4,5},{5,6},{6,7},{7,4},{8,9},{9,10},{10,1... | collective-permute-start | bytes 589832 | tf_op jit(solution)/shard_map/ppermute | solution.py:20
  13.4 5.0 %copy-start.10 = (f32[512]{0:T(512)S(1)}, f32[512]{0:T(512)}, u32[]{:S(2)}) copy-start(f32[512]{0:T(512)} %param.19) | copy-start | bytes 6148
  20.1 12.2 %copy-start.13 = (bf16[384,2048]{1,0:T(8,128)(2,1)S(1)}, bf16[384,2048]{1,0:T(8,128)(2,1)}, u32[]{:S(2)}) copy-start(bf16[384,2048]{1,0:T(8,128)(2,1)} %param.15) | copy-start | bytes 4718596
  20.1 12.2 %copy-start.16 = (bf16[2048,512]{1,0:T(8,128)(2,1)S(1)}, bf16[2048,512]{1,0:T(8,128)(2,1)}, u32[]{:S(2)}) copy-start(bf16[2048,512]{1,0:T(8,128)(2,1)} %add_convert_fusion) | copy-start | bytes 6291460
  20.1 10.9 %collective-permute-start.1 = (bf16[256,512]{1,0:T(8,128)(2,1)S(1)}, bf16[256,512]{1,0:T(8,128)(2,1)S(1)}, u32[]{:S(2)}, u32[]{:S(2)}) collective-permute-start(bf16[256,512]{1,0:T(8,128)(2,1)S(1)} %copy-done.4), channel_id=1, source_target_pairs={{0,1},{1,2},{2,3},{3,0},{4,5},{5,6},{6,7},{7,4},{8,9},{9,10},{10,1... | collective-permute-start | bytes 786440 | tf_op jit(solution)/shard_map/ppermute | solution.py:20
  32.3 1.8 copy-start.7
  34.1 1.9 copy-start.17
  36.0 22.9 %all-to-all-start = ((f32[4,96,512]{2,1,0:T(8,128)}), f32[4,96,512]{2,1,0:T(8,128)S(1)}, u32[]{:S(2)}, u32[]{:S(2)}) async-start(f32[4,96,512]{2,1,0:T(8,128)} %bitcast.109), calls=%async_computation | async-start | bytes 1572864 | tf_op jit(solution)/shard_map/all_to_all | solution.py:37
  53.5 24.2 %collective-permute-start.6 = (f32[520,512]{1,0:T(8,128)}, f32[520,512]{1,0:T(8,128)}, u32[]{:S(2)}, u32[]{:S(2)}) collective-permute-start(f32[520,512]{1,0:T(8,128)} %get-tuple-element.26), channel_id=1, source_target_pairs={{0,4},{4,0},{1,5},{5,1},{2,6},{6,2},{3,7},{7,3},{8,12},{12,8},{9,1... | collective-permute-start | bytes 3194888 | tf_op jit(solution)/shard_map/ppermute | solution.py:45
  59.9 13.3 %all-to-all-start.3 = ((bf16[4,96,512]{2,1,0:T(8,128)(2,1)}), bf16[4,96,512]{2,1,0:T(8,128)(2,1)}, u32[]{:S(2)}, u32[]{:S(2)}) async-start(bf16[4,96,512]{2,1,0:T(8,128)(2,1)} %broadcast_in_dim.46), calls=%async_computation.3 | async-start | bytes 786432 | tf_op jit(solution)/shard_map/all_to_all | solution.py:37
  64.3 15.6 %copy-start.1 = (f32[520,512]{1,0:T(8,128)S(1)}, f32[520,512]{1,0:T(8,128)}, u32[]{:S(2)}) copy-start(f32[520,512]{1,0:T(8,128)} %get-tuple-element.25.mine) | copy-start | bytes 3194884
  68.2 52.6 %collective-permute-start.11 = (bf16[384,1024]{0,1:T(8,128)(2,1)}, bf16[384,1024]{0,1:T(8,128)(2,1)}, u32[]{:S(2)}, u32[]{:S(2)}) collective-permute-start(bf16[384,1024]{0,1:T(8,128)(2,1)} %bitcast.15), channel_id=1, source_target_pairs={{0,8},{8,16},{16,24},{24,0},{1,9},{9,17},{17,25},{25,1},{2,10},{10... | collective-permute-start | bytes 2359304 | tf_op jit(solution)/shard_map/ppermute | solution.py:20
  69.4 59.1 %collective-permute-start.15 = (bf16[384,1024]{0,1:T(8,128)(2,1)}, bf16[384,1024]{0,1:T(8,128)(2,1)}, u32[]{:S(2)}, u32[]{:S(2)}) collective-permute-start(bf16[384,1024]{0,1:T(8,128)(2,1)} %bitcast.17), channel_id=1, source_target_pairs={{0,24},{8,0},{16,8},{24,16},{1,25},{9,1},{17,9},{25,17},{2,26},{10... | collective-permute-start | bytes 2359304 | tf_op jit(solution)/shard_map/ppermute | solution.py:20
  70.9 71.6 %collective-permute-start.13 = (bf16[384,1024]{0,1:T(8,128)(2,1)}, bf16[384,1024]{0,1:T(8,128)(2,1)}, u32[]{:S(2)}, u32[]{:S(2)}) collective-permute-start(bf16[384,1024]{0,1:T(8,128)(2,1)} %bitcast.16), channel_id=1, source_target_pairs={{0,16},{8,24},{16,0},{24,8},{1,17},{9,25},{17,1},{25,9},{2,18},{10... | collective-permute-start | bytes 2359304 | tf_op jit(solution)/shard_map/ppermute | solution.py:20
  77.3 45.1 %collective-permute-start.12 = (bf16[384,256]{1,0:T(8,128)(2,1)}, bf16[384,256]{1,0:T(8,128)(2,1)}, u32[]{:S(2)}, u32[]{:S(2)}) collective-permute-start(bf16[384,256]{1,0:T(8,128)(2,1)} %get-tuple-element.50), channel_id=1, source_target_pairs={{0,8},{8,16},{16,24},{24,0},{1,9},{9,17},{17,25},{25,1},{2,10},{10... | collective-permute-start | bytes 589832 | tf_op jit(solution)/shard_map/ppermute | solution.py:20
  77.7 54.2 %collective-permute-start.16 = (bf16[384,256]{1,0:T(8,128)(2,1)}, bf16[384,256]{1,0:T(8,128)(2,1)}, u32[]{:S(2)}, u32[]{:S(2)}) collective-permute-start(bf16[384,256]{1,0:T(8,128)(2,1)} %get-tuple-element.50), channel_id=1, source_target_pairs={{0,24},{8,0},{16,8},{24,16},{1,25},{9,1},{17,9},{25,17},{2,26},{10... | collective-permute-start | bytes 589832 | tf_op jit(solution)/shard_map/ppermute | solution.py:20
  79.9 7.0 %copy-start.6 = (bf16[384,256]{1,0:T(8,128)(2,1)S(1)}, bf16[384,256]{1,0:T(8,128)(2,1)}, u32[]{:S(2)}) copy-start(bf16[384,256]{1,0:T(8,128)(2,1)} %copy-done.5) | copy-start | bytes 589828
  81.5 5.4 %copy-start.3 = (bf16[512,384]{1,0:T(8,128)(2,1)S(1)}, bf16[512,384]{1,0:T(8,128)(2,1)}, u32[]{:S(2)}) copy-start(bf16[512,384]{1,0:T(8,128)(2,1)} %copy.31) | copy-start | bytes 1179652
  82.5 35.1 %all-to-all-start.1 = ((f16[16,40,512]{2,1,0:T(8,128)(2,1)}), f16[16,40,512]{2,1,0:T(8,128)(2,1)}, u32[]{:S(2)}, u32[]{:S(2)}) async-start(f16[16,40,512]{2,1,0:T(8,128)(2,1)} %convert_element_type.90), calls=%async_computation.1 | async-start | bytes 1310720 | tf_op jit(solution)/shard_map/all_to_all | solution.py:37
  87.3 1.8 copy-start.2
  120.8 21.7 %collective-permute-start.14 = (bf16[384,256]{1,0:T(8,128)(2,1)}, bf16[384,256]{1,0:T(8,128)(2,1)S(1)}, u32[]{:S(2)}, u32[]{:S(2)}) collective-permute-start(bf16[384,256]{1,0:T(8,128)(2,1)} %get-tuple-element.50), channel_id=1, source_target_pairs={{0,16},{8,24},{16,0},{24,8},{1,17},{9,25},{17,1},{25,9},{2,18},{10... | collective-permute-start | bytes 589832 | tf_op jit(solution)/shard_map/ppermute | solution.py:20
  122.4 3.5 %collective-permute-start.7 = (f32[40,512]{1,0:T(8,128)S(1)}, f32[40,512]{1,0:T(8,128)S(1)}, u32[]{:S(2)}, u32[]{:S(2)}) collective-permute-start(f32[40,512]{1,0:T(8,128)S(1)} %select_maximum_fusion), channel_id=1, source_target_pairs={{0,32},{32,0},{64,96},{96,64},{128,160},{160,128},{192,224},{224,1... | collective-permute-start | bytes 245768 | tf_op jit(solution)/shard_map/ppermute | solution.py:176
  125.8 25.1 %collective-permute-start.18 = (f32[264,256]{1,0:T(8,128)S(1)}, f32[264,256]{1,0:T(8,128)}, u32[]{:S(2)}, u32[]{:S(2)}) collective-permute-start(f32[264,256]{1,0:T(8,128)S(1)} %fusion.11), channel_id=1, source_target_pairs={{0,4},{4,0},{1,5},{5,1},{2,6},{6,2},{3,7},{7,3},{8,12},{12,8},{9,1... | collective-permute-start | bytes 811016 | tf_op jit(solution)/shard_map/ppermute | solution.py:20
  128.5 7.9 %collective-permute-start.8 = (f32[40,512]{1,0:T(8,128)S(1)}, f32[40,512]{1,0:T(8,128)S(1)}, u32[]{:S(2)}, u32[]{:S(2)}) collective-permute-start(f32[40,512]{1,0:T(8,128)S(1)} %fusion.35), channel_id=1, source_target_pairs={{0,64},{32,96},{64,0},{96,32},{128,192},{160,224},{192,128},{224,1... | collective-permute-start | bytes 245768 | tf_op jit(solution)/shard_map/ppermute | solution.py:176
  136.4 7.9 %collective-permute-start.9 = (f32[40,512]{1,0:T(8,128)S(1)}, f32[40,512]{1,0:T(8,128)S(1)}, u32[]{:S(2)}, u32[]{:S(2)}) collective-permute-start(f32[40,512]{1,0:T(8,128)S(1)} %add.168), channel_id=1, source_target_pairs={{0,128},{32,160},{64,192},{96,224},{128,0},{160,32},{192,64},{224,... | collective-permute-start | bytes 245768 | tf_op jit(solution)/shard_map/ppermute | solution.py:176
  145.4 19.7 %all-to-all-start.2 = ((f16[16,40,512]{2,1,0:T(8,128)(2,1)}), f16[16,40,512]{2,1,0:T(8,128)(2,1)}, u32[]{:S(2)}, u32[]{:S(2)}) async-start(f16[16,40,512]{2,1,0:T(8,128)(2,1)} %broadcast_in_dim.45), calls=%async_computation.2 | async-start | bytes 1310720 | tf_op jit(solution)/shard_map/all_to_all | solution.py:37
  152.2 9.0 %collective-permute-start.19 = (f32[72,256]{1,0:T(8,128)S(1)}, f32[72,256]{1,0:T(8,128)S(1)}, u32[]{:S(2)}, u32[]{:S(2)}) collective-permute-start(f32[72,256]{1,0:T(8,128)S(1)} %get-tuple-element.51), channel_id=1, source_target_pairs={{0,8},{8,16},{16,24},{24,0},{1,9},{9,17},{17,25},{25,1},{2,10},{10... | collective-permute-start | bytes 221192 | tf_op jit(solution)/shard_map/ppermute | solution.py:20
  153.6 11.5 %collective-permute-start.20 = (f32[72,256]{1,0:T(8,128)S(1)}, f32[72,256]{1,0:T(8,128)S(1)}, u32[]{:S(2)}, u32[]{:S(2)}) collective-permute-start(f32[72,256]{1,0:T(8,128)S(1)} %get-tuple-element.52), channel_id=1, source_target_pairs={{0,16},{8,24},{16,0},{24,8},{1,17},{9,25},{17,1},{25,9},{2,18},{10... | collective-permute-start | bytes 221192 | tf_op jit(solution)/shard_map/ppermute | solution.py:20
  156.0 9.1 %collective-permute-start.21 = (f32[72,256]{1,0:T(8,128)S(1)}, f32[72,256]{1,0:T(8,128)S(1)}, u32[]{:S(2)}, u32[]{:S(2)}) collective-permute-start(f32[72,256]{1,0:T(8,128)S(1)} %get-tuple-element.53), channel_id=1, source_target_pairs={{0,24},{8,0},{16,8},{24,16},{1,25},{9,1},{17,9},{25,17},{2,26},{10... | collective-permute-start | bytes 221192 | tf_op jit(solution)/shard_map/ppermute | solution.py:20
  158.0 9.1 %collective-permute-start.17 = (f32[8,64,256]{2,1,0:T(8,128)}, f32[8,64,256]{2,1,0:T(8,128)}, u32[]{:S(2)}, u32[]{:S(2)}) collective-permute-start(f32[8,64,256]{2,1,0:T(8,128)} %dynamic-slice_bitcast_fusion), channel_id=1, source_target_pairs={{0,4},{4,0},{1,5},{5,1},{2,6},{6,2},{3,7},{7,3},{8,12},{12,8},{9,1... | collective-permute-start | bytes 1572872 | tf_op jit(solution)/shard_map/ppermute | solution.py:45
  165.1 25.5 %collective-permute-start.10 = (f16[16,40,512]{2,1,0:T(8,128)(2,1)}, f16[16,40,512]{2,1,0:T(8,128)(2,1)S(1)}, u32[]{:S(2)}, u32[]{:S(2)}) collective-permute-start(f16[16,40,512]{2,1,0:T(8,128)(2,1)} %all-to-all-done.2), channel_id=1, source_target_pairs={{0,4},{4,0},{1,5},{5,1},{2,6},{6,2},{3,7},{7,3},{8,12},{12,8},{9,1... | collective-permute-start | bytes 1966088 | tf_op jit(solution)/shard_map/ppermute | solution.py:45
where the time goes:
time: 196 us; the launch traced here: 195 us
  starting transfers between devices  59.6 us (30%)
  waiting for transfers between devices  44.1 us (22%)
  matrix products  25.4 us (13%)
  blocking collectives  20.2 us (10%)
  Pallas kernels  18.1 us (9%)
  local copies, waits for them, and re-layouts  15.9 us (8%)
  other arithmetic  8.33 us (4%)
  between operations  2.98 us (2%)
    all_to_all x4, waiting for transfers between devices, exchanged(): return lax.all_to_all(x, axis, 0, 0, tiled=True)  28.5 us
    ppermute x16, starting transfers between devices, shift(): return lax.ppermute(x, axis, [(i, (i + k) % n) for i in range(n)])  23.7 us
    all_to_all x1, blocking collectives, exchanged(): return lax.all_to_all(x, axis, 0, 0, tiled=True)  20.2 us
    all_to_all x4, starting transfers between devices, exchanged(): return lax.all_to_all(x, axis, 0, 0, tiled=True)  19 us
    pallas_call x1, Pallas kernels, trunk_backward(): pl.pallas_call(functools.partial(back_kernel, inv_scale=inv_scale), grid_...  12.9 us
    ppermute x16, waiting for transfers between devices, shift(): return lax.ppermute(x, axis, [(i, (i + k) % n) for i in range(n)])  12.1 us
    ppermute x3, starting transfers between devices, summed_in_pairs(): x = x + lax.ppermute(x, axis, [(i, i ^ k) for i in range(n)])  11 us
    dot_general x5, matrix products, contract_rows(): lax.dot_general(left, right, (((0,), (0,)), ((), ())), precision=precisio...  6.79 us
  transfers between devices with their start and end apart: 26, of which 7 were waited for; matrix products, arithmetic and copies ran while one was open for 20% of the time, Pallas kernels for 9%

commit v1 on v0

--- a/solution.py
+++ b/solution.py
@@ -37,10 +37,6 @@
     return lax.all_to_all(x, axis, 0, 0, tiled=True)
 
 
-def told_to_all(x, axis):
-    return exchanged(jnp.broadcast_to(x[None], (lax.axis_size(axis), *x.shape)), axis)
-
-
 def other_core(x):
     return lax.ppermute(x, "c", [(0, 1), (1, 0)])
 
@@ -65,18 +61,174 @@
     )
 
 
-def trunk_forward(coords, v_one, c_one, v_two, c_two, v_three, c_three):
-    first_act = jnp.tanh(
-        coords[0][:, None] * v_one[0][None, :] + coords[1][:, None] * v_one[1][None, :] + c_one
-    )
-    first_b = first_act.astype(jnp.bfloat16)
-    second_act = jnp.tanh(jnp.dot(first_b, v_two, preferred_element_type=jnp.float32) + c_two)
-    second_b = second_act.astype(jnp.bfloat16)
-    basis_full = jnp.dot(second_b, v_three, preferred_element_type=jnp.float32) + c_three
-    return basis_full.astype(jnp.bfloat16)
-
-
-def back_kernel(core, coords, misfit, coeffs, rows_in, v_two, v_three, mine, give, acc3, acc2, accs, *, inv_scale):
+def points_of(index):
+    coords = index.astype(jnp.float32) / (GRID - 1)
+    columns = jnp.concatenate([coords, jnp.zeros((6, coords.shape[1]), jnp.float32)]).T
+    return columns[:, 0:1], columns[:, 1:2]
+
+
+def whole(*shape):
+    return pl.BlockSpec(shape, lambda i, *_: (0,) * len(shape))
+
+
+def trunk_forward(query_index, v_one, c_one, v_two, c_two, v_three, c_three):
+    queries = query_index.shape[1]
+    trunk, basis = v_three.shape
+    block = 512
+
+    def body(index, v_one, c_one, v_two, c_two, v_three, c_three, out, first_out, second_out):
+        x, y = points_of(index[...])
+        first = jnp.tanh(x * v_one[0:1, :] + y * v_one[1:2, :] + c_one[...])
+        second = jnp.dot(first.astype(jnp.bfloat16), v_two[...], preferred_element_type=jnp.float32)
+        second = jnp.tanh(second + c_two[...])
+        first_out[...] = first
+        second_out[...] = second
+        full = jnp.dot(second.astype(jnp.bfloat16), v_three[...], preferred_element_type=jnp.float32) + c_three[...]
+        out[...] = full.astype(jnp.bfloat16)
+
+    return pl.pallas_call(
+        body,
+        grid=(queries // block,),
+        in_specs=[
+            pl.BlockSpec((2, block), lambda i: (0, i)),
+            whole(2, trunk),
+            whole(1, trunk),
+            whole(trunk, trunk),
+            whole(1, trunk),
+            whole(trunk, basis),
+            whole(1, basis),
+        ],
+        out_specs=[
+            pl.BlockSpec((block, basis), lambda i: (i, 0)),
+            pl.BlockSpec((block, trunk), lambda i: (i, 0)),
+            pl.BlockSpec((block, trunk), lambda i: (i, 0)),
+        ],
+        out_shape=[
+            jax.ShapeDtypeStruct((queries, basis), jnp.bfloat16),
+            jax.ShapeDtypeStruct((queries, trunk), jnp.float32),
+            jax.ShapeDtypeStruct((queries, trunk), jnp.float32),
+        ],
+        cost_estimate=pl.CostEstimate(flops=4 * queries * trunk * basis, bytes_accessed=4_000_000, transcendentals=2 * queries * trunk),
+        compiler_params=pltpu.CompilerParams(vmem_limit_bytes=60 * 2**20),
+        name="trunk_forward",
+    )(query_index, v_one, c_one[None], v_two, c_two[None], v_three, c_three[None])
+
+
+def misfit_of(hidden_all, w_two_all, b_two, basis, targets, inv_scale, grad_scale):
+    n = len(hidden_all)
+    funcs, queries = targets.shape
+    width = basis.shape[1]
+    block = 512
+
+    def body(*refs):
+        hidden, w_two = refs[:n], refs[n : 2 * n]
+        b_two, basis, targets, coeffs, misfit_b, squares, grad = refs[2 * n :]
+
+        @pl.when(pl.program_id(0) == 0)
+        def _():
+            total = b_two[...]
+            for h, w in zip(hidden, w_two):
+                total = total + jnp.dot(h[...], w[...], preferred_element_type=jnp.float32)
+            coeffs[...] = total.astype(jnp.bfloat16)
+            squares[...] = jnp.zeros_like(squares)
+            grad[...] = jnp.zeros_like(grad)
+
+        misfit = contract_cols(coeffs[...], basis[...]) * inv_scale - targets[...].astype(jnp.float32)
+        squares[...] += jnp.sum(misfit * misfit, axis=0, keepdims=True)
+        scaled_b = (misfit * grad_scale).astype(jnp.bfloat16)
+        misfit_b[...] = scaled_b
+        grad[...] += jnp.dot(scaled_b, basis[...], preferred_element_type=jnp.float32) * inv_scale
+
+    return pl.pallas_call(
+        body,
+        grid=(queries // block,),
+        in_specs=[whole(*h.shape) for h in hidden_all]
+        + [whole(*w.shape) for w in w_two_all]
+        + [
+            whole(1, width),
+            pl.BlockSpec((block, width), lambda i: (i, 0)),
+            pl.BlockSpec((funcs, block), lambda i: (0, i)),
+        ],
+        out_specs=[
+            whole(funcs, width),
+            pl.BlockSpec((funcs, block), lambda i: (0, i)),
+            whole(1, block),
+            whole(funcs, width),
+        ],
+        out_shape=[
+            jax.ShapeDtypeStruct((funcs, width), jnp.bfloat16),
+            jax.ShapeDtypeStruct((funcs, queries), jnp.bfloat16),
+            jax.ShapeDtypeStruct((1, block), jnp.float32),
+            jax.ShapeDtypeStruct((funcs, width), jnp.float32),
+        ],
+        cost_estimate=pl.CostEstimate(flops=5 * funcs * queries * width, bytes_accessed=8_000_000, transcendentals=0),
+        compiler_params=pltpu.CompilerParams(vmem_limit_bytes=60 * 2**20),
+        name="misfit_of",
+    )(*hidden_all, *w_two_all, b_two[None], basis, targets)
+
+
+def pre_of(ix, pieces, hidden, w_two):
+    n = len(pieces)
+    rows, basis = pieces[0].shape
+    funcs, width = hidden.shape
+
+    def body(ix, *refs):
+        hidden, w_two, pre_b, bias, product, grad = refs[n:]
+        for k in range(n):
+            at = lax.rem(ix[0] + n - k, n) * rows
+            grad[pl.ds(pl.multiple_of(at, rows), rows), :] = refs[k][...]
+        act = hidden[...]
+        pre = contract_cols(grad[...], w_two[...]) * (1.0 - act * act)
+        pre_b[...] = pre.astype(jnp.bfloat16)
+        bias[...] = jnp.sum(pre, axis=0, keepdims=True)
+        product[...] = contract_rows(grad[...], act.astype(jnp.bfloat16))
+
+    return pl.pallas_call(
+        body,
+        grid_spec=pltpu.PrefetchScalarGridSpec(
+            num_scalar_prefetch=1,
+            grid=(1,),
+            in_specs=[whole(rows, basis)] * n + [whole(funcs, width), whole(width, basis)],
+            out_specs=[whole(funcs, width), whole(1, width), whole(basis, width)],
+            scratch_shapes=[pltpu.VMEM((funcs, basis), jnp.bfloat16)],
+        ),
+        out_shape=[
+            jax.ShapeDtypeStruct((funcs, width), jnp.bfloat16),
+            jax.ShapeDtypeStruct((1, width), jnp.float32),
+            jax.ShapeDtypeStruct((basis, width), jnp.float32),
+        ],
+        cost_estimate=pl.CostEstimate(flops=4 * funcs * basis * width, bytes_accessed=2_000_000, transcendentals=0),
+        compiler_params=pltpu.CompilerParams(vmem_limit_bytes=12 * 2**20),
+        name="pre_of",
+    )(ix.reshape(1), *pieces, hidden, w_two)
+
+
+def columns_by_y(sensors, iy, nz, ny, width):
+    funcs = sensors.shape[0]
+
+    def body(y, *refs):
+        for src, dst in zip(refs[:ny], refs[ny:]):
+            dst[...] = src[...].T
+
+    def source(k):
+        return pl.BlockSpec((funcs, width), lambda z, y: (0, z * ny + lax.rem(y[0] + k, ny)))
+
+    return pl.pallas_call(
+        body,
+        grid_spec=pltpu.PrefetchScalarGridSpec(
+            num_scalar_prefetch=1,
+            grid=(nz,),
+            in_specs=[source(k) for k in range(ny)],
+            out_specs=[pl.BlockSpec((width, funcs), lambda z, y: (z, 0))] * ny,
+        ),
+        out_shape=[jax.ShapeDtypeStruct((nz * width, funcs), sensors.dtype)] * ny,
+        cost_estimate=pl.CostEstimate(flops=8_000_000, bytes_accessed=4 * sensors.size, transcendentals=0),
+        compiler_params=pltpu.CompilerParams(vmem_limit_bytes=60 * 2**20),
+        name="columns_by_y",
+    )(iy.reshape(1), *[sensors] * ny)
+
+
+def back_kernel(core, index, misfit, coeffs, first_act, second_act, v_two, v_three, mine, give, acc3, acc2, accs, *, inv_scale):
     step = pl.program_id(0)
 
     @pl.when(step == 0)
@@ -85,12 +237,9 @@
         acc2[...] = jnp.zeros_like(acc2)
         accs[...] = jnp.zeros_like(accs)
 
-    points = coords[...].T
-    x, y = points[:, 0:1], points[:, 1:2]
-    first = jnp.tanh(x * rows_in[0:1, :] + y * rows_in[1:2, :] + rows_in[2:3, :])
-    first_b = first.astype(jnp.bfloat16)
-    second = jnp.tanh(jnp.dot(first_b, v_two[...], preferred_element_type=jnp.float32) + rows_in[3:4, :])
-    second_b = second.astype(jnp.bfloat16)
+    x, y = points_of(index[...])
+    first, second = first_act[...], second_act[...]
+    first_b, second_b = first.astype(jnp.bfloat16), second.astype(jnp.bfloat16)
     grad = contract_rows(misfit[...], coeffs[...]) * inv_scale
     grad_b = grad.astype(jnp.bfloat16)
     acc3[...] += contract_rows(second_b, grad_b)
@@ -122,16 +271,12 @@
             give[:rows, :] = acc3[...]
 
 
-def trunk_backward(core, coords, misfit_b, coeffs_b, v_one, c_one, v_two, c_two, v_three, inv_scale):
+def trunk_backward(core, query_index, misfit_b, coeffs_b, first_act, second_act, v_two, v_three, inv_scale):
     queries = misfit_b.shape[1]
     funcs, basis = coeffs_b.shape
     trunk = v_two.shape[0]
     block = 512
 
-    def whole(*shape):
-        return pl.BlockSpec(shape, lambda i, core: (0,) * len(shape))
-
-    rows_in = jnp.concatenate([v_one, c_one[None], c_two[None], jnp.zeros((4, trunk), jnp.float32)])
     out = jax.ShapeDtypeStruct((trunk + 8, basis), jnp.float32)
     return pl.pallas_call(
         functools.partial(back_kernel, inv_scale=inv_scale),
@@ -139,10 +284,11 @@
             num_scalar_prefetch=1,
             grid=(queries // block,),
             in_specs=[
-                pl.BlockSpec((8, block), lambda i, core: (0, i)),
+                pl.BlockSpec((2, block), lambda i, core: (0, i)),
                 pl.BlockSpec((funcs, block), lambda i, core: (0, i)),
                 whole(funcs, basis),
-                whole(8, trunk),
+                pl.BlockSpec((block, trunk), lambda i, core: (i, 0)),
+                pl.BlockSpec((block, trunk), lambda i, core: (i, 0)),
                 whole(trunk, trunk),
                 whole(trunk, basis),
             ],
@@ -157,17 +303,13 @@
         cost_estimate=pl.CostEstimate(flops=12 * queries * trunk * basis, bytes_accessed=8_000_000, transcendentals=2 * queries * trunk),
         compiler_params=pltpu.CompilerParams(vmem_limit_bytes=60 * 2**20),
         name="trunk_backward",
-    )(core.reshape(1), coords, misfit_b, coeffs_b, rows_in, v_two, v_three)
+    )(core.reshape(1), query_index, misfit_b, coeffs_b, first_act, second_act, v_two, v_three)
 
 
 def scaled(x, axes=None):
     top = jnp.max(jnp.abs(x), axis=axes, keepdims=True)
     e = jnp.clip(jnp.floor(jnp.log2(jnp.maximum(top, 1e-30))), -100.0, 127.0) - 14.0
     return x * jnp.exp2(-e), e
-
-
-def power(e):
-    return jnp.exp2(e.astype(jnp.float32))
 
 
 def summed_in_pairs(x, axis):
@@ -186,15 +328,18 @@
     out[j, rows + 2 : rows + 3, :] = jnp.broadcast_to(piece_e, (1, w))
 
 
-def plane_messages(mine, got, late, n):
+def plane_messages(mine, got, b_two, squares, n):
     w = mine.shape[1]
     rows = mine.shape[0] - 8
     per = n // 8
     k = w // per
 
-    def body(mine, got, late, out):
+    def body(mine, got, b_two, squares, out):
         big, big_e = scaled(mine[:rows, :] + got[:rows, :])
-        small, small_e = scaled(mine[rows:, :] + got[rows:, :] + late[...], 1)
+        row = lax.broadcasted_iota(jnp.int32, (8, w), 0)
+        small = mine[rows:, :] + got[rows:, :]
+        small = jnp.where(row == 5, b_two[...], jnp.where(row == 6, squares[...], small))
+        small, small_e = scaled(small, 1)
         out[:, : rows // n, :] = big.reshape(n, rows // n, w)
         for j in range(n):
             i, at = j // per, j % per * k
@@ -205,8 +350,30 @@
         out_shape=jax.ShapeDtypeStruct((n, rows // n + 8, w), jnp.float32),
         compiler_params=pltpu.CompilerParams(vmem_limit_bytes=12 * 2**20),
         name="plane_messages",
-    )(mine, got, late)
+    )(mine, got, b_two, squares)
     return out.astype(jnp.float16)
+
+
+def plane_total(got):
+    n, rows, w = got.shape[0], got.shape[1] - 8, got.shape[2]
+
+    def body(got, out):
+        def total(lo, hi, e):
+            x = got[0, lo:hi, :] * jnp.exp2(got[0, e : e + 1, :])
+            for j in range(1, n):
+                x = x + got[j, lo:hi, :] * jnp.exp2(got[j, e : e + 1, :])
+            return x
+
+        out[:rows, :] = total(0, rows, rows + 1)
+        out[rows:, :] = jnp.zeros((8, w), jnp.float32)
+        out[rows : rows + 1, :] = total(rows, rows + 1, rows + 2)
+
+    return pl.pallas_call(
+        body,
+        out_shape=jax.ShapeDtypeStruct((rows + 8, w), jnp.float32),
+        compiler_params=pltpu.CompilerParams(vmem_limit_bytes=12 * 2**20),
+        name="plane_total",
+    )(got)
 
 
 def total_message(both, side):
@@ -262,45 +429,41 @@
     return out.astype(jnp.float16)
 
 
-def read(got, rows, side):
-    big = got[:, :rows].astype(jnp.float32) * power(got[:, rows + 1 : rows + 2, :1])
-    small = got[:, rows, :side].astype(jnp.float32) * power(got[:, rows + 2, :1])
-    return big, small
-
-
-def finished(core, got, other, side):
+def finished(place, got, other, side, ny, nx):
     n, rows, w = got.shape[0], got.shape[1] - 8, got.shape[2]
     per = n // 8
 
-    def body(core, got, other, one, two, v_one, c_one, c_two, c_three, b_two, loss):
+    def body(place, got, other, one, two, v_one, c_one, c_two, c_three, b_two, loss, small, more):
         def put(zero, last):
-            for x, out in ((zero, one), (last, two)):
-                out[...] = (x[:, :rows, :] * jnp.exp2(x[:, rows + 1 : rows + 2, :])).reshape(n * rows, w)
-            small = zero[:, rows : rows + 1, :side] * jnp.exp2(zero[:, rows + 2 : rows + 3, :side])
-            more = last[:, rows : rows + 1, :side] * jnp.exp2(last[:, rows + 2 : rows + 3, :side])
-            both = small + more
-            for p in range(per):
-                at = slice(p * side, (p + 1) * side)
-                v_one[0:1, at] = small[p]
-                v_one[1:2, at] = small[per + p]
-                c_one[:, at] = small[2 * per + p]
-                c_two[:, at] = small[3 * per + p]
-                c_three[:, at] = small[4 * per + p]
-                b_two[:, at] = both[5 * per + p]
-                loss[:, at] = both[6 * per + p]
-
-        @pl.when(core[0] == 0)
+            for q in range(n):
+                at = lax.rem(place[1] + ny - q // nx, ny) * nx + lax.rem(place[2] + nx - q % nx, nx)
+                into = pl.ds(pl.multiple_of(at * rows, rows), rows)
+                for x, out, part in ((zero, one, small), (last, two, more)):
+                    out[into, :] = x[q, :rows, :] * jnp.exp2(x[q, rows + 1 : rows + 2, :])
+                    part[pl.ds(at, 1), :] = x[q, rows : rows + 1, :side] * jnp.exp2(
+                        x[q, rows + 2 : rows + 3, :side]
+                    )
+
+        @pl.when(place[0] == 0)
         def _():
             put(got, other)
 
-        @pl.when(core[0] != 0)
+        @pl.when(place[0] != 0)
         def _():
             put(other, got)
 
-    def whole(*shape):
-        return pl.BlockSpec(shape, lambda i, core: (0,) * len(shape))
-
-    shapes = [(n * rows, w), (n * rows, w), (2, w)] + [(1, w)] * 5
+        total = jnp.zeros((1, 1), jnp.float32)
+        for p in range(per):
+            at = slice(p * side, (p + 1) * side)
+            for i, (out, j) in enumerate(((v_one, 0), (v_one, 1), (c_one, 0), (c_two, 0), (c_three, 0))):
+                out[j : j + 1, at] = small[i * per + p : i * per + p + 1, :]
+            k = 5 * per + p
+            b_two[:, at] = small[k : k + 1, :] + more[k : k + 1, :]
+            k = 6 * per + p
+            total = total + jnp.sum(small[k : k + 1, :] + more[k : k + 1, :], axis=1, keepdims=True)
+        loss[...] = total
+
+    shapes = [(n * rows, w), (n * rows, w), (2, w)] + [(1, w)] * 4 + [(1, 1)]
     return pl.pallas_call(
         body,
         grid_spec=pltpu.PrefetchScalarGridSpec(
@@ -308,11 +471,12 @@
             grid=(1,),
             in_specs=[whole(*got.shape), whole(*got.shape)],
             out_specs=[whole(*shape) for shape in shapes],
+            scratch_shapes=[pltpu.VMEM((n, side), jnp.float32)] * 2,
         ),
         out_shape=[jax.ShapeDtypeStruct(shape, jnp.float32) for shape in shapes],
         compiler_params=pltpu.CompilerParams(vmem_limit_bytes=24 * 2**20),
         name="finished",
-    )(core.reshape(1), got, other)
+    )(place, got, other)
 
 
 def z_finished(got, rows):
@@ -339,23 +503,23 @@
     )(got)
 
 
-def sum_of_all(mine, give, late):
+def sum_of_all(mine, give, b_two, squares):
     w = mine.shape[1]
-    rows = mine.shape[0] - 8
-    n = lax.axis_size("y") * lax.axis_size("query")
-    per, side = rows // n, 8 * w // n
-    plane = ("y", "query")
+    ny, nx = lax.axis_size("y"), lax.axis_size("query")
+    n = ny * nx
+    side = 8 * w // n
     got = other_core(give)
 
-    got = exchanged(plane_messages(mine, got, late, n), plane)
-    big, small = read(got, per, side)
-    big, small = jnp.sum(big, axis=0), jnp.sum(small, axis=0)
-    both = jnp.concatenate([big, jnp.pad(small[None], ((0, 7), (0, w - side)))])
+    got = exchanged(plane_messages(mine, got, b_two, squares, n), ("y", "query"))
+    both = plane_total(got.astype(jnp.float32))
     both = summed_in_pairs(both, "z")
-    got = told_to_all(total_message(both, side), plane)
+    got = total_message(both, side)
+    got = jnp.stack([got] + [shift(got, "query", k) for k in range(1, nx)])
+    got = jnp.concatenate([got] + [shift(got, "y", k) for k in range(1, ny)])
     other = other_core(got)
+    place = jnp.stack([lax.axis_index(a) for a in ("c", "y", "query")])
     return finished(
-        lax.axis_index("c"), got.astype(jnp.float32), other.astype(jnp.float32), side
+        place, got.astype(jnp.float32), other.astype(jnp.float32), side, ny, nx
     )
 
 
@@ -381,59 +545,42 @@
     count_all = funcs * nz * ny * nc * query_rows * nx
     grad_scale = 64.0 / math.sqrt(count_all)
     inv_scale = 1.0 / math.sqrt(basis_count)
-    coords = query_index.astype(jnp.float32) / (GRID - 1)
 
     w_two_all = [w_two] + [shift(w_two, "query", k) for k in range(1, nx)]
     hidden = jnp.tanh(jnp.dot(sensors, w_one, preferred_element_type=jnp.float32) + b_one)
     hidden_b = hidden.astype(jnp.bfloat16)
     hidden_all = [hidden_b] + [shift(hidden_b, "query", k) for k in range(1, nx)]
-    basis = trunk_forward(
-        coords, v_one, c_one, v_two, c_two, v_three, c_three
+    basis, first_act, second_act = trunk_forward(
+        query_index, v_one, c_one, v_two, c_two, v_three, c_three
     )
 
     rows_own = sensor_count // (nz * ny * nc)
-    iy = lax.axis_index("y")
+    iy, ic = lax.axis_index("y"), lax.axis_index("c")
     sensors_late, _ = lax.optimization_barrier((sensors, hidden_b))
-    columns = sensors_late.reshape(funcs, nz, ny, nc * rows_own)
-
-    def columns_of(y):
-        return lax.dynamic_index_in_dim(columns, y, 2, False).reshape(funcs, -1)
-
-    sens_y = [columns_of(iy)] + [
-        shift(columns_of((iy + k) % ny), "y", k) for k in range(1, ny)
-    ]
-
-    coeffs = b_two
-    for h, w in zip(hidden_all, w_two_all):
-        coeffs = coeffs + jnp.dot(h, w, preferred_element_type=jnp.float32)
-    coeffs_b = coeffs.astype(jnp.bfloat16)
-    prediction = contract_cols(coeffs_b, basis) * inv_scale
-    misfit = prediction - targets.astype(jnp.float32)
-    loss_part = jnp.sum(misfit * misfit)
-    misfit_b = (misfit * grad_scale).astype(jnp.bfloat16)
-    grad_part = jnp.dot(misfit_b, basis, preferred_element_type=jnp.float32) * inv_scale
+    sens_y = columns_by_y(sensors_late, iy, nz, ny, nc * rows_own)
+    sens_y = [sens_y[0]] + [shift(sens_y[k], "y", k) for k in range(1, ny)]
+
+    coeffs_b, misfit_b, squares, grad_part = misfit_of(
+        hidden_all, w_two_all, b_two, basis, targets, inv_scale, grad_scale
+    )
     grad_own = exchanged(grad_part.reshape(nx, -1, basis_count), "query")
     grad_own = jnp.sum(grad_own, axis=0)
-    b_two_part = jnp.sum(grad_own, axis=0)
-    grad_coeffs_b = told_to_all(grad_own.astype(jnp.bfloat16), "query").reshape(funcs, basis_count)
-
-    ic = lax.axis_index("c")
-    mine, give = trunk_backward(
-        ic, jnp.pad(coords, ((0, 6), (0, 0))), misfit_b, coeffs_b, v_one, c_one, v_two, c_two, v_three, inv_scale
-    )
-    late = jnp.stack([b_two_part, jnp.broadcast_to(loss_part, (basis_count,))])
-    totals = sum_of_all(mine, give, jnp.pad(late, ((5, 1), (0, 0))))
+    b_two_part = jnp.sum(grad_own, axis=0, keepdims=True)
+    grad_own_b = grad_own.astype(jnp.bfloat16)
+    grad_pieces = [grad_own_b] + [shift(grad_own_b, "query", k) for k in range(1, nx)]
+
+    mine, give = trunk_backward(ic, query_index, misfit_b, coeffs_b, first_act, second_act, v_two, v_three, inv_scale)
+    totals = sum_of_all(mine, give, b_two_part, squares)
     g_v_three, g_v_two, g_v_one, g_c_one, g_c_two, g_c_three, g_b_two, loss = totals
 
-    grad_pre = contract_cols(grad_coeffs_b, w_two) * (1.0 - hidden * hidden)
-    b_one_part = jnp.sum(grad_pre, axis=0)
-    grad_pre_b = grad_pre.astype(jnp.bfloat16)
+    grad_pre_b, b_one_part, w_two_part = pre_of(
+        lax.axis_index("query"), grad_pieces, hidden, w_two
+    )
 
     pre_y = [grad_pre_b] + [shift(grad_pre_b, "y", k) for k in range(1, ny)]
 
-    w_two_part = contract_rows(grad_coeffs_b, hidden_b)
     w_two_part = w_two_part.reshape(nz, ny, nc, -1, hidden_count)
-    b_one_rows = jnp.pad(b_one_part[None], ((0, 7), (0, 0)))
+    b_one_rows = jnp.pad(b_one_part, ((0, 7), (0, 0)))
 
     def with_bias(rows, n):
         rows = rows.reshape(n, -1, hidden_count)
@@ -445,9 +592,11 @@
     both = scattered_sum(with_bias(w_two_part.transpose(1, 0, 2, 3), ny), "y")
     w_two_part, b_one_row = both[:-8].reshape(nz, -1, hidden_count), both[-8:-7]
 
-    w_one_part = contract_rows(sens_y[0], pre_y[0])
+    w_one_part = jnp.dot(sens_y[0], pre_y[0], preferred_element_type=jnp.float32)
     for k in range(1, ny):
-        w_one_part = w_one_part + contract_rows(sens_y[k], pre_y[k])
+        w_one_part = w_one_part + jnp.dot(
+            sens_y[k], pre_y[k], preferred_element_type=jnp.float32
+        )
     w_one_part = w_one_part.reshape(nz, nc, rows_own, hidden_count)
     got = other_core(lax.dynamic_index_in_dim(w_one_part, 1 - ic, 1, False))
     sent = z_messages(ic, w_one_part, got, w_two_part, b_one_row)

time: 196 us -> 188 us (0.959)
  blocking collectives: 20.2 us -> 0 us
  Pallas kernels: 18.1 us -> 36.9 us
  starting transfers between devices: 59.6 us -> 75.1 us
  matrix products: 25.4 us -> 12.1 us
  waiting for transfers between devices: 44.1 us -> 36.5 us
  local copies, waits for them, and re-layouts: 15.9 us -> 13.8 us
    pallas_call x0 -> x5, Pallas kernels: none -> 21.8 us  [the longest x1 6.65 us: misfit_of(): pl.pallas_call(body, grid=(queries // block,), in_specs=[whole(*h.shape)...]
    all_to_all x1 -> x0, blocking collectives: 20.2 us -> none  [exchanged(): return lax.all_to_all(x, axis, 0, 0, tiled=True)]
    dot_general x13 -> x4, matrix products: 21.7 us -> 8.57 us  [the longest x3 6.8 us: local(): jnp.dot(sens_y[k], pre_y[k], preferred_element_type=jnp.float32)]
    ppermute x16 -> x25, starting transfers between devices: 23.7 us -> 36.3 us  [shift(): return lax.ppermute(x, axis, [(i, (i + k) % n) for i in range(n)])]
    unnamed x36 -> x45, local copies, waits for them, and re-layouts: 1.59 us -> 11.2 us
    ppermute x3, starting transfers between devices: 5.84 us -> 13.3 us  [other_core(): return lax.ppermute(x, 'c', [(0, 1), (1, 0)])]
    all_to_all x4 -> x3, waiting for transfers between devices: 28.5 us -> 21 us  [exchanged(): return lax.all_to_all(x, axis, 0, 0, tiled=True)]
    optimization_barrier x1 -> x0, local copies, waits for them, and re-layouts: 4.64 us -> none  [local(): sensors_late, _ = lax.optimization_barrier((sensors, hidden_b))]
  transfers between devices with their start and end apart: 26 -> 34, of which waited for: 7 -> 15; matrix products, arithmetic and copies ran while one was open for 20% -> 12% of each run, Pallas kernels for 9% -> 19%
where the time goes in v1:
time: 188 us; the launch traced here: 187 us
  starting transfers between devices  75.1 us (40%)
  Pallas kernels  36.9 us (20%)
  waiting for transfers between devices  36.5 us (19%)
  local copies, waits for them, and re-layouts  13.8 us (7%)
  matrix products  12.1 us (6%)
  other arithmetic  9.36 us (5%)
  between operations  2.78 us (1%)
    ppermute x25, starting transfers between devices, shift(): return lax.ppermute(x, axis, [(i, (i + k) % n) for i in range(n)])  36.3 us
    all_to_all x3, waiting for transfers between devices, exchanged(): return lax.all_to_all(x, axis, 0, 0, tiled=True)  21 us
    all_to_all x3, starting transfers between devices, exchanged(): return lax.all_to_all(x, axis, 0, 0, tiled=True)  15 us
    ppermute x3, starting transfers between devices, other_core(): return lax.ppermute(x, 'c', [(0, 1), (1, 0)])  13.3 us
    ppermute x25, waiting for transfers between devices, shift(): return lax.ppermute(x, axis, [(i, (i + k) % n) for i in range(n)])  13 us
    pallas_call x1, Pallas kernels, trunk_backward(): pl.pallas_call(functools.partial(back_kernel, inv_scale=inv_scale), grid_...  11.6 us
    unnamed x45, local copies, waits for them, and re-layouts  11.2 us
    ppermute x3, starting transfers between devices, summed_in_pairs(): x = x + lax.ppermute(x, axis, [(i, i ^ k) for i in range(n)])  10.5 us
  transfers between devices with their start and end apart: 34, of which 15 were waited for; matrix products, arithmetic and copies ran while one was open for 12% of the time, Pallas kernels for 19%

profile of v1, /device:TPU:1, one launch (start us, length us, event | category | flops | bytes accessed | tf_op | source)
XLA Modules:
  0.0 186.6 jit_solution(16044702247410436581)
XLA Ops:
  0.7 1.6 copy-done
  2.2 3.6 %fusion.20 = (bf16[384,256]{1,0:T(8,128)(2,1)}, f32[384,256]{1,0:T(8,128)S(1)}) fusion(f32[256]{0:T(256)} %param.17, bf16[384,4096]{1,0:T(8,128)(2,1)} %refs_3_, bf16[4096,256]{1,0:T(8,128)(2,1)S(1)} %copy-done), kind=kOutput, calls=%fused_computation.46 | convolution fusion | flops 805502976 | bytes 5833728 | tf_op jit(solution)/shard_map/dot_general | solution.py:550
  5.8 2.0 %collective-permute-start = (bf16[384,256]{1,0:T(8,128)(2,1)}, bf16[384,256]{1,0:T(8,128)(2,1)}, u32[]{:S(2)}, u32[]{:S(2)}) collective-permute-start(bf16[384,256]{1,0:T(8,128)(2,1)} %get-tuple-element.74.refs_0_), channel_id=1, source_target_pairs={{0,1},{1,2},{2,3},{3,0},{4,5},{5,6},{6,7},{7,4},{8,9},{9,10},{10,1... | collective-permute-start | bytes 589832 | tf_op jit(solution)/shard_map/ppermute | solution.py:20
  7.8 1.2 collective-permute-start.3
  9.0 1.3 collective-permute-start.4
  10.3 2.1 %collective-permute-start.5 = (bf16[256,512]{1,0:T(8,128)(2,1)S(1)}, bf16[256,512]{1,0:T(8,128)(2,1)S(1)}, u32[]{:S(2)}, u32[]{:S(2)}) collective-permute-start(bf16[256,512]{1,0:T(8,128)(2,1)S(1)} %copy-done.3), channel_id=1, source_target_pairs={{0,3},{1,0},{2,1},{3,2},{4,7},{5,4},{6,5},{7,6},{8,11},{9,8},{10,9... | collective-permute-start | bytes 786440 | tf_op jit(solution)/shard_map/ppermute | solution.py:20
  12.9 6.5 %columns_by_y.1 = (bf16[1024,384]{1,0:T(8,128)(2,1)}, bf16[1024,384]{1,0:T(8,128)(2,1)}, bf16[1024,384]{1,0:T(8,128)(2,1)}, bf16[1024,384]{1,0:T(8,128)(2,1)}) custom-call(s32[1]{0:T(128)} %bitcast.1.y, bf16[384,4096]{1,0:T(8,128)(2,1)} %refs_3_, bf16[384,4096]{1,0:T(8,128)(2,1)} %refs_3_, bf16[384,4096]{1,0:T(8,128)(2,1)} %refs_3_, bf16[384,4096]{1,0:T(8,128)(2,1)} %refs_3_), custom_call_target="tpu_custom_call" | custom-call | flops 8000000 | bytes 6291456 | tf_op jit(solution)/shard_map/columns_by_y/pallas_call | solution.py:216
  19.3 1.4 collective-permute-start.2
  20.7 6.5 %trunk_forward.1 = (bf16[2048,512]{1,0:T(8,128)(2,1)}, f32[2048,512]{1,0:T(8,128)}, f32[2048,512]{1,0:T(8,128)}) custom-call(s32[2,2048]{1,0:T(2,128)} %index.3, f32[2,512]{1,0:T(2,128)} %v_one.1, f32[1,512]{1,0:T(1,128)} %bitcast.85, bf16[512,512]{1,0:T(8,128)(2,1)} %v_two.3, f32[1,512]{1,0:T(1,128)} %bitcast.86, bf16[512,512]{1,0:T(8,128)(2,1)} %v_three.3, ...), custom_call_target="tpu_custom_call" | custom-call | flops 2147483648 | bytes 4000000 | tf_op jit(solution)/shard_map/trunk_forward/pallas_call | solution.py:89
  27.2 3.2 %collective-permute-done.1.refs_2_ = bf16[384,256]{1,0:T(8,128)(2,1)} collective-permute-done((bf16[384,256]{1,0:T(8,128)(2,1)}, bf16[384,256]{1,0:T(8,128)(2,1)}, u32[]{:S(2)}, u32[]{:S(2)}) %collective-permute-start.1) | collective-permute-done | bytes 196640 | tf_op jit(solution)/shard_map/ppermute | solution.py:20
  30.4 2.7 %collective-permute-start.24 = (bf16[1024,384]{1,0:T(8,128)(2,1)}, bf16[1024,384]{1,0:T(8,128)(2,1)}, u32[]{:S(2)}, u32[]{:S(2)}) collective-permute-start(bf16[1024,384]{1,0:T(8,128)(2,1)} %get-tuple-element.54), channel_id=1, source_target_pairs={{0,24},{8,0},{16,8},{24,16},{1,25},{9,1},{17,9},{25,17},{2,26},{10... | collective-permute-start | bytes 2359304 | tf_op jit(solution)/shard_map/ppermute | solution.py:20
  33.1 0.8 collective-permute-start.22
  34.9 6.6 %misfit_of.1 = (bf16[384,512]{1,0:T(8,128)(2,1)}, bf16[384,2048]{1,0:T(8,128)(2,1)}, f32[1,512]{1,0:T(1,128)}, f32[384,512]{1,0:T(8,128)}) custom-call(bf16[384,256]{1,0:T(8,128)(2,1)} %get-tuple-element.74.refs_0_, bf16[384,256]{1,0:T(8,128)(2,1)} %collective-permute-done.refs_1_, bf16[384,256]{1,0:T(8,128)(2,1)} %collective-permute-done.1.refs_2_, ...), custom_call_target="tpu_custom_call" | custom-call | flops 2013265920 | bytes 8000000 | tf_op jit(solution)/shard_map/misfit_of/pallas_call | solution.py:142
  41.5 4.6 %all-to-all-start = ((f32[4,96,512]{2,1,0:T(8,128)}), f32[4,96,512]{2,1,0:T(8,128)}, u32[]{:S(2)}, u32[]{:S(2)}) async-start(f32[4,96,512]{2,1,0:T(8,128)} %bitcast.77), calls=%async_computation | async-start | bytes 1572864 | tf_op jit(solution)/shard_map/all_to_all | solution.py:37
  46.1 11.6 %trunk_backward.1 = (f32[520,512]{1,0:T(8,128)}, f32[520,512]{1,0:T(8,128)}) custom-call(s32[1]{0:T(128)} %bitcast.core, s32[2,2048]{1,0:T(2,128)} %index.3, bf16[384,2048]{1,0:T(8,128)(2,1)} %get-tuple-element.40.misfit, bf16[384,512]{1,0:T(8,128)(2,1)} %get-tuple-element.41.coeffs, f32[2048,512]{1,0:T(8,128)} %get-tuple-element.42.first_act, ...), custom_call_target="tpu_custom_call" | custom-call | flops 6442450944 | bytes 8000000 | tf_op jit(solution)/shard_map/trunk_backward/pallas_call | solution.py:281
  57.7 1.4 collective-permute-start.6
  59.1 1.9 %fusion.19 = (bf16[96,512]{1,0:T(8,128)(2,1)}, f32[512]{0:T(512)}) fusion(f32[4,96,512]{2,1,0:T(8,128)} %all-to-all-done), kind=kLoop, calls=%fused_computation.45 | loop fusion | flops 343552 | bytes 886784 | tf_op jit(solution)/shard_map/reduce_sum | solution.py:567
  61.0 1.7 collective-permute-start.17
  62.7 2.4 %collective-permute-start.18 = (bf16[96,512]{1,0:T(8,128)(2,1)}, bf16[96,512]{1,0:T(8,128)(2,1)S(1)}, u32[]{:S(2)}, u32[]{:S(2)}) collective-permute-start(bf16[96,512]{1,0:T(8,128)(2,1)} %get-tuple-element.67.refs_0_), channel_id=1, source_target_pairs={{0,2},{1,3},{2,0},{3,1},{4,6},{5,7},{6,4},{7,5},{8,10},{9,11},{10,... | collective-permute-start | bytes 294920 | tf_op jit(solution)/shard_map/ppermute | solution.py:20
  65.1 1.8 collective-permute-done.17.refs_1_
  67.5 1.6 collective-permute-start.19
  69.1 1.2 collective-permute-done.18.refs_2_
  71.5 0.9 copy-done.4
  72.5 0.9 copy-done.6
  73.3 0.9 copy-done.8
  74.2 2.1 %pre_of.1 = (bf16[384,256]{1,0:T(8,128)(2,1)}, f32[1,256]{1,0:T(1,128)S(1)}, f32[512,256]{1,0:T(8,128)S(1)}) custom-call(s32[1]{0:T(128)} %bitcast.2.ix, bf16[96,512]{1,0:T(8,128)(2,1)} %get-tuple-element.67.refs_0_, bf16[96,512]{1,0:T(8,128)(2,1)S(1)} %copy-done.6, bf16[96,512]{1,0:T(8,128)(2,1)S(1)} %copy-done.8, ...), custom_call_target="tpu_custom_call" | custom-call | flops 201326592 | bytes 2000000 | tf_op jit(solution)/shard_map/pre_of/pallas_call | solution.py:186
  76.3 0.8 copy-done.2
  77.6 2.1 %collective-permute-start.25 = (bf16[384,256]{1,0:T(8,128)(2,1)}, bf16[384,256]{1,0:T(8,128)(2,1)}, u32[]{:S(2)}, u32[]{:S(2)}) collective-permute-start(bf16[384,256]{1,0:T(8,128)(2,1)} %get-tuple-element.51), channel_id=1, source_target_pairs={{0,24},{8,0},{16,8},{24,16},{1,25},{9,1},{17,9},{25,17},{2,26},{10... | collective-permute-start | bytes 589832 | tf_op jit(solution)/shard_map/ppermute | solution.py:20
  79.7 1.1 copy.27
  80.8 0.7 pad.4
  81.7 1.4 collective-permute-start.23
  83.2 1.7 collective-permute-start.21
  84.9 2.6 %fusion.23 = f32[1024,256]{1,0:T(8,128)} fusion(bf16[1024,384]{1,0:T(8,128)(2,1)} %collective-permute-done.24, bf16[384,256]{1,0:T(8,128)(2,1)} %collective-permute-done.25), kind=kOutput, calls=%fused_computation.49 | convolution fusion | flops 201326592 | bytes 2031616 | tf_op jit(solution)/shard_map/dot_general | solution.py:597
  87.4 4.5 %collective-permute-start.27 = (f32[264,256]{1,0:T(8,128)S(1)}, f32[264,256]{1,0:T(8,128)}, u32[]{:S(2)}, u32[]{:S(2)}) collective-permute-start(f32[264,256]{1,0:T(8,128)S(1)} %fusion.4), channel_id=1, source_target_pairs={{0,4},{4,0},{1,5},{5,1},{2,6},{6,2},{3,7},{7,3},{8,12},{12,8},{9,1... | collective-permute-start | bytes 811016 | tf_op jit(solution)/shard_map/ppermute | solution.py:20
  92.0 3.0 %collective-permute-done.23 = bf16[384,256]{1,0:T(8,128)(2,1)S(1)} collective-permute-done((bf16[384,256]{1,0:T(8,128)(2,1)}, bf16[384,256]{1,0:T(8,128)(2,1)S(1)}, u32[]{:S(2)}, u32[]{:S(2)}) %collective-permute-start.23) | collective-permute-done | bytes 196640 | tf_op jit(solution)/shard_map/ppermute | solution.py:20
  94.9 2.5 %fusion.22 = f32[1024,256]{1,0:T(8,128)} fusion(bf16[1024,384]{1,0:T(8,128)(2,1)} %collective-permute-done.22, bf16[384,256]{1,0:T(8,128)(2,1)S(1)} %collective-permute-done.23), kind=kOutput, calls=%fused_computation.48 | convolution fusion | flops 201326592 | bytes 2031616 | tf_op jit(solution)/shard_map/dot_general | solution.py:597
  97.8 1.0 convert_element_type.34
  98.8 4.3 %all-to-all-start.1 = ((f16[16,40,512]{2,1,0:T(8,128)(2,1)}), f16[16,40,512]{2,1,0:T(8,128)(2,1)}, u32[]{:S(2)}, u32[]{:S(2)}) async-start(f16[16,40,512]{2,1,0:T(8,128)(2,1)} %convert_element_type.34), calls=%async_computation.1 | async-start | bytes 1310720 | tf_op jit(solution)/shard_map/all_to_all | solution.py:37
  103.1 1.7 fusion.21
  104.8 1.8 fusion.1
  106.6 7.3 %all-to-all-done.1 = f16[16,40,512]{2,1,0:T(8,128)(2,1)} async-done(((f16[16,40,512]{2,1,0:T(8,128)(2,1)}), f16[16,40,512]{2,1,0:T(8,128)(2,1)}, u32[]{:S(2)}, u32[]{:S(2)}) %all-to-all-start.1) | async-done | bytes 655392 | tf_op jit(solution)/shard_map/all_to_all | solution.py:37
  114.0 1.3 convert_element_type.35.got
  115.4 1.7 collective-permute-start.7
  117.2 3.4 %collective-permute-start.26 = (f32[8,64,256]{2,1,0:T(8,128)S(1)}, f32[8,64,256]{2,1,0:T(8,128)S(1)}, u32[]{:S(2)}, u32[]{:S(2)}) collective-permute-start(f32[8,64,256]{2,1,0:T(8,128)S(1)} %dynamic-slice_bitcast_fusion), channel_id=1, source_target_pairs={{0,4},{4,0},{1,5},{5,1},{2,6},{6,2},{3,7},{7,3},{8,12},{12,8},{9,1... | collective-permute-start | bytes 1572872 | tf_op jit(solution)/shard_map/ppermute | solution.py:41
  120.6 3.1 %collective-permute-start.8 = (f32[40,512]{1,0:T(8,128)S(1)}, f32[40,512]{1,0:T(8,128)S(1)}, u32[]{:S(2)}, u32[]{:S(2)}) collective-permute-start(f32[40,512]{1,0:T(8,128)S(1)} %add.92), channel_id=1, source_target_pairs={{0,64},{32,96},{64,0},{96,32},{128,192},{160,224},{192,128},{224,1... | collective-permute-start | bytes 245768 | tf_op jit(solution)/shard_map/ppermute | solution.py:318
  123.7 1.0 fusion.7
  124.7 1.4 collective-permute-done.8
  126.2 5.7 %collective-permute-start.9 = (f32[40,512]{1,0:T(8,128)S(1)}, f32[40,512]{1,0:T(8,128)S(1)}, u32[]{:S(2)}, u32[]{:S(2)}) collective-permute-start(f32[40,512]{1,0:T(8,128)S(1)} %add.93), channel_id=1, source_target_pairs={{0,128},{32,160},{64,192},{96,224},{128,0},{160,32},{192,64},{224,... | collective-permute-start | bytes 245768 | tf_op jit(solution)/shard_map/ppermute | solution.py:318
  132.5 0.7 collective-permute-start.29
  133.4 1.0 collective-permute-done.9
  135.6 1.1 collective-permute-start.11
  137.3 0.8 collective-permute-start.12
  138.3 1.2 collective-permute-done.10
  140.4 1.0 collective-permute-start.13
  141.4 1.9 %collective-permute-start.14 = (f16[4,40,512]{2,1,0:T(8,128)(2,1)S(1)}, f16[4,40,512]{2,1,0:T(8,128)(2,1)S(1)}, u32[]{:S(2)}, u32[]{:S(2)}) collective-permute-start(f16[4,40,512]{2,1,0:T(8,128)(2,1)S(1)} %pad_maximum_fusion), channel_id=1, source_target_pairs={{0,16},{8,24},{16,0},{24,8},{1,17},{9,25},{17,1},{25,9},{2,18},{10... | collective-permute-start | bytes 491528 | tf_op jit(solution)/shard_map/ppermute | solution.py:20
  143.3 1.8 collective-permute-start.15
  147.7 0.9 collective-permute-done.14
  150.0 8.5 %collective-permute-start.16 = (f16[16,40,512]{2,1,0:T(8,128)(2,1)}, f16[16,40,512]{2,1,0:T(8,128)(2,1)}, u32[]{:S(2)}, u32[]{:S(2)}) collective-permute-start(f16[16,40,512]{2,1,0:T(8,128)(2,1)} %constant_dynamic-update-slice_fusion), channel_id=1, source_target_pairs={{0,4},{4,0},{1,5},{5,1},{2,6},{6,2},{3,7},{7,3},{8,12},{12,8},{9,1... | collective-permute-start | bytes 1966088 | tf_op jit(solution)/shard_map/ppermute | solution.py:41
  158.7 0.8 convert_element_type.41
  159.5 6.2 %all-to-all-start.2 = ((f16[8,80,256]{2,1,0:T(8,128)(2,1)}), f16[8,80,256]{2,1,0:T(8,128)(2,1)S(1)}, u32[]{:S(2)}, u32[]{:S(2)}) async-start(f16[8,80,256]{2,1,0:T(8,128)(2,1)} %convert_element_type.41), calls=%async_computation.2 | async-start | bytes 655360 | tf_op jit(solution)/shard_map/all_to_all | solution.py:37
  165.8 13.7 %all-to-all-done.2 = f16[8,80,256]{2,1,0:T(8,128)(2,1)S(1)} async-done(((f16[8,80,256]{2,1,0:T(8,128)(2,1)}), f16[8,80,256]{2,1,0:T(8,128)(2,1)S(1)}, u32[]{:S(2)}, u32[]{:S(2)}) %all-to-all-start.2) | async-done | bytes 327712 | tf_op jit(solution)/shard_map/all_to_all | solution.py:37
  180.2 1.2 convert_element_type.38.got
  181.5 1.3 convert_element_type.39.other
  182.7 2.1 %finished.1 = (f32[512,512]{1,0:T(8,128)}, f32[512,512]{1,0:T(8,128)}, f32[2,512]{1,0:T(2,128)}, f32[1,512]{1,0:T(1,128)}, f32[1,512]{1,0:T(1,128)}, /*index=5*/...) custom-call(s32[3]{0:T(128)S(1)} %pad_add_fusion.place, f32[16,40,512]{2,1,0:T(8,128)S(1)} %convert_element_type.38.got, ...), custom_call_target="tpu_custom_call" | custom-call | tf_op jit(solution)/shard_map/finished/pallas_call | solution.py:467
  (93 shorter events, 13.4 us)
Async XLA Ops:
  0.6 1.6 copy-start
  0.7 7.2 %copy-start.3 = (bf16[256,512]{1,0:T(8,128)(2,1)S(1)}, bf16[256,512]{1,0:T(8,128)(2,1)}, u32[]{:S(2)}) copy-start(bf16[256,512]{1,0:T(8,128)(2,1)} %refs_5_.1) | copy-start | bytes 786436
  5.8 13.5 %collective-permute-start = (bf16[384,256]{1,0:T(8,128)(2,1)}, bf16[384,256]{1,0:T(8,128)(2,1)}, u32[]{:S(2)}, u32[]{:S(2)}) collective-permute-start(bf16[384,256]{1,0:T(8,128)(2,1)} %get-tuple-element.74.refs_0_), channel_id=1, source_target_pairs={{0,1},{1,2},{2,3},{3,0},{4,5},{5,6},{6,7},{7,4},{8,9},{9,10},{10,1... | collective-permute-start | bytes 589832 | tf_op jit(solution)/shard_map/ppermute | solution.py:20
  7.8 26.1 %collective-permute-start.3 = (bf16[256,512]{1,0:T(8,128)(2,1)S(1)}, bf16[256,512]{1,0:T(8,128)(2,1)S(1)}, u32[]{:S(2)}, u32[]{:S(2)}) collective-permute-start(bf16[256,512]{1,0:T(8,128)(2,1)S(1)} %copy-done.3), channel_id=1, source_target_pairs={{0,1},{1,2},{2,3},{3,0},{4,5},{5,6},{6,7},{7,4},{8,9},{9,10},{10,1... | collective-permute-start | bytes 786440 | tf_op jit(solution)/shard_map/ppermute | solution.py:20
  9.0 24.9 %collective-permute-start.4 = (bf16[256,512]{1,0:T(8,128)(2,1)S(1)}, bf16[256,512]{1,0:T(8,128)(2,1)S(1)}, u32[]{:S(2)}, u32[]{:S(2)}) collective-permute-start(bf16[256,512]{1,0:T(8,128)(2,1)S(1)} %copy-done.3), channel_id=1, source_target_pairs={{0,2},{1,3},{2,0},{3,1},{4,6},{5,7},{6,4},{7,5},{8,10},{9,11},{10,... | collective-permute-start | bytes 786440 | tf_op jit(solution)/shard_map/ppermute | solution.py:20
  10.3 23.6 %collective-permute-start.5 = (bf16[256,512]{1,0:T(8,128)(2,1)S(1)}, bf16[256,512]{1,0:T(8,128)(2,1)S(1)}, u32[]{:S(2)}, u32[]{:S(2)}) collective-permute-start(bf16[256,512]{1,0:T(8,128)(2,1)S(1)} %copy-done.3), channel_id=1, source_target_pairs={{0,3},{1,0},{2,1},{3,2},{4,7},{5,4},{6,5},{7,6},{8,11},{9,8},{10,9... | collective-permute-start | bytes 786440 | tf_op jit(solution)/shard_map/ppermute | solution.py:20
  12.3 18.0 %collective-permute-start.1 = (bf16[384,256]{1,0:T(8,128)(2,1)}, bf16[384,256]{1,0:T(8,128)(2,1)}, u32[]{:S(2)}, u32[]{:S(2)}) collective-permute-start(bf16[384,256]{1,0:T(8,128)(2,1)} %get-tuple-element.74.refs_0_), channel_id=1, source_target_pairs={{0,2},{1,3},{2,0},{3,1},{4,6},{5,7},{6,4},{7,5},{8,10},{9,11},{10,... | collective-permute-start | bytes 589832 | tf_op jit(solution)/shard_map/ppermute | solution.py:20
  19.3 13.7 %collective-permute-start.2 = (bf16[384,256]{1,0:T(8,128)(2,1)}, bf16[384,256]{1,0:T(8,128)(2,1)S(1)}, u32[]{:S(2)}, u32[]{:S(2)}) collective-permute-start(bf16[384,256]{1,0:T(8,128)(2,1)} %get-tuple-element.74.refs_0_), channel_id=1, source_target_pairs={{0,3},{1,0},{2,1},{3,2},{4,7},{5,4},{6,5},{7,6},{8,11},{9,8},{10,9... | collective-permute-start | bytes 589832 | tf_op jit(solution)/shard_map/ppermute | solution.py:20
  30.4 51.3 %collective-permute-start.24 = (bf16[1024,384]{1,0:T(8,128)(2,1)}, bf16[1024,384]{1,0:T(8,128)(2,1)}, u32[]{:S(2)}, u32[]{:S(2)}) collective-permute-start(bf16[1024,384]{1,0:T(8,128)(2,1)} %get-tuple-element.54), channel_id=1, source_target_pairs={{0,24},{8,0},{16,8},{24,16},{1,25},{9,1},{17,9},{25,17},{2,26},{10... | collective-permute-start | bytes 2359304 | tf_op jit(solution)/shard_map/ppermute | solution.py:20
  33.1 0.8 copy-start.19
  33.1 54.4 %collective-permute-start.22 = (bf16[1024,384]{1,0:T(8,128)(2,1)}, bf16[1024,384]{1,0:T(8,128)(2,1)}, u32[]{:S(2)}, u32[]{:S(2)}) collective-permute-start(bf16[1024,384]{1,0:T(8,128)(2,1)} %get-tuple-element.53), channel_id=1, source_target_pairs={{0,16},{8,24},{16,0},{24,8},{1,17},{9,25},{17,1},{25,9},{2,18},{10... | collective-permute-start | bytes 2359304 | tf_op jit(solution)/shard_map/ppermute | solution.py:20
  33.9 0.7 copy-start.16
  33.9 0.9 copy-start.17
  33.9 0.9 copy-start.18
  41.5 17.6 %all-to-all-start = ((f32[4,96,512]{2,1,0:T(8,128)}), f32[4,96,512]{2,1,0:T(8,128)}, u32[]{:S(2)}, u32[]{:S(2)}) async-start(f32[4,96,512]{2,1,0:T(8,128)} %bitcast.77), calls=%async_computation | async-start | bytes 1572864 | tf_op jit(solution)/shard_map/all_to_all | solution.py:37
  57.7 39.8 %collective-permute-start.6 = (f32[520,512]{1,0:T(8,128)}, f32[520,512]{1,0:T(8,128)S(1)}, u32[]{:S(2)}, u32[]{:S(2)}) collective-permute-start(f32[520,512]{1,0:T(8,128)} %get-tuple-element.45), channel_id=1, source_target_pairs={{0,4},{4,0},{1,5},{5,1},{2,6},{6,2},{3,7},{7,3},{8,12},{12,8},{9,1... | collective-permute-start | bytes 3194888 | tf_op jit(solution)/shard_map/ppermute | solution.py:41
  61.0 5.9 %collective-permute-start.17 = (bf16[96,512]{1,0:T(8,128)(2,1)}, bf16[96,512]{1,0:T(8,128)(2,1)S(1)}, u32[]{:S(2)}, u32[]{:S(2)}) collective-permute-start(bf16[96,512]{1,0:T(8,128)(2,1)} %get-tuple-element.67.refs_0_), channel_id=1, source_target_pairs={{0,1},{1,2},{2,3},{3,0},{4,5},{5,6},{6,7},{7,4},{8,9},{9,10},{10,1... | collective-permute-start | bytes 294920 | tf_op jit(solution)/shard_map/ppermute | solution.py:20
  62.7 7.6 %collective-permute-start.18 = (bf16[96,512]{1,0:T(8,128)(2,1)}, bf16[96,512]{1,0:T(8,128)(2,1)S(1)}, u32[]{:S(2)}, u32[]{:S(2)}) collective-permute-start(bf16[96,512]{1,0:T(8,128)(2,1)} %get-tuple-element.67.refs_0_), channel_id=1, source_target_pairs={{0,2},{1,3},{2,0},{3,1},{4,6},{5,7},{6,4},{7,5},{8,10},{9,11},{10,... | collective-permute-start | bytes 294920 | tf_op jit(solution)/shard_map/ppermute | solution.py:20
  66.9 0.6 copy-start.5
  67.5 4.0 %collective-permute-start.19 = (bf16[96,512]{1,0:T(8,128)(2,1)}, bf16[96,512]{1,0:T(8,128)(2,1)}, u32[]{:S(2)}, u32[]{:S(2)}) collective-permute-start(bf16[96,512]{1,0:T(8,128)(2,1)} %get-tuple-element.67.refs_0_), channel_id=1, source_target_pairs={{0,3},{1,0},{2,1},{3,2},{4,7},{5,4},{6,5},{7,6},{8,11},{9,8},{10,9... | collective-permute-start | bytes 294920 | tf_op jit(solution)/shard_map/ppermute | solution.py:20
  70.3 0.6 copy-start.7
  70.9 32.2 %collective-permute-start.20 = (bf16[1024,384]{1,0:T(8,128)(2,1)}, bf16[1024,384]{1,0:T(8,128)(2,1)}, u32[]{:S(2)}, u32[]{:S(2)}) collective-permute-start(bf16[1024,384]{1,0:T(8,128)(2,1)} %get-tuple-element.52), channel_id=1, source_target_pairs={{0,8},{8,16},{16,24},{24,0},{1,9},{9,17},{17,25},{25,1},{2,10},{10... | collective-permute-start | bytes 2359304 | tf_op jit(solution)/shard_map/ppermute | solution.py:20
  71.5 1.0 copy-start.4
  72.5 0.9 copy-start.6
  73.3 0.9 copy-start.8
  76.3 0.8 copy-start.2
  77.1 0.6 copy-start.11
  77.6 5.5 %collective-permute-start.25 = (bf16[384,256]{1,0:T(8,128)(2,1)}, bf16[384,256]{1,0:T(8,128)(2,1)}, u32[]{:S(2)}, u32[]{:S(2)}) collective-permute-start(bf16[384,256]{1,0:T(8,128)(2,1)} %get-tuple-element.51), channel_id=1, source_target_pairs={{0,24},{8,0},{16,8},{24,16},{1,25},{9,1},{17,9},{25,17},{2,26},{10... | collective-permute-start | bytes 589832 | tf_op jit(solution)/shard_map/ppermute | solution.py:20
  80.8 0.8 copy-start.12
  81.7 15.8 %copy-start.1 = (f32[520,512]{1,0:T(8,128)S(1)}, f32[520,512]{1,0:T(8,128)}, u32[]{:S(2)}) copy-start(f32[520,512]{1,0:T(8,128)} %get-tuple-element.44.mine) | copy-start | bytes 3194884
  81.7 15.8 %copy-start.9 = (f32[512]{0:T(512)S(1)}, f32[512]{0:T(512)}, u32[]{:S(2)}) copy-start(f32[512]{0:T(512)} %get-tuple-element.68) | copy-start | bytes 6148
  81.7 15.8 %copy-start.10 = (f32[1,512]{1,0:T(1,128)S(1)}, f32[1,512]{1,0:T(1,128)}, u32[]{:S(2)}) copy-start(f32[1,512]{1,0:T(1,128)} %get-tuple-element.47.squares) | copy-start | bytes 6148
  81.7 13.2 %collective-permute-start.23 = (bf16[384,256]{1,0:T(8,128)(2,1)}, bf16[384,256]{1,0:T(8,128)(2,1)S(1)}, u32[]{:S(2)}, u32[]{:S(2)}) collective-permute-start(bf16[384,256]{1,0:T(8,128)(2,1)} %get-tuple-element.51), channel_id=1, source_target_pairs={{0,16},{8,24},{16,0},{24,8},{1,17},{9,25},{17,1},{25,9},{2,18},{10... | collective-permute-start | bytes 589832 | tf_op jit(solution)/shard_map/ppermute | solution.py:20
  83.2 19.9 %collective-permute-start.21 = (bf16[384,256]{1,0:T(8,128)(2,1)}, bf16[384,256]{1,0:T(8,128)(2,1)}, u32[]{:S(2)}, u32[]{:S(2)}) collective-permute-start(bf16[384,256]{1,0:T(8,128)(2,1)} %get-tuple-element.51), channel_id=1, source_target_pairs={{0,8},{8,16},{16,24},{24,0},{1,9},{9,17},{17,25},{25,1},{2,10},{10... | collective-permute-start | bytes 589832 | tf_op jit(solution)/shard_map/ppermute | solution.py:20
  87.4 36.2 %collective-permute-start.27 = (f32[264,256]{1,0:T(8,128)S(1)}, f32[264,256]{1,0:T(8,128)}, u32[]{:S(2)}, u32[]{:S(2)}) collective-permute-start(f32[264,256]{1,0:T(8,128)S(1)} %fusion.4), channel_id=1, source_target_pairs={{0,4},{4,0},{1,5},{5,1},{2,6},{6,2},{3,7},{7,3},{8,12},{12,8},{9,1... | collective-permute-start | bytes 811016 | tf_op jit(solution)/shard_map/ppermute | solution.py:20
  98.8 15.2 %all-to-all-start.1 = ((f16[16,40,512]{2,1,0:T(8,128)(2,1)}), f16[16,40,512]{2,1,0:T(8,128)(2,1)}, u32[]{:S(2)}, u32[]{:S(2)}) async-start(f16[16,40,512]{2,1,0:T(8,128)(2,1)} %convert_element_type.34), calls=%async_computation.1 | async-start | bytes 1310720 | tf_op jit(solution)/shard_map/all_to_all | solution.py:37
  103.1 1.8 copy-start.14
  103.1 1.8 copy-start.15
  114.0 9.7 %copy-start.13 = (f32[8,4,2,8,256]{4,3,1,0,2:T(8,128)S(1)}, f32[8,4,2,8,256]{4,3,1,0,2:T(8,128)}, u32[]{:S(2)}) copy-start(f32[8,4,2,8,256]{4,3,1,0,2:T(8,128)} %copy-done.12) | copy-start | bytes 1572868
  115.4 5.2 %collective-permute-start.7 = (f32[40,512]{1,0:T(8,128)S(1)}, f32[40,512]{1,0:T(8,128)S(1)}, u32[]{:S(2)}, u32[]{:S(2)}) collective-permute-start(f32[40,512]{1,0:T(8,128)S(1)} %plane_total.1), channel_id=1, source_target_pairs={{0,32},{32,0},{64,96},{96,64},{128,160},{160,128},{192,224},{224,1... | collective-permute-start | bytes 245768 | tf_op jit(solution)/shard_map/ppermute | solution.py:318
  117.2 41.3 %collective-permute-start.26 = (f32[8,64,256]{2,1,0:T(8,128)S(1)}, f32[8,64,256]{2,1,0:T(8,128)S(1)}, u32[]{:S(2)}, u32[]{:S(2)}) collective-permute-start(f32[8,64,256]{2,1,0:T(8,128)S(1)} %dynamic-slice_bitcast_fusion), channel_id=1, source_target_pairs={{0,4},{4,0},{1,5},{5,1},{2,6},{6,2},{3,7},{7,3},{8,12},{12,8},{9,1... | collective-permute-start | bytes 1572872 | tf_op jit(solution)/shard_map/ppermute | solution.py:41
  120.6 5.6 %collective-permute-start.8 = (f32[40,512]{1,0:T(8,128)S(1)}, f32[40,512]{1,0:T(8,128)S(1)}, u32[]{:S(2)}, u32[]{:S(2)}) collective-permute-start(f32[40,512]{1,0:T(8,128)S(1)} %add.92), channel_id=1, source_target_pairs={{0,64},{32,96},{64,0},{96,32},{128,192},{160,224},{192,128},{224,1... | collective-permute-start | bytes 245768 | tf_op jit(solution)/shard_map/ppermute | solution.py:318
  126.2 8.3 %collective-permute-start.9 = (f32[40,512]{1,0:T(8,128)S(1)}, f32[40,512]{1,0:T(8,128)S(1)}, u32[]{:S(2)}, u32[]{:S(2)}) collective-permute-start(f32[40,512]{1,0:T(8,128)S(1)} %add.93), channel_id=1, source_target_pairs={{0,128},{32,160},{64,192},{96,224},{128,0},{160,32},{192,64},{224,... | collective-permute-start | bytes 245768 | tf_op jit(solution)/shard_map/ppermute | solution.py:318
  131.9 3.7 %collective-permute-start.30 = (f32[72,256]{1,0:T(8,128)S(1)}, f32[72,256]{1,0:T(8,128)S(1)}, u32[]{:S(2)}, u32[]{:S(2)}) collective-permute-start(f32[72,256]{1,0:T(8,128)S(1)} %get-tuple-element.73), channel_id=1, source_target_pairs={{0,24},{8,0},{16,8},{24,16},{1,25},{9,1},{17,9},{25,17},{2,26},{10... | collective-permute-start | bytes 221192 | tf_op jit(solution)/shard_map/ppermute | solution.py:20
  132.5 4.7 %collective-permute-start.29 = (f32[72,256]{1,0:T(8,128)S(1)}, f32[72,256]{1,0:T(8,128)S(1)}, u32[]{:S(2)}, u32[]{:S(2)}) collective-permute-start(f32[72,256]{1,0:T(8,128)S(1)} %get-tuple-element.72), channel_id=1, source_target_pairs={{0,16},{8,24},{16,0},{24,8},{1,17},{9,25},{17,1},{25,9},{2,18},{10... | collective-permute-start | bytes 221192 | tf_op jit(solution)/shard_map/ppermute | solution.py:20
  133.3 5.0 %collective-permute-start.28 = (f32[72,256]{1,0:T(8,128)S(1)}, f32[72,256]{1,0:T(8,128)S(1)}, u32[]{:S(2)}, u32[]{:S(2)}) collective-permute-start(f32[72,256]{1,0:T(8,128)S(1)} %get-tuple-element.71), channel_id=1, source_target_pairs={{0,8},{8,16},{16,24},{24,0},{1,9},{9,17},{17,25},{25,1},{2,10},{10... | collective-permute-start | bytes 221192 | tf_op jit(solution)/shard_map/ppermute | solution.py:20
  135.3 4.2 %collective-permute-start.10 = (f16[40,512]{1,0:T(8,128)(2,1)S(1)}, f16[40,512]{1,0:T(8,128)(2,1)S(1)}, u32[]{:S(2)}, u32[]{:S(2)}) collective-permute-start(f16[40,512]{1,0:T(8,128)(2,1)S(1)} %bitcast.78), channel_id=1, source_target_pairs={{0,1},{1,2},{2,3},{3,0},{4,5},{5,6},{6,7},{7,4},{8,9},{9,10},{10,1... | collective-permute-start | bytes 122888 | tf_op jit(solution)/shard_map/ppermute | solution.py:20
  135.6 4.4 %collective-permute-start.11 = (f16[40,512]{1,0:T(8,128)(2,1)S(1)}, f16[40,512]{1,0:T(8,128)(2,1)S(1)}, u32[]{:S(2)}, u32[]{:S(2)}) collective-permute-start(f16[40,512]{1,0:T(8,128)(2,1)S(1)} %bitcast.79), channel_id=1, source_target_pairs={{0,2},{1,3},{2,0},{3,1},{4,6},{5,7},{6,4},{7,5},{8,10},{9,11},{10,... | collective-permute-start | bytes 122888 | tf_op jit(solution)/shard_map/ppermute | solution.py:20
  137.3 3.1 %collective-permute-start.12 = (f16[40,512]{1,0:T(8,128)(2,1)S(1)}, f16[40,512]{1,0:T(8,128)(2,1)S(1)}, u32[]{:S(2)}, u32[]{:S(2)}) collective-permute-start(f16[40,512]{1,0:T(8,128)(2,1)S(1)} %bitcast.80), channel_id=1, source_target_pairs={{0,3},{1,0},{2,1},{3,2},{4,7},{5,4},{6,5},{7,6},{8,11},{9,8},{10,9... | collective-permute-start | bytes 122888 | tf_op jit(solution)/shard_map/ppermute | solution.py:20
  140.4 6.6 %collective-permute-start.13 = (f16[4,40,512]{2,1,0:T(8,128)(2,1)S(1)}, f16[4,40,512]{2,1,0:T(8,128)(2,1)S(1)}, u32[]{:S(2)}, u32[]{:S(2)}) collective-permute-start(f16[4,40,512]{2,1,0:T(8,128)(2,1)S(1)} %pad_maximum_fusion), channel_id=1, source_target_pairs={{0,8},{8,16},{16,24},{24,0},{1,9},{9,17},{17,25},{25,1},{2,10},{10... | collective-permute-start | bytes 491528 | tf_op jit(solution)/shard_map/ppermute | solution.py:20
  141.4 7.1 %collective-permute-start.14 = (f16[4,40,512]{2,1,0:T(8,128)(2,1)S(1)}, f16[4,40,512]{2,1,0:T(8,128)(2,1)S(1)}, u32[]{:S(2)}, u32[]{:S(2)}) collective-permute-start(f16[4,40,512]{2,1,0:T(8,128)(2,1)S(1)} %pad_maximum_fusion), channel_id=1, source_target_pairs={{0,16},{8,24},{16,0},{24,8},{1,17},{9,25},{17,1},{25,9},{2,18},{10... | collective-permute-start | bytes 491528 | tf_op jit(solution)/shard_map/ppermute | solution.py:20
  143.3 5.9 %collective-permute-start.15 = (f16[4,40,512]{2,1,0:T(8,128)(2,1)S(1)}, f16[4,40,512]{2,1,0:T(8,128)(2,1)S(1)}, u32[]{:S(2)}, u32[]{:S(2)}) collective-permute-start(f16[4,40,512]{2,1,0:T(8,128)(2,1)S(1)} %pad_maximum_fusion), channel_id=1, source_target_pairs={{0,24},{8,0},{16,8},{24,16},{1,25},{9,1},{17,9},{25,17},{2,26},{10... | collective-permute-start | bytes 491528 | tf_op jit(solution)/shard_map/ppermute | solution.py:20
  150.0 31.5 %collective-permute-start.16 = (f16[16,40,512]{2,1,0:T(8,128)(2,1)}, f16[16,40,512]{2,1,0:T(8,128)(2,1)}, u32[]{:S(2)}, u32[]{:S(2)}) collective-permute-start(f16[16,40,512]{2,1,0:T(8,128)(2,1)} %constant_dynamic-update-slice_fusion), channel_id=1, source_target_pairs={{0,4},{4,0},{1,5},{5,1},{2,6},{6,2},{3,7},{7,3},{8,12},{12,8},{9,1... | collective-permute-start | bytes 1966088 | tf_op jit(solution)/shard_map/ppermute | solution.py:41
  159.5 19.9 %all-to-all-start.2 = ((f16[8,80,256]{2,1,0:T(8,128)(2,1)}), f16[8,80,256]{2,1,0:T(8,128)(2,1)S(1)}, u32[]{:S(2)}, u32[]{:S(2)}) async-start(f16[8,80,256]{2,1,0:T(8,128)(2,1)} %convert_element_type.41), calls=%async_computation.2 | async-start | bytes 655360 | tf_op jit(solution)/shard_map/all_to_all | solution.py:37

commit v2 on v1

--- a/solution.py
+++ b/solution.py
@@ -11,6 +11,8 @@
 
 
 GRID = 128
+BLOCK = 1024
+CUT = 1024
 DP = ("z", "y", "c")
 ALL = ("z", "y", "c", "query")
 
@@ -74,17 +76,26 @@
 def trunk_forward(query_index, v_one, c_one, v_two, c_two, v_three, c_three):
     queries = query_index.shape[1]
     trunk, basis = v_three.shape
-    block = 512
+    block = BLOCK
 
     def body(index, v_one, c_one, v_two, c_two, v_three, c_three, out, first_out, second_out):
         x, y = points_of(index[...])
-        first = jnp.tanh(x * v_one[0:1, :] + y * v_one[1:2, :] + c_one[...])
-        second = jnp.dot(first.astype(jnp.bfloat16), v_two[...], preferred_element_type=jnp.float32)
-        second = jnp.tanh(second + c_two[...])
-        first_out[...] = first
-        second_out[...] = second
-        full = jnp.dot(second.astype(jnp.bfloat16), v_three[...], preferred_element_type=jnp.float32) + c_three[...]
-        out[...] = full.astype(jnp.bfloat16)
+        cuts = [slice(at, at + CUT) for at in range(0, block, CUT)]
+        firsts = [
+            jnp.tanh(x[c] * v_one[0:1, :] + y[c] * v_one[1:2, :] + c_one[...]) for c in cuts
+        ]
+        seconds = [
+            jnp.dot(first.astype(jnp.bfloat16), v_two[...], preferred_element_type=jnp.float32)
+            for first in firsts
+        ]
+        seconds = [jnp.tanh(second + c_two[...]) for second in seconds]
+        for c, first, second in zip(cuts, firsts, seconds):
+            first_out[c, :] = first
+            second_out[c, :] = second
+            full = jnp.dot(
+                second.astype(jnp.bfloat16), v_three[...], preferred_element_type=jnp.float32
+            )
+            out[c, :] = (full + c_three[...]).astype(jnp.bfloat16)
 
     return pl.pallas_call(
         body,
@@ -118,7 +129,7 @@
     n = len(hidden_all)
     funcs, queries = targets.shape
     width = basis.shape[1]
-    block = 512
+    block = BLOCK
 
     def body(*refs):
         hidden, w_two = refs[:n], refs[n : 2 * n]
@@ -134,7 +145,9 @@
             grad[...] = jnp.zeros_like(grad)
 
         misfit = contract_cols(coeffs[...], basis[...]) * inv_scale - targets[...].astype(jnp.float32)
-        squares[...] += jnp.sum(misfit * misfit, axis=0, keepdims=True)
+        total = jnp.sum(misfit * misfit, axis=0, keepdims=True)
+        for at in range(0, block, width):
+            squares[...] += total[:, at : at + width]
         scaled_b = (misfit * grad_scale).astype(jnp.bfloat16)
         misfit_b[...] = scaled_b
         grad[...] += jnp.dot(scaled_b, basis[...], preferred_element_type=jnp.float32) * inv_scale
@@ -152,13 +165,13 @@
         out_specs=[
             whole(funcs, width),
             pl.BlockSpec((funcs, block), lambda i: (0, i)),
-            whole(1, block),
+            whole(1, width),
             whole(funcs, width),
         ],
         out_shape=[
             jax.ShapeDtypeStruct((funcs, width), jnp.bfloat16),
             jax.ShapeDtypeStruct((funcs, queries), jnp.bfloat16),
-            jax.ShapeDtypeStruct((1, block), jnp.float32),
+            jax.ShapeDtypeStruct((1, width), jnp.float32),
             jax.ShapeDtypeStruct((funcs, width), jnp.float32),
         ],
         cost_estimate=pl.CostEstimate(flops=5 * funcs * queries * width, bytes_accessed=8_000_000, transcendentals=0),
@@ -275,7 +288,7 @@
     queries = misfit_b.shape[1]
     funcs, basis = coeffs_b.shape
     trunk = v_two.shape[0]
-    block = 512
+    block = BLOCK
 
     out = jax.ShapeDtypeStruct((trunk + 8, basis), jnp.float32)
     return pl.pallas_call(
@@ -315,7 +328,8 @@
 def summed_in_pairs(x, axis):
     n, k = lax.axis_size(axis), 1
     while k < n:
-        x = x + lax.ppermute(x, axis, [(i, i ^ k) for i in range(n)])
+        pair = k | k >> 1 if 2 * k == n else k
+        x = x + lax.ppermute(x, axis, [(i, i ^ pair) for i in range(n)])
         k *= 2
     return x
 
@@ -429,19 +443,25 @@
     return out.astype(jnp.float16)
 
 
-def finished(place, got, other, side, ny, nx):
-    n, rows, w = got.shape[0], got.shape[1] - 8, got.shape[2]
+def finished(place, got, other, side):
+    ny = len(got)
+    nx, rows, w = got[0].shape[0], got[0].shape[1] - 8, got[0].shape[2]
+    n = ny * nx
     per = n // 8
 
-    def body(place, got, other, one, two, v_one, c_one, c_two, c_three, b_two, loss, small, more):
+    def body(place, *refs):
+        got, other = refs[:ny], refs[ny : 2 * ny]
+        one, two, v_one, c_one, c_two, c_three, b_two, loss, small, more = refs[2 * ny :]
+
         def put(zero, last):
             for q in range(n):
                 at = lax.rem(place[1] + ny - q // nx, ny) * nx + lax.rem(place[2] + nx - q % nx, nx)
                 into = pl.ds(pl.multiple_of(at * rows, rows), rows)
-                for x, out, part in ((zero, one, small), (last, two, more)):
-                    out[into, :] = x[q, :rows, :] * jnp.exp2(x[q, rows + 1 : rows + 2, :])
-                    part[pl.ds(at, 1), :] = x[q, rows : rows + 1, :side] * jnp.exp2(
-                        x[q, rows + 2 : rows + 3, :side]
+                for refs, out, part in ((zero, one, small), (last, two, more)):
+                    x, i = refs[q // nx], q % nx
+                    out[into, :] = x[i, :rows, :] * jnp.exp2(x[i, rows + 1 : rows + 2, :])
+                    part[pl.ds(at, 1), :] = x[i, rows : rows + 1, :side] * jnp.exp2(
+                        x[i, rows + 2 : rows + 3, :side]
                     )
 
         @pl.when(place[0] == 0)
@@ -469,14 +489,14 @@
         grid_spec=pltpu.PrefetchScalarGridSpec(
             num_scalar_prefetch=1,
             grid=(1,),
-            in_specs=[whole(*got.shape), whole(*got.shape)],
+            in_specs=[whole(*x.shape) for x in (*got, *other)],
             out_specs=[whole(*shape) for shape in shapes],
             scratch_shapes=[pltpu.VMEM((n, side), jnp.float32)] * 2,
         ),
         out_shape=[jax.ShapeDtypeStruct(shape, jnp.float32) for shape in shapes],
         compiler_params=pltpu.CompilerParams(vmem_limit_bytes=24 * 2**20),
         name="finished",
-    )(place, got, other)
+    )(place, *got, *other)
 
 
 def z_finished(got, rows):
@@ -515,11 +535,14 @@
     both = summed_in_pairs(both, "z")
     got = total_message(both, side)
     got = jnp.stack([got] + [shift(got, "query", k) for k in range(1, nx)])
-    got = jnp.concatenate([got] + [shift(got, "y", k) for k in range(1, ny)])
-    other = other_core(got)
+    pieces = [got] + [shift(got, "y", k) for k in range(1, ny)]
+    others = [other_core(p) for p in pieces]
     place = jnp.stack([lax.axis_index(a) for a in ("c", "y", "query")])
     return finished(
-        place, got.astype(jnp.float32), other.astype(jnp.float32), side, ny, nx
+        place,
+        [p.astype(jnp.float32) for p in pieces],
+        [p.astype(jnp.float32) for p in others],
+        side,
     )
 
 

time: 188 us -> 176 us (0.936)
  waiting for transfers between devices: 36.5 us -> 29.4 us
  starting transfers between devices: 75.1 us -> 71.3 us
  local copies, waits for them, and re-layouts: 13.8 us -> 10.5 us
  other arithmetic: 9.36 us -> 11.4 us
    all_to_all x3, waiting for transfers between devices: 21 us -> 6.03 us  [exchanged(): return lax.all_to_all(x, axis, 0, 0, tiled=True)]
    ppermute x25, waiting for transfers between devices: 13 us -> 21.7 us  [shift(): return lax.ppermute(x, axis, [(i, (i + k) % n) for i in range(n)])]
    ppermute x3 -> x6, starting transfers between devices: 13.3 us -> 17 us  [other_core(): return lax.ppermute(x, 'c', [(0, 1), (1, 0)])]
    unnamed x45 -> x40, local copies, waits for them, and re-layouts: 11.2 us -> 7.81 us
    ppermute x25, starting transfers between devices: 36.3 us -> 33.1 us  [shift(): return lax.ppermute(x, axis, [(i, (i + k) % n) for i in range(n)])]
    all_to_all x3, starting transfers between devices: 15 us -> 12.6 us  [exchanged(): return lax.all_to_all(x, axis, 0, 0, tiled=True)]
    ppermute x3, starting transfers between devices: 10.5 us -> 8.6 us  [summed_in_pairs(): x = x + lax.ppermute(x, axis, [(i, i ^ pair) for i in range(n)])]
    convert_element_type x2 -> x9, other arithmetic: 2.5 us -> 3.88 us  [the longest x7 3.86 us: sum_of_all(): p.astype(jnp.float32)]
  transfers between devices with their start and end apart: 34 -> 37, of which waited for: 15 -> 11; matrix products, arithmetic and copies ran while one was open for 12% -> 13% of each run, Pallas kernels for 19% -> 16%
where the time goes in v2:
time: 176 us; the launch traced here: 175 us
  starting transfers between devices  71.3 us (41%)
  Pallas kernels  36.5 us (21%)
  waiting for transfers between devices  29.4 us (17%)
  matrix products  13.2 us (8%)
  other arithmetic  11.4 us (6%)
  local copies, waits for them, and re-layouts  10.5 us (6%)
  between operations  2.86 us (2%)
    ppermute x25, starting transfers between devices, shift(): return lax.ppermute(x, axis, [(i, (i + k) % n) for i in range(n)])  33.1 us
    ppermute x25, waiting for transfers between devices, shift(): return lax.ppermute(x, axis, [(i, (i + k) % n) for i in range(n)])  21.7 us
    ppermute x6, starting transfers between devices, other_core(): return lax.ppermute(x, 'c', [(0, 1), (1, 0)])  17 us
    all_to_all x3, starting transfers between devices, exchanged(): return lax.all_to_all(x, axis, 0, 0, tiled=True)  12.6 us
    pallas_call x1, Pallas kernels, trunk_backward(): pl.pallas_call(functools.partial(back_kernel, inv_scale=inv_scale), grid_...  11.5 us
    ppermute x3, starting transfers between devices, summed_in_pairs(): x = x + lax.ppermute(x, axis, [(i, i ^ pair) for i in range(n)])  8.6 us
    unnamed x40, local copies, waits for them, and re-layouts  7.81 us
    dot_general x3, matrix products, local(): jnp.dot(sens_y[k], pre_y[k], preferred_element_type=jnp.float32)  7.65 us
  transfers between devices with their start and end apart: 37, of which 11 were waited for; matrix products, arithmetic and copies ran while one was open for 13% of the time, Pallas kernels for 16%

profile of v2, /device:TPU:1, one launch (start us, length us, event | category | flops | bytes accessed | tf_op | source)
XLA Modules:
  0.0 175.2 jit_solution(13688903607066637382)
XLA Ops:
  0.7 1.6 copy-done
  2.2 2.9 %fusion.21 = (bf16[384,256]{1,0:T(8,128)(2,1)S(1)}, f32[384,256]{1,0:T(8,128)S(1)}) fusion(f32[256]{0:T(256)} %param.17, bf16[384,4096]{1,0:T(8,128)(2,1)} %refs_3_, bf16[4096,256]{1,0:T(8,128)(2,1)S(1)} %copy-done), kind=kOutput, calls=%fused_computation.40 | convolution fusion | flops 805502976 | bytes 5833728 | tf_op jit(solution)/shard_map/dot_general | solution.py:573
  5.1 2.1 %collective-permute-start = (bf16[384,256]{1,0:T(8,128)(2,1)S(1)}, bf16[384,256]{1,0:T(8,128)(2,1)S(1)}, u32[]{:S(2)}, u32[]{:S(2)}) collective-permute-start(bf16[384,256]{1,0:T(8,128)(2,1)S(1)} %get-tuple-element.74.refs_0_), channel_id=1, source_target_pairs={{0,1},{1,2},{2,3},{3,0},{4,5},{5,6},{6,7},{7,4},{8,9},{9,10},{10,1... | collective-permute-start | bytes 589832 | tf_op jit(solution)/shard_map/ppermute | solution.py:22
  7.2 1.2 collective-permute-start.3
  8.5 1.3 collective-permute-start.4
  9.8 2.0 %collective-permute-start.5 = (bf16[256,512]{1,0:T(8,128)(2,1)S(1)}, bf16[256,512]{1,0:T(8,128)(2,1)S(1)}, u32[]{:S(2)}, u32[]{:S(2)}) collective-permute-start(bf16[256,512]{1,0:T(8,128)(2,1)S(1)} %copy-done.3), channel_id=1, source_target_pairs={{0,3},{1,0},{2,1},{3,2},{4,7},{5,4},{6,5},{7,6},{8,11},{9,8},{10,9... | collective-permute-start | bytes 786440 | tf_op jit(solution)/shard_map/ppermute | solution.py:22
  12.3 2.0 %collective-permute-start.2 = (bf16[384,256]{1,0:T(8,128)(2,1)S(1)}, bf16[384,256]{1,0:T(8,128)(2,1)}, u32[]{:S(2)}, u32[]{:S(2)}) collective-permute-start(bf16[384,256]{1,0:T(8,128)(2,1)S(1)} %get-tuple-element.74.refs_0_), channel_id=1, source_target_pairs={{0,3},{1,0},{2,1},{3,2},{4,7},{5,4},{6,5},{7,6},{8,11},{9,8},{10,9... | collective-permute-start | bytes 589832 | tf_op jit(solution)/shard_map/ppermute | solution.py:22
  14.3 6.1 %trunk_forward.1 = (bf16[2048,512]{1,0:T(8,128)(2,1)}, f32[2048,512]{1,0:T(8,128)}, f32[2048,512]{1,0:T(8,128)}) custom-call(s32[2,2048]{1,0:T(2,128)} %index.3, f32[2,512]{1,0:T(2,128)} %v_one.1, f32[1,512]{1,0:T(1,128)} %bitcast.80, bf16[512,512]{1,0:T(8,128)(2,1)} %v_two.3, f32[1,512]{1,0:T(1,128)} %bitcast.81, bf16[512,512]{1,0:T(8,128)(2,1)} %v_three.3, ...), custom_call_target="tpu_custom_call" | custom-call | flops 2147483648 | bytes 4000000 | tf_op jit(solution)/shard_map/trunk_forward/pallas_call | solution.py:100
  20.4 9.0 %collective-permute-done.1.refs_2_ = bf16[384,256]{1,0:T(8,128)(2,1)S(1)} collective-permute-done((bf16[384,256]{1,0:T(8,128)(2,1)S(1)}, bf16[384,256]{1,0:T(8,128)(2,1)S(1)}, u32[]{:S(2)}, u32[]{:S(2)}) %collective-permute-start.1) | collective-permute-done | bytes 196640 | tf_op jit(solution)/shard_map/ppermute | solution.py:22
  29.5 0.8 collective-permute-done.2.refs_3_
  31.2 5.7 %misfit_of.1 = (bf16[384,512]{1,0:T(8,128)(2,1)}, bf16[384,2048]{1,0:T(8,128)(2,1)}, f32[1,512]{1,0:T(1,128)}, f32[384,512]{1,0:T(8,128)}) custom-call(bf16[384,256]{1,0:T(8,128)(2,1)} %copy-done.17, bf16[384,256]{1,0:T(8,128)(2,1)} %copy-done.18, bf16[384,256]{1,0:T(8,128)(2,1)} %copy-done.19, bf16[384,256]{1,0:T(8,128)(2,1)} %collective-permute-done.2.refs_3_, ...), custom_call_target="tpu_custom_call" | custom-call | flops 2013265920 | bytes 8000000 | tf_op jit(solution)/shard_map/misfit_of/pallas_call | solution.py:155
  36.9 4.8 %all-to-all-start = ((f32[4,96,512]{2,1,0:T(8,128)}), f32[4,96,512]{2,1,0:T(8,128)S(1)}, u32[]{:S(2)}, u32[]{:S(2)}) async-start(f32[4,96,512]{2,1,0:T(8,128)} %bitcast.75), calls=%async_computation | async-start | bytes 1572864 | tf_op jit(solution)/shard_map/all_to_all | solution.py:39
  41.7 6.5 %columns_by_y.1 = (bf16[1024,384]{1,0:T(8,128)(2,1)}, bf16[1024,384]{1,0:T(8,128)(2,1)}, bf16[1024,384]{1,0:T(8,128)(2,1)}, bf16[1024,384]{1,0:T(8,128)(2,1)}) custom-call(s32[1]{0:T(128)} %bitcast.1.y, bf16[384,4096]{1,0:T(8,128)(2,1)} %refs_3_, bf16[384,4096]{1,0:T(8,128)(2,1)} %refs_3_, bf16[384,4096]{1,0:T(8,128)(2,1)} %refs_3_, bf16[384,4096]{1,0:T(8,128)(2,1)} %refs_3_), custom_call_target="tpu_custom_call" | custom-call | flops 8000000 | bytes 6291456 | tf_op jit(solution)/shard_map/columns_by_y/pallas_call | solution.py:229
  48.2 2.8 %collective-permute-start.27 = (bf16[1024,384]{1,0:T(8,128)(2,1)}, bf16[1024,384]{1,0:T(8,128)(2,1)}, u32[]{:S(2)}, u32[]{:S(2)}) collective-permute-start(bf16[1024,384]{1,0:T(8,128)(2,1)} %get-tuple-element.54), channel_id=1, source_target_pairs={{0,24},{8,0},{16,8},{24,16},{1,25},{9,1},{17,9},{25,17},{2,26},{10... | collective-permute-start | bytes 2359304 | tf_op jit(solution)/shard_map/ppermute | solution.py:22
  51.3 1.9 %all-to-all-done = f32[4,96,512]{2,1,0:T(8,128)S(1)} async-done(((f32[4,96,512]{2,1,0:T(8,128)}), f32[4,96,512]{2,1,0:T(8,128)S(1)}, u32[]{:S(2)}, u32[]{:S(2)}) %all-to-all-start) | async-done | bytes 786464 | tf_op jit(solution)/shard_map/all_to_all | solution.py:39
  54.2 1.8 %collective-permute-start.21 = (bf16[96,512]{1,0:T(8,128)(2,1)}, bf16[96,512]{1,0:T(8,128)(2,1)S(1)}, u32[]{:S(2)}, u32[]{:S(2)}) collective-permute-start(bf16[96,512]{1,0:T(8,128)(2,1)} %get-tuple-element.67.refs_0_), channel_id=1, source_target_pairs={{0,2},{1,3},{2,0},{3,1},{4,6},{5,7},{6,4},{7,5},{8,10},{9,11},{10,... | collective-permute-start | bytes 294920 | tf_op jit(solution)/shard_map/ppermute | solution.py:22
  56.0 1.1 collective-permute-start.22
  57.1 11.5 %trunk_backward.1 = (f32[520,512]{1,0:T(8,128)}, f32[520,512]{1,0:T(8,128)}) custom-call(s32[1]{0:T(128)} %bitcast.core, s32[2,2048]{1,0:T(2,128)} %index.3, bf16[384,2048]{1,0:T(8,128)(2,1)} %get-tuple-element.40.misfit, bf16[384,512]{1,0:T(8,128)(2,1)} %get-tuple-element.41.coeffs, f32[2048,512]{1,0:T(8,128)} %get-tuple-element.42.first_act, ...), custom_call_target="tpu_custom_call" | custom-call | flops 6442450944 | bytes 8000000 | tf_op jit(solution)/shard_map/trunk_backward/pallas_call | solution.py:294
  69.2 2.6 %collective-permute-start.6 = (f32[520,512]{1,0:T(8,128)}, f32[520,512]{1,0:T(8,128)S(1)}, u32[]{:S(2)}, u32[]{:S(2)}) collective-permute-start(f32[520,512]{1,0:T(8,128)} %get-tuple-element.45), channel_id=1, source_target_pairs={{0,4},{4,0},{1,5},{5,1},{2,6},{6,2},{3,7},{7,3},{8,12},{12,8},{9,1... | collective-permute-start | bytes 3194888 | tf_op jit(solution)/shard_map/ppermute | solution.py:43
  73.1 0.9 copy-done.4
  74.0 0.9 copy-done.6
  74.9 0.9 copy-done.8
  75.8 2.1 %pre_of.1 = (bf16[384,256]{1,0:T(8,128)(2,1)}, f32[1,256]{1,0:T(1,128)S(1)}, f32[512,256]{1,0:T(8,128)S(1)}) custom-call(s32[1]{0:T(128)} %bitcast.2.ix, bf16[96,512]{1,0:T(8,128)(2,1)} %get-tuple-element.67.refs_0_, bf16[96,512]{1,0:T(8,128)(2,1)S(1)} %copy-done.6, bf16[96,512]{1,0:T(8,128)(2,1)S(1)} %copy-done.8, ...), custom_call_target="tpu_custom_call" | custom-call | flops 201326592 | bytes 2000000 | tf_op jit(solution)/shard_map/pre_of/pallas_call | solution.py:199
  79.2 2.0 %collective-permute-start.28 = (bf16[384,256]{1,0:T(8,128)(2,1)}, bf16[384,256]{1,0:T(8,128)(2,1)}, u32[]{:S(2)}, u32[]{:S(2)}) collective-permute-start(bf16[384,256]{1,0:T(8,128)(2,1)} %get-tuple-element.51), channel_id=1, source_target_pairs={{0,24},{8,0},{16,8},{24,16},{1,25},{9,1},{17,9},{25,17},{2,26},{10... | collective-permute-start | bytes 589832 | tf_op jit(solution)/shard_map/ppermute | solution.py:22
  81.2 1.1 copy.27
  83.1 1.5 collective-permute-start.26
  84.6 4.2 %collective-permute-done.28 = bf16[384,256]{1,0:T(8,128)(2,1)} collective-permute-done((bf16[384,256]{1,0:T(8,128)(2,1)}, bf16[384,256]{1,0:T(8,128)(2,1)}, u32[]{:S(2)}, u32[]{:S(2)}) %collective-permute-start.28) | collective-permute-done | bytes 196640 | tf_op jit(solution)/shard_map/ppermute | solution.py:22
  88.7 3.9 %collective-permute-start.24 = (bf16[384,256]{1,0:T(8,128)(2,1)}, bf16[384,256]{1,0:T(8,128)(2,1)S(1)}, u32[]{:S(2)}, u32[]{:S(2)}) collective-permute-start(bf16[384,256]{1,0:T(8,128)(2,1)} %get-tuple-element.51), channel_id=1, source_target_pairs={{0,8},{8,16},{16,24},{24,0},{1,9},{9,17},{17,25},{25,1},{2,10},{10... | collective-permute-start | bytes 589832 | tf_op jit(solution)/shard_map/ppermute | solution.py:22
  92.7 2.6 %fusion.24 = f32[1024,256]{1,0:T(8,128)} fusion(bf16[1024,384]{1,0:T(8,128)(2,1)} %collective-permute-done.27, bf16[384,256]{1,0:T(8,128)(2,1)} %collective-permute-done.28), kind=kOutput, calls=%fused_computation.43 | convolution fusion | flops 201326592 | bytes 2031616 | tf_op jit(solution)/shard_map/dot_general | solution.py:620
  95.2 0.9 collective-permute-start.30
  96.1 1.5 collective-permute-done.26
  97.7 2.5 %fusion.23 = f32[1024,256]{1,0:T(8,128)} fusion(bf16[1024,384]{1,0:T(8,128)(2,1)} %collective-permute-done.25, bf16[384,256]{1,0:T(8,128)(2,1)S(1)} %collective-permute-done.26), kind=kOutput, calls=%fused_computation.42 | convolution fusion | flops 201326592 | bytes 2031616 | tf_op jit(solution)/shard_map/dot_general | solution.py:620
  100.2 2.0 %collective-permute-done.24 = bf16[384,256]{1,0:T(8,128)(2,1)S(1)} collective-permute-done((bf16[384,256]{1,0:T(8,128)(2,1)}, bf16[384,256]{1,0:T(8,128)(2,1)S(1)}, u32[]{:S(2)}, u32[]{:S(2)}) %collective-permute-start.24) | collective-permute-done | bytes 196640 | tf_op jit(solution)/shard_map/ppermute | solution.py:22
  102.2 2.6 %fusion.22 = f32[1024,256]{1,0:T(8,128)} fusion(bf16[1024,384]{1,0:T(8,128)(2,1)} %collective-permute-done.23, bf16[384,256]{1,0:T(8,128)(2,1)S(1)} %collective-permute-done.24), kind=kOutput, calls=%fused_computation.41 | convolution fusion | flops 201326592 | bytes 2031616 | tf_op jit(solution)/shard_map/dot_general | solution.py:620
  105.1 1.0 convert_element_type.52
  106.1 4.3 %all-to-all-start.1 = ((f16[16,40,512]{2,1,0:T(8,128)(2,1)}), f16[16,40,512]{2,1,0:T(8,128)(2,1)}, u32[]{:S(2)}, u32[]{:S(2)}) async-start(f16[16,40,512]{2,1,0:T(8,128)(2,1)} %convert_element_type.52), calls=%async_computation.1 | async-start | bytes 1310720 | tf_op jit(solution)/shard_map/all_to_all | solution.py:39
  110.4 2.7 %fusion.1 = f32[1024,256]{1,0:T(8,128)S(1)} fusion(f32[1024,256]{1,0:T(8,128)} %fusion.24, f32[1024,256]{1,0:T(8,128)} %fusion.23, f32[1024,256]{1,0:T(8,128)} %fusion.22, bf16[1024,384]{1,0:T(8,128)(2,1)} %get-tuple-element.50, bf16[384,256]{1,0:T(8,128)(2,1)} %get-tuple-element.51), kind=kOutput, calls=%fused_computation.2 | convolution fusion | flops 202113024 | bytes 5177344 | tf_op jit(solution)/shard_map/dot_general | solution.py:618
  113.1 1.0 fusion.7
  114.9 2.5 %collective-permute-start.33 = (f32[72,256]{1,0:T(8,128)}, f32[72,256]{1,0:T(8,128)}, u32[]{:S(2)}, u32[]{:S(2)}) collective-permute-start(f32[72,256]{1,0:T(8,128)} %get-tuple-element.71), channel_id=1, source_target_pairs={{0,24},{8,0},{16,8},{24,16},{1,25},{9,1},{17,9},{25,17},{2,26},{10... | collective-permute-start | bytes 221192 | tf_op jit(solution)/shard_map/ppermute | solution.py:22
  118.6 4.1 %all-to-all-done.1 = f16[16,40,512]{2,1,0:T(8,128)(2,1)} async-done(((f16[16,40,512]{2,1,0:T(8,128)(2,1)}), f16[16,40,512]{2,1,0:T(8,128)(2,1)}, u32[]{:S(2)}, u32[]{:S(2)}) %all-to-all-start.1) | async-done | bytes 655392 | tf_op jit(solution)/shard_map/all_to_all | solution.py:39
  122.7 1.2 convert_element_type.53.got
  124.1 1.7 collective-permute-start.7
  125.8 0.8 dynamic-slice_bitcast_fusion
  126.7 2.1 %collective-permute-start.29 = (f32[8,64,256]{2,1,0:T(8,128)}, f32[8,64,256]{2,1,0:T(8,128)}, u32[]{:S(2)}, u32[]{:S(2)}) collective-permute-start(f32[8,64,256]{2,1,0:T(8,128)} %dynamic-slice_bitcast_fusion), channel_id=1, source_target_pairs={{0,4},{4,0},{1,5},{5,1},{2,6},{6,2},{3,7},{7,3},{8,12},{12,8},{9,1... | collective-permute-start | bytes 1572872 | tf_op jit(solution)/shard_map/ppermute | solution.py:43
  128.7 0.9 add.92
  129.6 3.1 %collective-permute-start.8 = (f32[40,512]{1,0:T(8,128)S(1)}, f32[40,512]{1,0:T(8,128)S(1)}, u32[]{:S(2)}, u32[]{:S(2)}) collective-permute-start(f32[40,512]{1,0:T(8,128)S(1)} %add.92), channel_id=1, source_target_pairs={{0,64},{32,96},{64,0},{96,32},{128,192},{160,224},{192,128},{224,1... | collective-permute-start | bytes 245768 | tf_op jit(solution)/shard_map/ppermute | solution.py:332
  132.7 1.0 fusion.14
  133.7 1.7 collective-permute-done.8
  135.4 3.8 %collective-permute-start.9 = (f32[40,512]{1,0:T(8,128)S(1)}, f32[40,512]{1,0:T(8,128)S(1)}, u32[]{:S(2)}, u32[]{:S(2)}) collective-permute-start(f32[40,512]{1,0:T(8,128)S(1)} %add.93), channel_id=1, source_target_pairs={{0,192},{32,224},{64,128},{96,160},{128,64},{160,96},{192,0},{224,... | collective-permute-start | bytes 245768 | tf_op jit(solution)/shard_map/ppermute | solution.py:332
  139.3 1.3 z_messages.1
  141.3 3.4 %all-to-all-start.2 = ((f16[8,80,256]{2,1,0:T(8,128)(2,1)}), f16[8,80,256]{2,1,0:T(8,128)(2,1)S(1)}, u32[]{:S(2)}, u32[]{:S(2)}) async-start(f16[8,80,256]{2,1,0:T(8,128)(2,1)} %convert_element_type.65), calls=%async_computation.2 | async-start | bytes 655360 | tf_op jit(solution)/shard_map/all_to_all | solution.py:39
  145.2 2.1 %collective-permute-start.11 = (f16[40,512]{1,0:T(8,128)(2,1)S(1)}, f16[40,512]{1,0:T(8,128)(2,1)S(1)}, u32[]{:S(2)}, u32[]{:S(2)}) collective-permute-start(f16[40,512]{1,0:T(8,128)(2,1)S(1)} %convert_bitcast_fusion), channel_id=1, source_target_pairs={{0,2},{1,3},{2,0},{3,1},{4,6},{5,7},{6,4},{7,5},{8,10},{9,11},{10,... | collective-permute-start | bytes 122888 | tf_op jit(solution)/shard_map/ppermute | solution.py:22
  147.9 1.6 collective-permute-done.11
  149.5 1.8 %collective-permute-done.10 = f16[40,512]{1,0:T(8,128)(2,1)S(1)} collective-permute-done((f16[40,512]{1,0:T(8,128)(2,1)S(1)}, f16[40,512]{1,0:T(8,128)(2,1)S(1)}, u32[]{:S(2)}, u32[]{:S(2)}) %collective-permute-start.10) | collective-permute-done | bytes 40992 | tf_op jit(solution)/shard_map/ppermute | solution.py:22
  151.5 1.6 collective-permute-start.14
  153.1 1.1 collective-permute-start.15
  154.1 6.5 %collective-permute-start.16 = (f16[4,40,512]{2,1,0:T(8,128)(2,1)S(1)}, f16[4,40,512]{2,1,0:T(8,128)(2,1)}, u32[]{:S(2)}, u32[]{:S(2)}) collective-permute-start(f16[4,40,512]{2,1,0:T(8,128)(2,1)S(1)} %get-tuple-element.72), channel_id=1, source_target_pairs={{0,4},{4,0},{1,5},{5,1},{2,6},{6,2},{3,7},{7,3},{8,12},{12,8},{9,1... | collective-permute-start | bytes 491528 | tf_op jit(solution)/shard_map/ppermute | solution.py:43
  160.7 5.0 %collective-permute-start.17 = (f16[4,40,512]{2,1,0:T(8,128)(2,1)S(1)}, f16[4,40,512]{2,1,0:T(8,128)(2,1)}, u32[]{:S(2)}, u32[]{:S(2)}) collective-permute-start(f16[4,40,512]{2,1,0:T(8,128)(2,1)S(1)} %collective-permute-done.13), channel_id=1, source_target_pairs={{0,4},{4,0},{1,5},{5,1},{2,6},{6,2},{3,7},{7,3},{8,12},{12,8},{9,1... | collective-permute-start | bytes 491528 | tf_op jit(solution)/shard_map/ppermute | solution.py:43
  165.6 0.9 collective-permute-start.19
  167.5 0.9 convert_element_type.60.refs_4_
  168.4 0.9 convert_element_type.61.refs_5_
  169.4 0.9 convert_element_type.62.refs_6_
  170.4 0.9 convert_element_type.63.refs_7_
  171.3 2.1 %finished.1 = (f32[512,512]{1,0:T(8,128)}, f32[512,512]{1,0:T(8,128)}, f32[2,512]{1,0:T(2,128)}, f32[1,512]{1,0:T(1,128)}, f32[1,512]{1,0:T(1,128)}, /*index=5*/...) custom-call(s32[3]{0:T(128)S(1)} %pad_add_fusion.place, f32[4,40,512]{2,1,0:T(8,128)S(1)} %get-tuple-element.73.refs_0_, ...), custom_call_target="tpu_custom_call" | custom-call | tf_op jit(solution)/shard_map/finished/pallas_call | solution.py:487
  (99 shorter events, 12.0 us)
Async XLA Ops:
  0.6 1.6 copy-start
  0.7 6.6 %copy-start.3 = (bf16[256,512]{1,0:T(8,128)(2,1)S(1)}, bf16[256,512]{1,0:T(8,128)(2,1)}, u32[]{:S(2)}) copy-start(bf16[256,512]{1,0:T(8,128)(2,1)} %refs_5_.1) | copy-start | bytes 786436
  5.1 15.3 %copy-start.17 = (bf16[384,256]{1,0:T(8,128)(2,1)}, bf16[384,256]{1,0:T(8,128)(2,1)S(1)}, u32[]{:S(2)}) copy-start(bf16[384,256]{1,0:T(8,128)(2,1)S(1)} %get-tuple-element.74.refs_0_) | copy-start | bytes 589828
  5.1 7.2 %collective-permute-start = (bf16[384,256]{1,0:T(8,128)(2,1)S(1)}, bf16[384,256]{1,0:T(8,128)(2,1)S(1)}, u32[]{:S(2)}, u32[]{:S(2)}) collective-permute-start(bf16[384,256]{1,0:T(8,128)(2,1)S(1)} %get-tuple-element.74.refs_0_), channel_id=1, source_target_pairs={{0,1},{1,2},{2,3},{3,0},{4,5},{5,6},{6,7},{7,4},{8,9},{9,10},{10,1... | collective-permute-start | bytes 589832 | tf_op jit(solution)/shard_map/ppermute | solution.py:22
  7.2 23.0 %collective-permute-start.3 = (bf16[256,512]{1,0:T(8,128)(2,1)S(1)}, bf16[256,512]{1,0:T(8,128)(2,1)S(1)}, u32[]{:S(2)}, u32[]{:S(2)}) collective-permute-start(bf16[256,512]{1,0:T(8,128)(2,1)S(1)} %copy-done.3), channel_id=1, source_target_pairs={{0,1},{1,2},{2,3},{3,0},{4,5},{5,6},{6,7},{7,4},{8,9},{9,10},{10,1... | collective-permute-start | bytes 786440 | tf_op jit(solution)/shard_map/ppermute | solution.py:22
  8.5 21.8 %collective-permute-start.4 = (bf16[256,512]{1,0:T(8,128)(2,1)S(1)}, bf16[256,512]{1,0:T(8,128)(2,1)S(1)}, u32[]{:S(2)}, u32[]{:S(2)}) collective-permute-start(bf16[256,512]{1,0:T(8,128)(2,1)S(1)} %copy-done.3), channel_id=1, source_target_pairs={{0,2},{1,3},{2,0},{3,1},{4,6},{5,7},{6,4},{7,5},{8,10},{9,11},{10,... | collective-permute-start | bytes 786440 | tf_op jit(solution)/shard_map/ppermute | solution.py:22
  9.8 20.5 %collective-permute-start.5 = (bf16[256,512]{1,0:T(8,128)(2,1)S(1)}, bf16[256,512]{1,0:T(8,128)(2,1)S(1)}, u32[]{:S(2)}, u32[]{:S(2)}) collective-permute-start(bf16[256,512]{1,0:T(8,128)(2,1)S(1)} %copy-done.3), channel_id=1, source_target_pairs={{0,3},{1,0},{2,1},{3,2},{4,7},{5,4},{6,5},{7,6},{8,11},{9,8},{10,9... | collective-permute-start | bytes 786440 | tf_op jit(solution)/shard_map/ppermute | solution.py:22
  11.8 17.7 %collective-permute-start.1 = (bf16[384,256]{1,0:T(8,128)(2,1)S(1)}, bf16[384,256]{1,0:T(8,128)(2,1)S(1)}, u32[]{:S(2)}, u32[]{:S(2)}) collective-permute-start(bf16[384,256]{1,0:T(8,128)(2,1)S(1)} %get-tuple-element.74.refs_0_), channel_id=1, source_target_pairs={{0,2},{1,3},{2,0},{3,1},{4,6},{5,7},{6,4},{7,5},{8,10},{9,11},{10,... | collective-permute-start | bytes 589832 | tf_op jit(solution)/shard_map/ppermute | solution.py:22
  12.3 8.1 %copy-start.18 = (bf16[384,256]{1,0:T(8,128)(2,1)}, bf16[384,256]{1,0:T(8,128)(2,1)S(1)}, u32[]{:S(2)}) copy-start(bf16[384,256]{1,0:T(8,128)(2,1)S(1)} %collective-permute-done.refs_1_) | copy-start | bytes 589828
  12.3 18.0 %collective-permute-start.2 = (bf16[384,256]{1,0:T(8,128)(2,1)S(1)}, bf16[384,256]{1,0:T(8,128)(2,1)}, u32[]{:S(2)}, u32[]{:S(2)}) collective-permute-start(bf16[384,256]{1,0:T(8,128)(2,1)S(1)} %get-tuple-element.74.refs_0_), channel_id=1, source_target_pairs={{0,3},{1,0},{2,1},{3,2},{4,7},{5,4},{6,5},{7,6},{8,11},{9,8},{10,9... | collective-permute-start | bytes 589832 | tf_op jit(solution)/shard_map/ppermute | solution.py:22
  29.5 0.9 copy-start.19
  30.3 0.7 copy-start.14
  30.3 0.8 copy-start.15
  30.3 0.9 copy-start.16
  36.9 16.3 %all-to-all-start = ((f32[4,96,512]{2,1,0:T(8,128)}), f32[4,96,512]{2,1,0:T(8,128)S(1)}, u32[]{:S(2)}, u32[]{:S(2)}) async-start(f32[4,96,512]{2,1,0:T(8,128)} %bitcast.75), calls=%async_computation | async-start | bytes 1572864 | tf_op jit(solution)/shard_map/all_to_all | solution.py:39
  48.2 34.8 %collective-permute-start.27 = (bf16[1024,384]{1,0:T(8,128)(2,1)}, bf16[1024,384]{1,0:T(8,128)(2,1)}, u32[]{:S(2)}, u32[]{:S(2)}) collective-permute-start(bf16[1024,384]{1,0:T(8,128)(2,1)} %get-tuple-element.54), channel_id=1, source_target_pairs={{0,24},{8,0},{16,8},{24,16},{1,25},{9,1},{17,9},{25,17},{2,26},{10... | collective-permute-start | bytes 2359304 | tf_op jit(solution)/shard_map/ppermute | solution.py:22
  51.0 44.2 %collective-permute-start.25 = (bf16[1024,384]{1,0:T(8,128)(2,1)}, bf16[1024,384]{1,0:T(8,128)(2,1)}, u32[]{:S(2)}, u32[]{:S(2)}) collective-permute-start(bf16[1024,384]{1,0:T(8,128)(2,1)} %get-tuple-element.53), channel_id=1, source_target_pairs={{0,16},{8,24},{16,0},{24,8},{1,17},{9,25},{17,1},{25,9},{2,18},{10... | collective-permute-start | bytes 2359304 | tf_op jit(solution)/shard_map/ppermute | solution.py:22
  53.9 14.6 %collective-permute-start.20 = (bf16[96,512]{1,0:T(8,128)(2,1)}, bf16[96,512]{1,0:T(8,128)(2,1)S(1)}, u32[]{:S(2)}, u32[]{:S(2)}) collective-permute-start(bf16[96,512]{1,0:T(8,128)(2,1)} %get-tuple-element.67.refs_0_), channel_id=1, source_target_pairs={{0,1},{1,2},{2,3},{3,0},{4,5},{5,6},{6,7},{7,4},{8,9},{9,10},{10,1... | collective-permute-start | bytes 294920 | tf_op jit(solution)/shard_map/ppermute | solution.py:22
  54.2 17.5 %collective-permute-start.21 = (bf16[96,512]{1,0:T(8,128)(2,1)}, bf16[96,512]{1,0:T(8,128)(2,1)S(1)}, u32[]{:S(2)}, u32[]{:S(2)}) collective-permute-start(bf16[96,512]{1,0:T(8,128)(2,1)} %get-tuple-element.67.refs_0_), channel_id=1, source_target_pairs={{0,2},{1,3},{2,0},{3,1},{4,6},{5,7},{6,4},{7,5},{8,10},{9,11},{10,... | collective-permute-start | bytes 294920 | tf_op jit(solution)/shard_map/ppermute | solution.py:22
  56.0 17.1 %collective-permute-start.22 = (bf16[96,512]{1,0:T(8,128)(2,1)}, bf16[96,512]{1,0:T(8,128)(2,1)}, u32[]{:S(2)}, u32[]{:S(2)}) collective-permute-start(bf16[96,512]{1,0:T(8,128)(2,1)} %get-tuple-element.67.refs_0_), channel_id=1, source_target_pairs={{0,3},{1,0},{2,1},{3,2},{4,7},{5,4},{6,5},{7,6},{8,11},{9,8},{10,9... | collective-permute-start | bytes 294920 | tf_op jit(solution)/shard_map/ppermute | solution.py:22
  68.5 0.6 copy-start.5
  69.2 35.6 %collective-permute-start.6 = (f32[520,512]{1,0:T(8,128)}, f32[520,512]{1,0:T(8,128)S(1)}, u32[]{:S(2)}, u32[]{:S(2)}) collective-permute-start(f32[520,512]{1,0:T(8,128)} %get-tuple-element.45), channel_id=1, source_target_pairs={{0,4},{4,0},{1,5},{5,1},{2,6},{6,2},{3,7},{7,3},{8,12},{12,8},{9,1... | collective-permute-start | bytes 3194888 | tf_op jit(solution)/shard_map/ppermute | solution.py:43
  71.7 0.6 copy-start.7
  72.4 27.8 %collective-permute-start.23 = (bf16[1024,384]{1,0:T(8,128)(2,1)}, bf16[1024,384]{1,0:T(8,128)(2,1)}, u32[]{:S(2)}, u32[]{:S(2)}) collective-permute-start(bf16[1024,384]{1,0:T(8,128)(2,1)} %get-tuple-element.52), channel_id=1, source_target_pairs={{0,8},{8,16},{16,24},{24,0},{1,9},{9,17},{17,25},{25,1},{2,10},{10... | collective-permute-start | bytes 2359304 | tf_op jit(solution)/shard_map/ppermute | solution.py:22
  73.1 1.0 copy-start.4
  74.0 0.9 copy-start.6
  74.9 0.9 copy-start.8
  77.9 0.8 copy-start.2
  78.7 0.6 copy-start.11
  79.2 9.5 %collective-permute-start.28 = (bf16[384,256]{1,0:T(8,128)(2,1)}, bf16[384,256]{1,0:T(8,128)(2,1)}, u32[]{:S(2)}, u32[]{:S(2)}) collective-permute-start(bf16[384,256]{1,0:T(8,128)(2,1)} %get-tuple-element.51), channel_id=1, source_target_pairs={{0,24},{8,0},{16,8},{24,16},{1,25},{9,1},{17,9},{25,17},{2,26},{10... | collective-permute-start | bytes 589832 | tf_op jit(solution)/shard_map/ppermute | solution.py:22
  82.3 10.3 %copy-start.12 = (f32[8,4,2,8,256]{4,3,1,0,2:T(8,128)}, f32[8,4,2,8,256]{4,3,1,0,2:T(8,128)S(1)}, u32[]{:S(2)}) copy-start(f32[8,4,2,8,256]{4,3,1,0,2:T(8,128)S(1)} %copy.27) | copy-start | bytes 1572868
  83.1 14.6 %collective-permute-start.26 = (bf16[384,256]{1,0:T(8,128)(2,1)}, bf16[384,256]{1,0:T(8,128)(2,1)S(1)}, u32[]{:S(2)}, u32[]{:S(2)}) collective-permute-start(bf16[384,256]{1,0:T(8,128)(2,1)} %get-tuple-element.51), channel_id=1, source_target_pairs={{0,16},{8,24},{16,0},{24,8},{1,17},{9,25},{17,1},{25,9},{2,18},{10... | collective-permute-start | bytes 589832 | tf_op jit(solution)/shard_map/ppermute | solution.py:22
  88.7 13.5 %collective-permute-start.24 = (bf16[384,256]{1,0:T(8,128)(2,1)}, bf16[384,256]{1,0:T(8,128)(2,1)S(1)}, u32[]{:S(2)}, u32[]{:S(2)}) collective-permute-start(bf16[384,256]{1,0:T(8,128)(2,1)} %get-tuple-element.51), channel_id=1, source_target_pairs={{0,8},{8,16},{16,24},{24,0},{1,9},{9,17},{17,25},{25,1},{2,10},{10... | collective-permute-start | bytes 589832 | tf_op jit(solution)/shard_map/ppermute | solution.py:22
  95.2 9.6 %copy-start.1 = (f32[520,512]{1,0:T(8,128)S(1)}, f32[520,512]{1,0:T(8,128)}, u32[]{:S(2)}) copy-start(f32[520,512]{1,0:T(8,128)} %get-tuple-element.44.mine) | copy-start | bytes 3194884
  95.2 9.6 %copy-start.9 = (f32[512]{0:T(512)S(1)}, f32[512]{0:T(512)}, u32[]{:S(2)}) copy-start(f32[512]{0:T(512)} %get-tuple-element.68) | copy-start | bytes 6148
  95.2 9.6 %copy-start.10 = (f32[1,512]{1,0:T(1,128)S(1)}, f32[1,512]{1,0:T(1,128)}, u32[]{:S(2)}) copy-start(f32[1,512]{1,0:T(1,128)} %get-tuple-element.47.squares) | copy-start | bytes 6148
  95.2 17.9 %collective-permute-start.30 = (f32[264,256]{1,0:T(8,128)S(1)}, f32[264,256]{1,0:T(8,128)}, u32[]{:S(2)}, u32[]{:S(2)}) collective-permute-start(f32[264,256]{1,0:T(8,128)S(1)} %fusion.4), channel_id=1, source_target_pairs={{0,4},{4,0},{1,5},{5,1},{2,6},{6,2},{3,7},{7,3},{8,12},{12,8},{9,1... | collective-permute-start | bytes 811016 | tf_op jit(solution)/shard_map/ppermute | solution.py:22
  106.1 16.6 %all-to-all-start.1 = ((f16[16,40,512]{2,1,0:T(8,128)(2,1)}), f16[16,40,512]{2,1,0:T(8,128)(2,1)}, u32[]{:S(2)}, u32[]{:S(2)}) async-start(f16[16,40,512]{2,1,0:T(8,128)(2,1)} %convert_element_type.52), calls=%async_computation.1 | async-start | bytes 1310720 | tf_op jit(solution)/shard_map/all_to_all | solution.py:39
  110.4 2.7 %copy-start.13 = (f32[8,4,2,8,256]{4,3,1,0,2:T(8,128)S(1)}, f32[8,4,2,8,256]{4,3,1,0,2:T(8,128)}, u32[]{:S(2)}) copy-start(f32[8,4,2,8,256]{4,3,1,0,2:T(8,128)} %copy-done.12) | copy-start | bytes 1572868
  114.9 17.8 %collective-permute-start.33 = (f32[72,256]{1,0:T(8,128)}, f32[72,256]{1,0:T(8,128)}, u32[]{:S(2)}, u32[]{:S(2)}) collective-permute-start(f32[72,256]{1,0:T(8,128)} %get-tuple-element.71), channel_id=1, source_target_pairs={{0,24},{8,0},{16,8},{24,16},{1,25},{9,1},{17,9},{25,17},{2,26},{10... | collective-permute-start | bytes 221192 | tf_op jit(solution)/shard_map/ppermute | solution.py:22
  117.4 15.3 %collective-permute-start.32 = (f32[72,256]{1,0:T(8,128)}, f32[72,256]{1,0:T(8,128)}, u32[]{:S(2)}, u32[]{:S(2)}) collective-permute-start(f32[72,256]{1,0:T(8,128)} %get-tuple-element.70), channel_id=1, source_target_pairs={{0,16},{8,24},{16,0},{24,8},{1,17},{9,25},{17,1},{25,9},{2,18},{10... | collective-permute-start | bytes 221192 | tf_op jit(solution)/shard_map/ppermute | solution.py:22
  118.0 14.7 %collective-permute-start.31 = (f32[72,256]{1,0:T(8,128)}, f32[72,256]{1,0:T(8,128)}, u32[]{:S(2)}, u32[]{:S(2)}) collective-permute-start(f32[72,256]{1,0:T(8,128)} %get-tuple-element.69), channel_id=1, source_target_pairs={{0,8},{8,16},{16,24},{24,0},{1,9},{9,17},{17,25},{25,1},{2,10},{10... | collective-permute-start | bytes 221192 | tf_op jit(solution)/shard_map/ppermute | solution.py:22
  124.1 4.6 %collective-permute-start.7 = (f32[40,512]{1,0:T(8,128)S(1)}, f32[40,512]{1,0:T(8,128)}, u32[]{:S(2)}, u32[]{:S(2)}) collective-permute-start(f32[40,512]{1,0:T(8,128)S(1)} %plane_total.1), channel_id=1, source_target_pairs={{0,32},{32,0},{64,96},{96,64},{128,160},{160,128},{192,224},{224,1... | collective-permute-start | bytes 245768 | tf_op jit(solution)/shard_map/ppermute | solution.py:332
  126.7 12.6 %collective-permute-start.29 = (f32[8,64,256]{2,1,0:T(8,128)}, f32[8,64,256]{2,1,0:T(8,128)}, u32[]{:S(2)}, u32[]{:S(2)}) collective-permute-start(f32[8,64,256]{2,1,0:T(8,128)} %dynamic-slice_bitcast_fusion), channel_id=1, source_target_pairs={{0,4},{4,0},{1,5},{5,1},{2,6},{6,2},{3,7},{7,3},{8,12},{12,8},{9,1... | collective-permute-start | bytes 1572872 | tf_op jit(solution)/shard_map/ppermute | solution.py:43
  129.6 5.8 %collective-permute-start.8 = (f32[40,512]{1,0:T(8,128)S(1)}, f32[40,512]{1,0:T(8,128)S(1)}, u32[]{:S(2)}, u32[]{:S(2)}) collective-permute-start(f32[40,512]{1,0:T(8,128)S(1)} %add.92), channel_id=1, source_target_pairs={{0,64},{32,96},{64,0},{96,32},{128,192},{160,224},{192,128},{224,1... | collective-permute-start | bytes 245768 | tf_op jit(solution)/shard_map/ppermute | solution.py:332
  135.4 9.3 %collective-permute-start.9 = (f32[40,512]{1,0:T(8,128)S(1)}, f32[40,512]{1,0:T(8,128)S(1)}, u32[]{:S(2)}, u32[]{:S(2)}) collective-permute-start(f32[40,512]{1,0:T(8,128)S(1)} %add.93), channel_id=1, source_target_pairs={{0,192},{32,224},{64,128},{96,160},{128,64},{160,96},{192,0},{224,... | collective-permute-start | bytes 245768 | tf_op jit(solution)/shard_map/ppermute | solution.py:332
  141.3 25.3 %all-to-all-start.2 = ((f16[8,80,256]{2,1,0:T(8,128)(2,1)}), f16[8,80,256]{2,1,0:T(8,128)(2,1)S(1)}, u32[]{:S(2)}, u32[]{:S(2)}) async-start(f16[8,80,256]{2,1,0:T(8,128)(2,1)} %convert_element_type.65), calls=%async_computation.2 | async-start | bytes 655360 | tf_op jit(solution)/shard_map/all_to_all | solution.py:39
  145.0 2.9 %collective-permute-start.12 = (f16[40,512]{1,0:T(8,128)(2,1)S(1)}, f16[40,512]{1,0:T(8,128)(2,1)S(1)}, u32[]{:S(2)}, u32[]{:S(2)}) collective-permute-start(f16[40,512]{1,0:T(8,128)(2,1)S(1)} %convert_bitcast_fusion), channel_id=1, source_target_pairs={{0,3},{1,0},{2,1},{3,2},{4,7},{5,4},{6,5},{7,6},{8,11},{9,8},{10,9... | collective-permute-start | bytes 122888 | tf_op jit(solution)/shard_map/ppermute | solution.py:22
  145.2 4.4 %collective-permute-start.11 = (f16[40,512]{1,0:T(8,128)(2,1)S(1)}, f16[40,512]{1,0:T(8,128)(2,1)S(1)}, u32[]{:S(2)}, u32[]{:S(2)}) collective-permute-start(f16[40,512]{1,0:T(8,128)(2,1)S(1)} %convert_bitcast_fusion), channel_id=1, source_target_pairs={{0,2},{1,3},{2,0},{3,1},{4,6},{5,7},{6,4},{7,5},{8,10},{9,11},{10,... | collective-permute-start | bytes 122888 | tf_op jit(solution)/shard_map/ppermute | solution.py:22
  147.3 4.1 %collective-permute-start.10 = (f16[40,512]{1,0:T(8,128)(2,1)S(1)}, f16[40,512]{1,0:T(8,128)(2,1)S(1)}, u32[]{:S(2)}, u32[]{:S(2)}) collective-permute-start(f16[40,512]{1,0:T(8,128)(2,1)S(1)} %convert_bitcast_fusion), channel_id=1, source_target_pairs={{0,1},{1,2},{2,3},{3,0},{4,5},{5,6},{6,7},{7,4},{8,9},{9,10},{10,1... | collective-permute-start | bytes 122888 | tf_op jit(solution)/shard_map/ppermute | solution.py:22
  151.4 9.3 %collective-permute-start.13 = (f16[4,40,512]{2,1,0:T(8,128)(2,1)S(1)}, f16[4,40,512]{2,1,0:T(8,128)(2,1)S(1)}, u32[]{:S(2)}, u32[]{:S(2)}) collective-permute-start(f16[4,40,512]{2,1,0:T(8,128)(2,1)S(1)} %get-tuple-element.72), channel_id=1, source_target_pairs={{0,8},{8,16},{16,24},{24,0},{1,9},{9,17},{17,25},{25,1},{2,10},{10... | collective-permute-start | bytes 491528 | tf_op jit(solution)/shard_map/ppermute | solution.py:22
  151.5 14.2 %collective-permute-start.14 = (f16[4,40,512]{2,1,0:T(8,128)(2,1)S(1)}, f16[4,40,512]{2,1,0:T(8,128)(2,1)S(1)}, u32[]{:S(2)}, u32[]{:S(2)}) collective-permute-start(f16[4,40,512]{2,1,0:T(8,128)(2,1)S(1)} %get-tuple-element.72), channel_id=1, source_target_pairs={{0,16},{8,24},{16,0},{24,8},{1,17},{9,25},{17,1},{25,9},{2,18},{10... | collective-permute-start | bytes 491528 | tf_op jit(solution)/shard_map/ppermute | solution.py:22
  153.1 12.6 %collective-permute-start.15 = (f16[4,40,512]{2,1,0:T(8,128)(2,1)S(1)}, f16[4,40,512]{2,1,0:T(8,128)(2,1)S(1)}, u32[]{:S(2)}, u32[]{:S(2)}) collective-permute-start(f16[4,40,512]{2,1,0:T(8,128)(2,1)S(1)} %get-tuple-element.72), channel_id=1, source_target_pairs={{0,24},{8,0},{16,8},{24,16},{1,25},{9,1},{17,9},{25,17},{2,26},{10... | collective-permute-start | bytes 491528 | tf_op jit(solution)/shard_map/ppermute | solution.py:22
  154.1 13.3 %collective-permute-start.16 = (f16[4,40,512]{2,1,0:T(8,128)(2,1)S(1)}, f16[4,40,512]{2,1,0:T(8,128)(2,1)}, u32[]{:S(2)}, u32[]{:S(2)}) collective-permute-start(f16[4,40,512]{2,1,0:T(8,128)(2,1)S(1)} %get-tuple-element.72), channel_id=1, source_target_pairs={{0,4},{4,0},{1,5},{5,1},{2,6},{6,2},{3,7},{7,3},{8,12},{12,8},{9,1... | collective-permute-start | bytes 491528 | tf_op jit(solution)/shard_map/ppermute | solution.py:43
  160.7 7.8 %collective-permute-start.17 = (f16[4,40,512]{2,1,0:T(8,128)(2,1)S(1)}, f16[4,40,512]{2,1,0:T(8,128)(2,1)}, u32[]{:S(2)}, u32[]{:S(2)}) collective-permute-start(f16[4,40,512]{2,1,0:T(8,128)(2,1)S(1)} %collective-permute-done.13), channel_id=1, source_target_pairs={{0,4},{4,0},{1,5},{5,1},{2,6},{6,2},{3,7},{7,3},{8,12},{12,8},{9,1... | collective-permute-start | bytes 491528 | tf_op jit(solution)/shard_map/ppermute | solution.py:43
  165.6 3.8 %collective-permute-start.18 = (f16[4,40,512]{2,1,0:T(8,128)(2,1)S(1)}, f16[4,40,512]{2,1,0:T(8,128)(2,1)}, u32[]{:S(2)}, u32[]{:S(2)}) collective-permute-start(f16[4,40,512]{2,1,0:T(8,128)(2,1)S(1)} %collective-permute-done.14), channel_id=1, source_target_pairs={{0,4},{4,0},{1,5},{5,1},{2,6},{6,2},{3,7},{7,3},{8,12},{12,8},{9,1... | collective-permute-start | bytes 491528 | tf_op jit(solution)/shard_map/ppermute | solution.py:43
  165.6 4.7 %collective-permute-start.19 = (f16[4,40,512]{2,1,0:T(8,128)(2,1)S(1)}, f16[4,40,512]{2,1,0:T(8,128)(2,1)}, u32[]{:S(2)}, u32[]{:S(2)}) collective-permute-start(f16[4,40,512]{2,1,0:T(8,128)(2,1)S(1)} %collective-permute-done.15), channel_id=1, source_target_pairs={{0,4},{4,0},{1,5},{5,1},{2,6},{6,2},{3,7},{7,3},{8,12},{12,8},{9,1... | collective-permute-start | bytes 491528 | tf_op jit(solution)/shard_map/ppermute | solution.py:43

commit v3 on v2

--- a/solution.py
+++ b/solution.py
@@ -219,26 +219,24 @@
 def columns_by_y(sensors, iy, nz, ny, width):
     funcs = sensors.shape[0]
 
-    def body(y, *refs):
-        for src, dst in zip(refs[:ny], refs[ny:]):
-            dst[...] = src[...].T
-
-    def source(k):
-        return pl.BlockSpec((funcs, width), lambda z, y: (0, z * ny + lax.rem(y[0] + k, ny)))
+    def body(y, src, *out):
+        for k, dst in enumerate(out):
+            at = lax.rem(y[0] + k, ny) * width
+            dst[...] = src[:, pl.ds(pl.multiple_of(at, width), width)].T
 
     return pl.pallas_call(
         body,
         grid_spec=pltpu.PrefetchScalarGridSpec(
             num_scalar_prefetch=1,
             grid=(nz,),
-            in_specs=[source(k) for k in range(ny)],
+            in_specs=[pl.BlockSpec((funcs, ny * width), lambda z, y: (0, z))],
             out_specs=[pl.BlockSpec((width, funcs), lambda z, y: (z, 0))] * ny,
         ),
         out_shape=[jax.ShapeDtypeStruct((nz * width, funcs), sensors.dtype)] * ny,
         cost_estimate=pl.CostEstimate(flops=8_000_000, bytes_accessed=4 * sensors.size, transcendentals=0),
         compiler_params=pltpu.CompilerParams(vmem_limit_bytes=60 * 2**20),
         name="columns_by_y",
-    )(iy.reshape(1), *[sensors] * ny)
+    )(iy.reshape(1), sensors)
 
 
 def back_kernel(core, index, misfit, coeffs, first_act, second_act, v_two, v_three, mine, give, acc3, acc2, accs, *, inv_scale):

time: 176 us -> 176 us (level)
  no operation moved by 1% of the time
where the time goes in v3:
time: 176 us; the launch traced here: 175 us
  starting transfers between devices  71 us (40%)
  Pallas kernels  36.3 us (21%)
  waiting for transfers between devices  29.9 us (17%)
  matrix products  13.2 us (8%)
  other arithmetic  11.4 us (6%)
  local copies, waits for them, and re-layouts  10.5 us (6%)
  between operations  2.86 us (2%)
    ppermute x25, starting transfers between devices, shift(): return lax.ppermute(x, axis, [(i, (i + k) % n) for i in range(n)])  32.9 us
    ppermute x25, waiting for transfers between devices, shift(): return lax.ppermute(x, axis, [(i, (i + k) % n) for i in range(n)])  21.9 us
    ppermute x6, starting transfers between devices, other_core(): return lax.ppermute(x, 'c', [(0, 1), (1, 0)])  17 us
    all_to_all x3, starting transfers between devices, exchanged(): return lax.all_to_all(x, axis, 0, 0, tiled=True)  12.6 us
    pallas_call x1, Pallas kernels, trunk_backward(): pl.pallas_call(functools.partial(back_kernel, inv_scale=inv_scale), grid_...  11.5 us
    ppermute x3, starting transfers between devices, summed_in_pairs(): x = x + lax.ppermute(x, axis, [(i, i ^ pair) for i in range(n)])  8.6 us
    unnamed x40, local copies, waits for them, and re-layouts  7.81 us
    dot_general x3, matrix products, local(): jnp.dot(sens_y[k], pre_y[k], preferred_element_type=jnp.float32)  7.65 us
  transfers between devices with their start and end apart: 37, of which 11 were waited for; matrix products, arithmetic and copies ran while one was open for 13% of the time, Pallas kernels for 16%

profile of v3, /device:TPU:1, one launch (start us, length us, event | category | flops | bytes accessed | tf_op | source)
XLA Modules:
  0.0 175.2 jit_solution(9904246182853446917)
XLA Ops:
  0.7 1.6 copy-done
  2.2 2.9 %fusion.21 = (bf16[384,256]{1,0:T(8,128)(2,1)S(1)}, f32[384,256]{1,0:T(8,128)S(1)}) fusion(f32[256]{0:T(256)} %param.17, bf16[384,4096]{1,0:T(8,128)(2,1)} %src, bf16[4096,256]{1,0:T(8,128)(2,1)S(1)} %copy-done), kind=kOutput, calls=%fused_computation.40 | convolution fusion | flops 805502976 | bytes 5833728 | tf_op jit(solution)/shard_map/dot_general | solution.py:571
  5.1 2.1 %collective-permute-start = (bf16[384,256]{1,0:T(8,128)(2,1)S(1)}, bf16[384,256]{1,0:T(8,128)(2,1)S(1)}, u32[]{:S(2)}, u32[]{:S(2)}) collective-permute-start(bf16[384,256]{1,0:T(8,128)(2,1)S(1)} %get-tuple-element.74.refs_0_), channel_id=1, source_target_pairs={{0,1},{1,2},{2,3},{3,0},{4,5},{5,6},{6,7},{7,4},{8,9},{9,10},{10,1... | collective-permute-start | bytes 589832 | tf_op jit(solution)/shard_map/ppermute | solution.py:22
  7.2 1.2 collective-permute-start.3
  8.5 1.3 collective-permute-start.4
  9.8 2.0 %collective-permute-start.5 = (bf16[256,512]{1,0:T(8,128)(2,1)S(1)}, bf16[256,512]{1,0:T(8,128)(2,1)S(1)}, u32[]{:S(2)}, u32[]{:S(2)}) collective-permute-start(bf16[256,512]{1,0:T(8,128)(2,1)S(1)} %copy-done.3), channel_id=1, source_target_pairs={{0,3},{1,0},{2,1},{3,2},{4,7},{5,4},{6,5},{7,6},{8,11},{9,8},{10,9... | collective-permute-start | bytes 786440 | tf_op jit(solution)/shard_map/ppermute | solution.py:22
  12.3 2.0 %collective-permute-start.2 = (bf16[384,256]{1,0:T(8,128)(2,1)S(1)}, bf16[384,256]{1,0:T(8,128)(2,1)}, u32[]{:S(2)}, u32[]{:S(2)}) collective-permute-start(bf16[384,256]{1,0:T(8,128)(2,1)S(1)} %get-tuple-element.74.refs_0_), channel_id=1, source_target_pairs={{0,3},{1,0},{2,1},{3,2},{4,7},{5,4},{6,5},{7,6},{8,11},{9,8},{10,9... | collective-permute-start | bytes 589832 | tf_op jit(solution)/shard_map/ppermute | solution.py:22
  14.3 6.1 %trunk_forward.1 = (bf16[2048,512]{1,0:T(8,128)(2,1)}, f32[2048,512]{1,0:T(8,128)}, f32[2048,512]{1,0:T(8,128)}) custom-call(s32[2,2048]{1,0:T(2,128)} %index.3, f32[2,512]{1,0:T(2,128)} %v_one.1, f32[1,512]{1,0:T(1,128)} %bitcast.80, bf16[512,512]{1,0:T(8,128)(2,1)} %v_two.3, f32[1,512]{1,0:T(1,128)} %bitcast.81, bf16[512,512]{1,0:T(8,128)(2,1)} %v_three.3, ...), custom_call_target="tpu_custom_call" | custom-call | flops 2147483648 | bytes 4000000 | tf_op jit(solution)/shard_map/trunk_forward/pallas_call | solution.py:100
  20.4 9.0 %collective-permute-done.1.refs_2_ = bf16[384,256]{1,0:T(8,128)(2,1)S(1)} collective-permute-done((bf16[384,256]{1,0:T(8,128)(2,1)S(1)}, bf16[384,256]{1,0:T(8,128)(2,1)S(1)}, u32[]{:S(2)}, u32[]{:S(2)}) %collective-permute-start.1) | collective-permute-done | bytes 196640 | tf_op jit(solution)/shard_map/ppermute | solution.py:22
  29.5 0.8 collective-permute-done.2.refs_3_
  31.2 5.7 %misfit_of.1 = (bf16[384,512]{1,0:T(8,128)(2,1)}, bf16[384,2048]{1,0:T(8,128)(2,1)}, f32[1,512]{1,0:T(1,128)}, f32[384,512]{1,0:T(8,128)}) custom-call(bf16[384,256]{1,0:T(8,128)(2,1)} %copy-done.17, bf16[384,256]{1,0:T(8,128)(2,1)} %copy-done.18, bf16[384,256]{1,0:T(8,128)(2,1)} %copy-done.19, bf16[384,256]{1,0:T(8,128)(2,1)} %collective-permute-done.2.refs_3_, ...), custom_call_target="tpu_custom_call" | custom-call | flops 2013265920 | bytes 8000000 | tf_op jit(solution)/shard_map/misfit_of/pallas_call | solution.py:155
  36.9 4.8 %all-to-all-start = ((f32[4,96,512]{2,1,0:T(8,128)}), f32[4,96,512]{2,1,0:T(8,128)S(1)}, u32[]{:S(2)}, u32[]{:S(2)}) async-start(f32[4,96,512]{2,1,0:T(8,128)} %bitcast.75), calls=%async_computation | async-start | bytes 1572864 | tf_op jit(solution)/shard_map/all_to_all | solution.py:39
  41.7 6.3 %columns_by_y.1 = (bf16[1024,384]{1,0:T(8,128)(2,1)}, bf16[1024,384]{1,0:T(8,128)(2,1)}, bf16[1024,384]{1,0:T(8,128)(2,1)}, bf16[1024,384]{1,0:T(8,128)(2,1)}) custom-call(s32[1]{0:T(128)} %bitcast.1.y, bf16[384,4096]{1,0:T(8,128)(2,1)} %src), custom_call_target="tpu_custom_call" | custom-call | flops 8000000 | bytes 6291456 | tf_op jit(solution)/shard_map/columns_by_y/pallas_call | solution.py:227
  48.0 2.7 %collective-permute-start.27 = (bf16[1024,384]{1,0:T(8,128)(2,1)}, bf16[1024,384]{1,0:T(8,128)(2,1)}, u32[]{:S(2)}, u32[]{:S(2)}) collective-permute-start(bf16[1024,384]{1,0:T(8,128)(2,1)} %get-tuple-element.54), channel_id=1, source_target_pairs={{0,24},{8,0},{16,8},{24,16},{1,25},{9,1},{17,9},{25,17},{2,26},{10... | collective-permute-start | bytes 2359304 | tf_op jit(solution)/shard_map/ppermute | solution.py:22
  51.1 2.1 %all-to-all-done = f32[4,96,512]{2,1,0:T(8,128)S(1)} async-done(((f32[4,96,512]{2,1,0:T(8,128)}), f32[4,96,512]{2,1,0:T(8,128)S(1)}, u32[]{:S(2)}, u32[]{:S(2)}) %all-to-all-start) | async-done | bytes 786464 | tf_op jit(solution)/shard_map/all_to_all | solution.py:39
  54.2 1.8 %collective-permute-start.21 = (bf16[96,512]{1,0:T(8,128)(2,1)}, bf16[96,512]{1,0:T(8,128)(2,1)S(1)}, u32[]{:S(2)}, u32[]{:S(2)}) collective-permute-start(bf16[96,512]{1,0:T(8,128)(2,1)} %get-tuple-element.67.refs_0_), channel_id=1, source_target_pairs={{0,2},{1,3},{2,0},{3,1},{4,6},{5,7},{6,4},{7,5},{8,10},{9,11},{10,... | collective-permute-start | bytes 294920 | tf_op jit(solution)/shard_map/ppermute | solution.py:22
  56.0 0.9 collective-permute-start.22
  56.9 11.5 %trunk_backward.1 = (f32[520,512]{1,0:T(8,128)}, f32[520,512]{1,0:T(8,128)}) custom-call(s32[1]{0:T(128)} %bitcast.core, s32[2,2048]{1,0:T(2,128)} %index.3, bf16[384,2048]{1,0:T(8,128)(2,1)} %get-tuple-element.40.misfit, bf16[384,512]{1,0:T(8,128)(2,1)} %get-tuple-element.41.coeffs, f32[2048,512]{1,0:T(8,128)} %get-tuple-element.42.first_act, ...), custom_call_target="tpu_custom_call" | custom-call | flops 6442450944 | bytes 8000000 | tf_op jit(solution)/shard_map/trunk_backward/pallas_call | solution.py:292
  69.0 2.6 %collective-permute-start.6 = (f32[520,512]{1,0:T(8,128)}, f32[520,512]{1,0:T(8,128)S(1)}, u32[]{:S(2)}, u32[]{:S(2)}) collective-permute-start(f32[520,512]{1,0:T(8,128)} %get-tuple-element.45), channel_id=1, source_target_pairs={{0,4},{4,0},{1,5},{5,1},{2,6},{6,2},{3,7},{7,3},{8,12},{12,8},{9,1... | collective-permute-start | bytes 3194888 | tf_op jit(solution)/shard_map/ppermute | solution.py:43
  73.0 0.9 copy-done.4
  73.9 0.9 copy-done.6
  74.8 0.9 copy-done.8
  75.7 2.1 %pre_of.1 = (bf16[384,256]{1,0:T(8,128)(2,1)}, f32[1,256]{1,0:T(1,128)S(1)}, f32[512,256]{1,0:T(8,128)S(1)}) custom-call(s32[1]{0:T(128)} %bitcast.2.ix, bf16[96,512]{1,0:T(8,128)(2,1)} %get-tuple-element.67.refs_0_, bf16[96,512]{1,0:T(8,128)(2,1)S(1)} %copy-done.6, bf16[96,512]{1,0:T(8,128)(2,1)S(1)} %copy-done.8, ...), custom_call_target="tpu_custom_call" | custom-call | flops 201326592 | bytes 2000000 | tf_op jit(solution)/shard_map/pre_of/pallas_call | solution.py:199
  79.1 1.9 %collective-permute-start.28 = (bf16[384,256]{1,0:T(8,128)(2,1)}, bf16[384,256]{1,0:T(8,128)(2,1)}, u32[]{:S(2)}, u32[]{:S(2)}) collective-permute-start(bf16[384,256]{1,0:T(8,128)(2,1)} %get-tuple-element.51), channel_id=1, source_target_pairs={{0,24},{8,0},{16,8},{24,16},{1,25},{9,1},{17,9},{25,17},{2,26},{10... | collective-permute-start | bytes 589832 | tf_op jit(solution)/shard_map/ppermute | solution.py:22
  81.0 1.1 copy.27
  82.9 1.5 collective-permute-start.26
  84.3 4.2 %collective-permute-done.28 = bf16[384,256]{1,0:T(8,128)(2,1)} collective-permute-done((bf16[384,256]{1,0:T(8,128)(2,1)}, bf16[384,256]{1,0:T(8,128)(2,1)}, u32[]{:S(2)}, u32[]{:S(2)}) %collective-permute-start.28) | collective-permute-done | bytes 196640 | tf_op jit(solution)/shard_map/ppermute | solution.py:22
  88.5 3.9 %collective-permute-start.24 = (bf16[384,256]{1,0:T(8,128)(2,1)}, bf16[384,256]{1,0:T(8,128)(2,1)S(1)}, u32[]{:S(2)}, u32[]{:S(2)}) collective-permute-start(bf16[384,256]{1,0:T(8,128)(2,1)} %get-tuple-element.51), channel_id=1, source_target_pairs={{0,8},{8,16},{16,24},{24,0},{1,9},{9,17},{17,25},{25,1},{2,10},{10... | collective-permute-start | bytes 589832 | tf_op jit(solution)/shard_map/ppermute | solution.py:22
  92.4 2.6 %fusion.24 = f32[1024,256]{1,0:T(8,128)} fusion(bf16[1024,384]{1,0:T(8,128)(2,1)} %collective-permute-done.27, bf16[384,256]{1,0:T(8,128)(2,1)} %collective-permute-done.28), kind=kOutput, calls=%fused_computation.43 | convolution fusion | flops 201326592 | bytes 2031616 | tf_op jit(solution)/shard_map/dot_general | solution.py:618
  95.0 0.9 collective-permute-start.30
  95.9 1.8 %collective-permute-done.26 = bf16[384,256]{1,0:T(8,128)(2,1)S(1)} collective-permute-done((bf16[384,256]{1,0:T(8,128)(2,1)}, bf16[384,256]{1,0:T(8,128)(2,1)S(1)}, u32[]{:S(2)}, u32[]{:S(2)}) %collective-permute-start.26) | collective-permute-done | bytes 196640 | tf_op jit(solution)/shard_map/ppermute | solution.py:22
  97.7 2.5 %fusion.23 = f32[1024,256]{1,0:T(8,128)} fusion(bf16[1024,384]{1,0:T(8,128)(2,1)} %collective-permute-done.25, bf16[384,256]{1,0:T(8,128)(2,1)S(1)} %collective-permute-done.26), kind=kOutput, calls=%fused_computation.42 | convolution fusion | flops 201326592 | bytes 2031616 | tf_op jit(solution)/shard_map/dot_general | solution.py:618
  100.2 2.0 %collective-permute-done.24 = bf16[384,256]{1,0:T(8,128)(2,1)S(1)} collective-permute-done((bf16[384,256]{1,0:T(8,128)(2,1)}, bf16[384,256]{1,0:T(8,128)(2,1)S(1)}, u32[]{:S(2)}, u32[]{:S(2)}) %collective-permute-start.24) | collective-permute-done | bytes 196640 | tf_op jit(solution)/shard_map/ppermute | solution.py:22
  102.2 2.6 %fusion.22 = f32[1024,256]{1,0:T(8,128)} fusion(bf16[1024,384]{1,0:T(8,128)(2,1)} %collective-permute-done.23, bf16[384,256]{1,0:T(8,128)(2,1)S(1)} %collective-permute-done.24), kind=kOutput, calls=%fused_computation.41 | convolution fusion | flops 201326592 | bytes 2031616 | tf_op jit(solution)/shard_map/dot_general | solution.py:618
  105.1 1.0 convert_element_type.52
  106.1 4.3 %all-to-all-start.1 = ((f16[16,40,512]{2,1,0:T(8,128)(2,1)}), f16[16,40,512]{2,1,0:T(8,128)(2,1)}, u32[]{:S(2)}, u32[]{:S(2)}) async-start(f16[16,40,512]{2,1,0:T(8,128)(2,1)} %convert_element_type.52), calls=%async_computation.1 | async-start | bytes 1310720 | tf_op jit(solution)/shard_map/all_to_all | solution.py:39
  110.4 2.7 %fusion.1 = f32[1024,256]{1,0:T(8,128)S(1)} fusion(f32[1024,256]{1,0:T(8,128)} %fusion.24, f32[1024,256]{1,0:T(8,128)} %fusion.23, f32[1024,256]{1,0:T(8,128)} %fusion.22, bf16[1024,384]{1,0:T(8,128)(2,1)} %get-tuple-element.50, bf16[384,256]{1,0:T(8,128)(2,1)} %get-tuple-element.51), kind=kOutput, calls=%fused_computation.2 | convolution fusion | flops 202113024 | bytes 5177344 | tf_op jit(solution)/shard_map/dot_general | solution.py:616
  113.1 1.0 fusion.7
  114.9 2.5 %collective-permute-start.33 = (f32[72,256]{1,0:T(8,128)}, f32[72,256]{1,0:T(8,128)}, u32[]{:S(2)}, u32[]{:S(2)}) collective-permute-start(f32[72,256]{1,0:T(8,128)} %get-tuple-element.71), channel_id=1, source_target_pairs={{0,24},{8,0},{16,8},{24,16},{1,25},{9,1},{17,9},{25,17},{2,26},{10... | collective-permute-start | bytes 221192 | tf_op jit(solution)/shard_map/ppermute | solution.py:22
  118.6 4.1 %all-to-all-done.1 = f16[16,40,512]{2,1,0:T(8,128)(2,1)} async-done(((f16[16,40,512]{2,1,0:T(8,128)(2,1)}), f16[16,40,512]{2,1,0:T(8,128)(2,1)}, u32[]{:S(2)}, u32[]{:S(2)}) %all-to-all-start.1) | async-done | bytes 655392 | tf_op jit(solution)/shard_map/all_to_all | solution.py:39
  122.7 1.2 convert_element_type.53.got
  124.1 1.7 collective-permute-start.7
  125.8 0.8 dynamic-slice_bitcast_fusion
  126.7 2.1 %collective-permute-start.29 = (f32[8,64,256]{2,1,0:T(8,128)}, f32[8,64,256]{2,1,0:T(8,128)}, u32[]{:S(2)}, u32[]{:S(2)}) collective-permute-start(f32[8,64,256]{2,1,0:T(8,128)} %dynamic-slice_bitcast_fusion), channel_id=1, source_target_pairs={{0,4},{4,0},{1,5},{5,1},{2,6},{6,2},{3,7},{7,3},{8,12},{12,8},{9,1... | collective-permute-start | bytes 1572872 | tf_op jit(solution)/shard_map/ppermute | solution.py:43
  128.7 0.9 add.92
  129.6 3.1 %collective-permute-start.8 = (f32[40,512]{1,0:T(8,128)S(1)}, f32[40,512]{1,0:T(8,128)S(1)}, u32[]{:S(2)}, u32[]{:S(2)}) collective-permute-start(f32[40,512]{1,0:T(8,128)S(1)} %add.92), channel_id=1, source_target_pairs={{0,64},{32,96},{64,0},{96,32},{128,192},{160,224},{192,128},{224,1... | collective-permute-start | bytes 245768 | tf_op jit(solution)/shard_map/ppermute | solution.py:330
  132.7 1.0 fusion.14
  133.7 1.7 collective-permute-done.8
  135.4 3.8 %collective-permute-start.9 = (f32[40,512]{1,0:T(8,128)S(1)}, f32[40,512]{1,0:T(8,128)S(1)}, u32[]{:S(2)}, u32[]{:S(2)}) collective-permute-start(f32[40,512]{1,0:T(8,128)S(1)} %add.93), channel_id=1, source_target_pairs={{0,192},{32,224},{64,128},{96,160},{128,64},{160,96},{192,0},{224,... | collective-permute-start | bytes 245768 | tf_op jit(solution)/shard_map/ppermute | solution.py:330
  139.3 1.3 z_messages.1
  141.3 3.4 %all-to-all-start.2 = ((f16[8,80,256]{2,1,0:T(8,128)(2,1)}), f16[8,80,256]{2,1,0:T(8,128)(2,1)S(1)}, u32[]{:S(2)}, u32[]{:S(2)}) async-start(f16[8,80,256]{2,1,0:T(8,128)(2,1)} %convert_element_type.65), calls=%async_computation.2 | async-start | bytes 655360 | tf_op jit(solution)/shard_map/all_to_all | solution.py:39
  145.2 2.1 %collective-permute-start.11 = (f16[40,512]{1,0:T(8,128)(2,1)S(1)}, f16[40,512]{1,0:T(8,128)(2,1)S(1)}, u32[]{:S(2)}, u32[]{:S(2)}) collective-permute-start(f16[40,512]{1,0:T(8,128)(2,1)S(1)} %convert_bitcast_fusion), channel_id=1, source_target_pairs={{0,2},{1,3},{2,0},{3,1},{4,6},{5,7},{6,4},{7,5},{8,10},{9,11},{10,... | collective-permute-start | bytes 122888 | tf_op jit(solution)/shard_map/ppermute | solution.py:22
  147.9 1.6 collective-permute-done.11
  149.5 1.8 %collective-permute-done.10 = f16[40,512]{1,0:T(8,128)(2,1)S(1)} collective-permute-done((f16[40,512]{1,0:T(8,128)(2,1)S(1)}, f16[40,512]{1,0:T(8,128)(2,1)S(1)}, u32[]{:S(2)}, u32[]{:S(2)}) %collective-permute-start.10) | collective-permute-done | bytes 40992 | tf_op jit(solution)/shard_map/ppermute | solution.py:22
  151.5 1.6 collective-permute-start.14
  153.1 1.1 collective-permute-start.15
  154.1 6.5 %collective-permute-start.16 = (f16[4,40,512]{2,1,0:T(8,128)(2,1)S(1)}, f16[4,40,512]{2,1,0:T(8,128)(2,1)}, u32[]{:S(2)}, u32[]{:S(2)}) collective-permute-start(f16[4,40,512]{2,1,0:T(8,128)(2,1)S(1)} %get-tuple-element.72), channel_id=1, source_target_pairs={{0,4},{4,0},{1,5},{5,1},{2,6},{6,2},{3,7},{7,3},{8,12},{12,8},{9,1... | collective-permute-start | bytes 491528 | tf_op jit(solution)/shard_map/ppermute | solution.py:43
  160.7 5.0 %collective-permute-start.17 = (f16[4,40,512]{2,1,0:T(8,128)(2,1)S(1)}, f16[4,40,512]{2,1,0:T(8,128)(2,1)}, u32[]{:S(2)}, u32[]{:S(2)}) collective-permute-start(f16[4,40,512]{2,1,0:T(8,128)(2,1)S(1)} %collective-permute-done.13), channel_id=1, source_target_pairs={{0,4},{4,0},{1,5},{5,1},{2,6},{6,2},{3,7},{7,3},{8,12},{12,8},{9,1... | collective-permute-start | bytes 491528 | tf_op jit(solution)/shard_map/ppermute | solution.py:43
  165.6 0.9 collective-permute-start.19
  167.5 0.9 convert_element_type.60.refs_4_
  168.4 0.9 convert_element_type.61.refs_5_
  169.4 0.9 convert_element_type.62.refs_6_
  170.4 0.9 convert_element_type.63.refs_7_
  171.3 2.1 %finished.1 = (f32[512,512]{1,0:T(8,128)}, f32[512,512]{1,0:T(8,128)}, f32[2,512]{1,0:T(2,128)}, f32[1,512]{1,0:T(1,128)}, f32[1,512]{1,0:T(1,128)}, /*index=5*/...) custom-call(s32[3]{0:T(128)S(1)} %pad_add_fusion.place, f32[4,40,512]{2,1,0:T(8,128)S(1)} %get-tuple-element.73.refs_0_, ...), custom_call_target="tpu_custom_call" | custom-call | tf_op jit(solution)/shard_map/finished/pallas_call | solution.py:485
  (99 shorter events, 12.1 us)
Async XLA Ops:
  0.6 1.6 copy-start
  0.7 6.6 %copy-start.3 = (bf16[256,512]{1,0:T(8,128)(2,1)S(1)}, bf16[256,512]{1,0:T(8,128)(2,1)}, u32[]{:S(2)}) copy-start(bf16[256,512]{1,0:T(8,128)(2,1)} %refs_5_.1) | copy-start | bytes 786436
  5.1 15.3 %copy-start.17 = (bf16[384,256]{1,0:T(8,128)(2,1)}, bf16[384,256]{1,0:T(8,128)(2,1)S(1)}, u32[]{:S(2)}) copy-start(bf16[384,256]{1,0:T(8,128)(2,1)S(1)} %get-tuple-element.74.refs_0_) | copy-start | bytes 589828
  5.1 7.2 %collective-permute-start = (bf16[384,256]{1,0:T(8,128)(2,1)S(1)}, bf16[384,256]{1,0:T(8,128)(2,1)S(1)}, u32[]{:S(2)}, u32[]{:S(2)}) collective-permute-start(bf16[384,256]{1,0:T(8,128)(2,1)S(1)} %get-tuple-element.74.refs_0_), channel_id=1, source_target_pairs={{0,1},{1,2},{2,3},{3,0},{4,5},{5,6},{6,7},{7,4},{8,9},{9,10},{10,1... | collective-permute-start | bytes 589832 | tf_op jit(solution)/shard_map/ppermute | solution.py:22
  7.2 23.0 %collective-permute-start.3 = (bf16[256,512]{1,0:T(8,128)(2,1)S(1)}, bf16[256,512]{1,0:T(8,128)(2,1)S(1)}, u32[]{:S(2)}, u32[]{:S(2)}) collective-permute-start(bf16[256,512]{1,0:T(8,128)(2,1)S(1)} %copy-done.3), channel_id=1, source_target_pairs={{0,1},{1,2},{2,3},{3,0},{4,5},{5,6},{6,7},{7,4},{8,9},{9,10},{10,1... | collective-permute-start | bytes 786440 | tf_op jit(solution)/shard_map/ppermute | solution.py:22
  8.5 21.8 %collective-permute-start.4 = (bf16[256,512]{1,0:T(8,128)(2,1)S(1)}, bf16[256,512]{1,0:T(8,128)(2,1)S(1)}, u32[]{:S(2)}, u32[]{:S(2)}) collective-permute-start(bf16[256,512]{1,0:T(8,128)(2,1)S(1)} %copy-done.3), channel_id=1, source_target_pairs={{0,2},{1,3},{2,0},{3,1},{4,6},{5,7},{6,4},{7,5},{8,10},{9,11},{10,... | collective-permute-start | bytes 786440 | tf_op jit(solution)/shard_map/ppermute | solution.py:22
  9.8 20.5 %collective-permute-start.5 = (bf16[256,512]{1,0:T(8,128)(2,1)S(1)}, bf16[256,512]{1,0:T(8,128)(2,1)S(1)}, u32[]{:S(2)}, u32[]{:S(2)}) collective-permute-start(bf16[256,512]{1,0:T(8,128)(2,1)S(1)} %copy-done.3), channel_id=1, source_target_pairs={{0,3},{1,0},{2,1},{3,2},{4,7},{5,4},{6,5},{7,6},{8,11},{9,8},{10,9... | collective-permute-start | bytes 786440 | tf_op jit(solution)/shard_map/ppermute | solution.py:22
  11.8 17.7 %collective-permute-start.1 = (bf16[384,256]{1,0:T(8,128)(2,1)S(1)}, bf16[384,256]{1,0:T(8,128)(2,1)S(1)}, u32[]{:S(2)}, u32[]{:S(2)}) collective-permute-start(bf16[384,256]{1,0:T(8,128)(2,1)S(1)} %get-tuple-element.74.refs_0_), channel_id=1, source_target_pairs={{0,2},{1,3},{2,0},{3,1},{4,6},{5,7},{6,4},{7,5},{8,10},{9,11},{10,... | collective-permute-start | bytes 589832 | tf_op jit(solution)/shard_map/ppermute | solution.py:22
  12.3 8.1 %copy-start.18 = (bf16[384,256]{1,0:T(8,128)(2,1)}, bf16[384,256]{1,0:T(8,128)(2,1)S(1)}, u32[]{:S(2)}) copy-start(bf16[384,256]{1,0:T(8,128)(2,1)S(1)} %collective-permute-done.refs_1_) | copy-start | bytes 589828
  12.3 18.0 %collective-permute-start.2 = (bf16[384,256]{1,0:T(8,128)(2,1)S(1)}, bf16[384,256]{1,0:T(8,128)(2,1)}, u32[]{:S(2)}, u32[]{:S(2)}) collective-permute-start(bf16[384,256]{1,0:T(8,128)(2,1)S(1)} %get-tuple-element.74.refs_0_), channel_id=1, source_target_pairs={{0,3},{1,0},{2,1},{3,2},{4,7},{5,4},{6,5},{7,6},{8,11},{9,8},{10,9... | collective-permute-start | bytes 589832 | tf_op jit(solution)/shard_map/ppermute | solution.py:22
  29.5 0.9 copy-start.19
  30.3 0.7 copy-start.14
  30.3 0.8 copy-start.15
  30.3 0.9 copy-start.16
  36.9 16.3 %all-to-all-start = ((f32[4,96,512]{2,1,0:T(8,128)}), f32[4,96,512]{2,1,0:T(8,128)S(1)}, u32[]{:S(2)}, u32[]{:S(2)}) async-start(f32[4,96,512]{2,1,0:T(8,128)} %bitcast.75), calls=%async_computation | async-start | bytes 1572864 | tf_op jit(solution)/shard_map/all_to_all | solution.py:39
  48.0 34.8 %collective-permute-start.27 = (bf16[1024,384]{1,0:T(8,128)(2,1)}, bf16[1024,384]{1,0:T(8,128)(2,1)}, u32[]{:S(2)}, u32[]{:S(2)}) collective-permute-start(bf16[1024,384]{1,0:T(8,128)(2,1)} %get-tuple-element.54), channel_id=1, source_target_pairs={{0,24},{8,0},{16,8},{24,16},{1,25},{9,1},{17,9},{25,17},{2,26},{10... | collective-permute-start | bytes 2359304 | tf_op jit(solution)/shard_map/ppermute | solution.py:22
  50.8 44.2 %collective-permute-start.25 = (bf16[1024,384]{1,0:T(8,128)(2,1)}, bf16[1024,384]{1,0:T(8,128)(2,1)}, u32[]{:S(2)}, u32[]{:S(2)}) collective-permute-start(bf16[1024,384]{1,0:T(8,128)(2,1)} %get-tuple-element.53), channel_id=1, source_target_pairs={{0,16},{8,24},{16,0},{24,8},{1,17},{9,25},{17,1},{25,9},{2,18},{10... | collective-permute-start | bytes 2359304 | tf_op jit(solution)/shard_map/ppermute | solution.py:22
  53.9 14.4 %collective-permute-start.20 = (bf16[96,512]{1,0:T(8,128)(2,1)}, bf16[96,512]{1,0:T(8,128)(2,1)S(1)}, u32[]{:S(2)}, u32[]{:S(2)}) collective-permute-start(bf16[96,512]{1,0:T(8,128)(2,1)} %get-tuple-element.67.refs_0_), channel_id=1, source_target_pairs={{0,1},{1,2},{2,3},{3,0},{4,5},{5,6},{6,7},{7,4},{8,9},{9,10},{10,1... | collective-permute-start | bytes 294920 | tf_op jit(solution)/shard_map/ppermute | solution.py:22
  54.2 17.3 %collective-permute-start.21 = (bf16[96,512]{1,0:T(8,128)(2,1)}, bf16[96,512]{1,0:T(8,128)(2,1)S(1)}, u32[]{:S(2)}, u32[]{:S(2)}) collective-permute-start(bf16[96,512]{1,0:T(8,128)(2,1)} %get-tuple-element.67.refs_0_), channel_id=1, source_target_pairs={{0,2},{1,3},{2,0},{3,1},{4,6},{5,7},{6,4},{7,5},{8,10},{9,11},{10,... | collective-permute-start | bytes 294920 | tf_op jit(solution)/shard_map/ppermute | solution.py:22
  56.0 16.9 %collective-permute-start.22 = (bf16[96,512]{1,0:T(8,128)(2,1)}, bf16[96,512]{1,0:T(8,128)(2,1)}, u32[]{:S(2)}, u32[]{:S(2)}) collective-permute-start(bf16[96,512]{1,0:T(8,128)(2,1)} %get-tuple-element.67.refs_0_), channel_id=1, source_target_pairs={{0,3},{1,0},{2,1},{3,2},{4,7},{5,4},{6,5},{7,6},{8,11},{9,8},{10,9... | collective-permute-start | bytes 294920 | tf_op jit(solution)/shard_map/ppermute | solution.py:22
  68.3 0.6 copy-start.5
  69.0 35.8 %collective-permute-start.6 = (f32[520,512]{1,0:T(8,128)}, f32[520,512]{1,0:T(8,128)S(1)}, u32[]{:S(2)}, u32[]{:S(2)}) collective-permute-start(f32[520,512]{1,0:T(8,128)} %get-tuple-element.45), channel_id=1, source_target_pairs={{0,4},{4,0},{1,5},{5,1},{2,6},{6,2},{3,7},{7,3},{8,12},{12,8},{9,1... | collective-permute-start | bytes 3194888 | tf_op jit(solution)/shard_map/ppermute | solution.py:43
  71.5 0.6 copy-start.7
  72.2 28.0 %collective-permute-start.23 = (bf16[1024,384]{1,0:T(8,128)(2,1)}, bf16[1024,384]{1,0:T(8,128)(2,1)}, u32[]{:S(2)}, u32[]{:S(2)}) collective-permute-start(bf16[1024,384]{1,0:T(8,128)(2,1)} %get-tuple-element.52), channel_id=1, source_target_pairs={{0,8},{8,16},{16,24},{24,0},{1,9},{9,17},{17,25},{25,1},{2,10},{10... | collective-permute-start | bytes 2359304 | tf_op jit(solution)/shard_map/ppermute | solution.py:22
  72.9 1.0 copy-start.4
  73.9 0.9 copy-start.6
  74.8 0.9 copy-start.8
  77.7 0.8 copy-start.2
  78.5 0.6 copy-start.11
  79.1 9.4 %collective-permute-start.28 = (bf16[384,256]{1,0:T(8,128)(2,1)}, bf16[384,256]{1,0:T(8,128)(2,1)}, u32[]{:S(2)}, u32[]{:S(2)}) collective-permute-start(bf16[384,256]{1,0:T(8,128)(2,1)} %get-tuple-element.51), channel_id=1, source_target_pairs={{0,24},{8,0},{16,8},{24,16},{1,25},{9,1},{17,9},{25,17},{2,26},{10... | collective-permute-start | bytes 589832 | tf_op jit(solution)/shard_map/ppermute | solution.py:22
  82.1 10.3 %copy-start.12 = (f32[8,4,2,8,256]{4,3,1,0,2:T(8,128)}, f32[8,4,2,8,256]{4,3,1,0,2:T(8,128)S(1)}, u32[]{:S(2)}) copy-start(f32[8,4,2,8,256]{4,3,1,0,2:T(8,128)S(1)} %copy.27) | copy-start | bytes 1572868
  82.9 14.8 %collective-permute-start.26 = (bf16[384,256]{1,0:T(8,128)(2,1)}, bf16[384,256]{1,0:T(8,128)(2,1)S(1)}, u32[]{:S(2)}, u32[]{:S(2)}) collective-permute-start(bf16[384,256]{1,0:T(8,128)(2,1)} %get-tuple-element.51), channel_id=1, source_target_pairs={{0,16},{8,24},{16,0},{24,8},{1,17},{9,25},{17,1},{25,9},{2,18},{10... | collective-permute-start | bytes 589832 | tf_op jit(solution)/shard_map/ppermute | solution.py:22
  88.5 13.7 %collective-permute-start.24 = (bf16[384,256]{1,0:T(8,128)(2,1)}, bf16[384,256]{1,0:T(8,128)(2,1)S(1)}, u32[]{:S(2)}, u32[]{:S(2)}) collective-permute-start(bf16[384,256]{1,0:T(8,128)(2,1)} %get-tuple-element.51), channel_id=1, source_target_pairs={{0,8},{8,16},{16,24},{24,0},{1,9},{9,17},{17,25},{25,1},{2,10},{10... | collective-permute-start | bytes 589832 | tf_op jit(solution)/shard_map/ppermute | solution.py:22
  95.0 9.8 %copy-start.1 = (f32[520,512]{1,0:T(8,128)S(1)}, f32[520,512]{1,0:T(8,128)}, u32[]{:S(2)}) copy-start(f32[520,512]{1,0:T(8,128)} %get-tuple-element.44.mine) | copy-start | bytes 3194884
  95.0 9.8 %copy-start.9 = (f32[512]{0:T(512)S(1)}, f32[512]{0:T(512)}, u32[]{:S(2)}) copy-start(f32[512]{0:T(512)} %get-tuple-element.68) | copy-start | bytes 6148
  95.0 9.8 %copy-start.10 = (f32[1,512]{1,0:T(1,128)S(1)}, f32[1,512]{1,0:T(1,128)}, u32[]{:S(2)}) copy-start(f32[1,512]{1,0:T(1,128)} %get-tuple-element.47.squares) | copy-start | bytes 6148
  95.0 18.1 %collective-permute-start.30 = (f32[264,256]{1,0:T(8,128)S(1)}, f32[264,256]{1,0:T(8,128)}, u32[]{:S(2)}, u32[]{:S(2)}) collective-permute-start(f32[264,256]{1,0:T(8,128)S(1)} %fusion.4), channel_id=1, source_target_pairs={{0,4},{4,0},{1,5},{5,1},{2,6},{6,2},{3,7},{7,3},{8,12},{12,8},{9,1... | collective-permute-start | bytes 811016 | tf_op jit(solution)/shard_map/ppermute | solution.py:22
  106.1 16.6 %all-to-all-start.1 = ((f16[16,40,512]{2,1,0:T(8,128)(2,1)}), f16[16,40,512]{2,1,0:T(8,128)(2,1)}, u32[]{:S(2)}, u32[]{:S(2)}) async-start(f16[16,40,512]{2,1,0:T(8,128)(2,1)} %convert_element_type.52), calls=%async_computation.1 | async-start | bytes 1310720 | tf_op jit(solution)/shard_map/all_to_all | solution.py:39
  110.4 2.7 %copy-start.13 = (f32[8,4,2,8,256]{4,3,1,0,2:T(8,128)S(1)}, f32[8,4,2,8,256]{4,3,1,0,2:T(8,128)}, u32[]{:S(2)}) copy-start(f32[8,4,2,8,256]{4,3,1,0,2:T(8,128)} %copy-done.12) | copy-start | bytes 1572868
  114.9 17.8 %collective-permute-start.33 = (f32[72,256]{1,0:T(8,128)}, f32[72,256]{1,0:T(8,128)}, u32[]{:S(2)}, u32[]{:S(2)}) collective-permute-start(f32[72,256]{1,0:T(8,128)} %get-tuple-element.71), channel_id=1, source_target_pairs={{0,24},{8,0},{16,8},{24,16},{1,25},{9,1},{17,9},{25,17},{2,26},{10... | collective-permute-start | bytes 221192 | tf_op jit(solution)/shard_map/ppermute | solution.py:22
  117.4 15.3 %collective-permute-start.32 = (f32[72,256]{1,0:T(8,128)}, f32[72,256]{1,0:T(8,128)}, u32[]{:S(2)}, u32[]{:S(2)}) collective-permute-start(f32[72,256]{1,0:T(8,128)} %get-tuple-element.70), channel_id=1, source_target_pairs={{0,16},{8,24},{16,0},{24,8},{1,17},{9,25},{17,1},{25,9},{2,18},{10... | collective-permute-start | bytes 221192 | tf_op jit(solution)/shard_map/ppermute | solution.py:22
  118.0 14.7 %collective-permute-start.31 = (f32[72,256]{1,0:T(8,128)}, f32[72,256]{1,0:T(8,128)}, u32[]{:S(2)}, u32[]{:S(2)}) collective-permute-start(f32[72,256]{1,0:T(8,128)} %get-tuple-element.69), channel_id=1, source_target_pairs={{0,8},{8,16},{16,24},{24,0},{1,9},{9,17},{17,25},{25,1},{2,10},{10... | collective-permute-start | bytes 221192 | tf_op jit(solution)/shard_map/ppermute | solution.py:22
  124.1 4.6 %collective-permute-start.7 = (f32[40,512]{1,0:T(8,128)S(1)}, f32[40,512]{1,0:T(8,128)}, u32[]{:S(2)}, u32[]{:S(2)}) collective-permute-start(f32[40,512]{1,0:T(8,128)S(1)} %plane_total.1), channel_id=1, source_target_pairs={{0,32},{32,0},{64,96},{96,64},{128,160},{160,128},{192,224},{224,1... | collective-permute-start | bytes 245768 | tf_op jit(solution)/shard_map/ppermute | solution.py:330
  126.7 12.6 %collective-permute-start.29 = (f32[8,64,256]{2,1,0:T(8,128)}, f32[8,64,256]{2,1,0:T(8,128)}, u32[]{:S(2)}, u32[]{:S(2)}) collective-permute-start(f32[8,64,256]{2,1,0:T(8,128)} %dynamic-slice_bitcast_fusion), channel_id=1, source_target_pairs={{0,4},{4,0},{1,5},{5,1},{2,6},{6,2},{3,7},{7,3},{8,12},{12,8},{9,1... | collective-permute-start | bytes 1572872 | tf_op jit(solution)/shard_map/ppermute | solution.py:43
  129.6 5.8 %collective-permute-start.8 = (f32[40,512]{1,0:T(8,128)S(1)}, f32[40,512]{1,0:T(8,128)S(1)}, u32[]{:S(2)}, u32[]{:S(2)}) collective-permute-start(f32[40,512]{1,0:T(8,128)S(1)} %add.92), channel_id=1, source_target_pairs={{0,64},{32,96},{64,0},{96,32},{128,192},{160,224},{192,128},{224,1... | collective-permute-start | bytes 245768 | tf_op jit(solution)/shard_map/ppermute | solution.py:330
  135.4 9.3 %collective-permute-start.9 = (f32[40,512]{1,0:T(8,128)S(1)}, f32[40,512]{1,0:T(8,128)S(1)}, u32[]{:S(2)}, u32[]{:S(2)}) collective-permute-start(f32[40,512]{1,0:T(8,128)S(1)} %add.93), channel_id=1, source_target_pairs={{0,192},{32,224},{64,128},{96,160},{128,64},{160,96},{192,0},{224,... | collective-permute-start | bytes 245768 | tf_op jit(solution)/shard_map/ppermute | solution.py:330
  141.3 25.3 %all-to-all-start.2 = ((f16[8,80,256]{2,1,0:T(8,128)(2,1)}), f16[8,80,256]{2,1,0:T(8,128)(2,1)S(1)}, u32[]{:S(2)}, u32[]{:S(2)}) async-start(f16[8,80,256]{2,1,0:T(8,128)(2,1)} %convert_element_type.65), calls=%async_computation.2 | async-start | bytes 655360 | tf_op jit(solution)/shard_map/all_to_all | solution.py:39
  145.0 2.9 %collective-permute-start.12 = (f16[40,512]{1,0:T(8,128)(2,1)S(1)}, f16[40,512]{1,0:T(8,128)(2,1)S(1)}, u32[]{:S(2)}, u32[]{:S(2)}) collective-permute-start(f16[40,512]{1,0:T(8,128)(2,1)S(1)} %convert_bitcast_fusion), channel_id=1, source_target_pairs={{0,3},{1,0},{2,1},{3,2},{4,7},{5,4},{6,5},{7,6},{8,11},{9,8},{10,9... | collective-permute-start | bytes 122888 | tf_op jit(solution)/shard_map/ppermute | solution.py:22
  145.2 4.4 %collective-permute-start.11 = (f16[40,512]{1,0:T(8,128)(2,1)S(1)}, f16[40,512]{1,0:T(8,128)(2,1)S(1)}, u32[]{:S(2)}, u32[]{:S(2)}) collective-permute-start(f16[40,512]{1,0:T(8,128)(2,1)S(1)} %convert_bitcast_fusion), channel_id=1, source_target_pairs={{0,2},{1,3},{2,0},{3,1},{4,6},{5,7},{6,4},{7,5},{8,10},{9,11},{10,... | collective-permute-start | bytes 122888 | tf_op jit(solution)/shard_map/ppermute | solution.py:22
  147.3 4.1 %collective-permute-start.10 = (f16[40,512]{1,0:T(8,128)(2,1)S(1)}, f16[40,512]{1,0:T(8,128)(2,1)S(1)}, u32[]{:S(2)}, u32[]{:S(2)}) collective-permute-start(f16[40,512]{1,0:T(8,128)(2,1)S(1)} %convert_bitcast_fusion), channel_id=1, source_target_pairs={{0,1},{1,2},{2,3},{3,0},{4,5},{5,6},{6,7},{7,4},{8,9},{9,10},{10,1... | collective-permute-start | bytes 122888 | tf_op jit(solution)/shard_map/ppermute | solution.py:22
  151.4 9.3 %collective-permute-start.13 = (f16[4,40,512]{2,1,0:T(8,128)(2,1)S(1)}, f16[4,40,512]{2,1,0:T(8,128)(2,1)S(1)}, u32[]{:S(2)}, u32[]{:S(2)}) collective-permute-start(f16[4,40,512]{2,1,0:T(8,128)(2,1)S(1)} %get-tuple-element.72), channel_id=1, source_target_pairs={{0,8},{8,16},{16,24},{24,0},{1,9},{9,17},{17,25},{25,1},{2,10},{10... | collective-permute-start | bytes 491528 | tf_op jit(solution)/shard_map/ppermute | solution.py:22
  151.5 14.2 %collective-permute-start.14 = (f16[4,40,512]{2,1,0:T(8,128)(2,1)S(1)}, f16[4,40,512]{2,1,0:T(8,128)(2,1)S(1)}, u32[]{:S(2)}, u32[]{:S(2)}) collective-permute-start(f16[4,40,512]{2,1,0:T(8,128)(2,1)S(1)} %get-tuple-element.72), channel_id=1, source_target_pairs={{0,16},{8,24},{16,0},{24,8},{1,17},{9,25},{17,1},{25,9},{2,18},{10... | collective-permute-start | bytes 491528 | tf_op jit(solution)/shard_map/ppermute | solution.py:22
  153.1 12.6 %collective-permute-start.15 = (f16[4,40,512]{2,1,0:T(8,128)(2,1)S(1)}, f16[4,40,512]{2,1,0:T(8,128)(2,1)S(1)}, u32[]{:S(2)}, u32[]{:S(2)}) collective-permute-start(f16[4,40,512]{2,1,0:T(8,128)(2,1)S(1)} %get-tuple-element.72), channel_id=1, source_target_pairs={{0,24},{8,0},{16,8},{24,16},{1,25},{9,1},{17,9},{25,17},{2,26},{10... | collective-permute-start | bytes 491528 | tf_op jit(solution)/shard_map/ppermute | solution.py:22
  154.1 13.3 %collective-permute-start.16 = (f16[4,40,512]{2,1,0:T(8,128)(2,1)S(1)}, f16[4,40,512]{2,1,0:T(8,128)(2,1)}, u32[]{:S(2)}, u32[]{:S(2)}) collective-permute-start(f16[4,40,512]{2,1,0:T(8,128)(2,1)S(1)} %get-tuple-element.72), channel_id=1, source_target_pairs={{0,4},{4,0},{1,5},{5,1},{2,6},{6,2},{3,7},{7,3},{8,12},{12,8},{9,1... | collective-permute-start | bytes 491528 | tf_op jit(solution)/shard_map/ppermute | solution.py:43
  160.7 7.8 %collective-permute-start.17 = (f16[4,40,512]{2,1,0:T(8,128)(2,1)S(1)}, f16[4,40,512]{2,1,0:T(8,128)(2,1)}, u32[]{:S(2)}, u32[]{:S(2)}) collective-permute-start(f16[4,40,512]{2,1,0:T(8,128)(2,1)S(1)} %collective-permute-done.13), channel_id=1, source_target_pairs={{0,4},{4,0},{1,5},{5,1},{2,6},{6,2},{3,7},{7,3},{8,12},{12,8},{9,1... | collective-permute-start | bytes 491528 | tf_op jit(solution)/shard_map/ppermute | solution.py:43
  165.6 3.8 %collective-permute-start.18 = (f16[4,40,512]{2,1,0:T(8,128)(2,1)S(1)}, f16[4,40,512]{2,1,0:T(8,128)(2,1)}, u32[]{:S(2)}, u32[]{:S(2)}) collective-permute-start(f16[4,40,512]{2,1,0:T(8,128)(2,1)S(1)} %collective-permute-done.14), channel_id=1, source_target_pairs={{0,4},{4,0},{1,5},{5,1},{2,6},{6,2},{3,7},{7,3},{8,12},{12,8},{9,1... | collective-permute-start | bytes 491528 | tf_op jit(solution)/shard_map/ppermute | solution.py:43
  165.6 4.7 %collective-permute-start.19 = (f16[4,40,512]{2,1,0:T(8,128)(2,1)S(1)}, f16[4,40,512]{2,1,0:T(8,128)(2,1)}, u32[]{:S(2)}, u32[]{:S(2)}) collective-permute-start(f16[4,40,512]{2,1,0:T(8,128)(2,1)S(1)} %collective-permute-done.15), channel_id=1, source_target_pairs={{0,4},{4,0},{1,5},{5,1},{2,6},{6,2},{3,7},{7,3},{8,12},{12,8},{9,1... | collective-permute-start | bytes 491528 | tf_op jit(solution)/shard_map/ppermute | solution.py:43

commit v4 on v3

--- a/solution.py
+++ b/solution.py
@@ -340,17 +340,17 @@
     out[j, rows + 2 : rows + 3, :] = jnp.broadcast_to(piece_e, (1, w))
 
 
-def plane_messages(mine, got, b_two, squares, n):
+def plane_messages(mine, got, late, n):
     w = mine.shape[1]
     rows = mine.shape[0] - 8
     per = n // 8
     k = w // per
 
-    def body(mine, got, b_two, squares, out):
+    def body(mine, got, late, out):
         big, big_e = scaled(mine[:rows, :] + got[:rows, :])
         row = lax.broadcasted_iota(jnp.int32, (8, w), 0)
         small = mine[rows:, :] + got[rows:, :]
-        small = jnp.where(row == 5, b_two[...], jnp.where(row == 6, squares[...], small))
+        small = jnp.where(row == 5, late[0:1, :], jnp.where(row == 6, late[1:2, :], small))
         small, small_e = scaled(small, 1)
         out[:, : rows // n, :] = big.reshape(n, rows // n, w)
         for j in range(n):
@@ -362,7 +362,7 @@
         out_shape=jax.ShapeDtypeStruct((n, rows // n + 8, w), jnp.float32),
         compiler_params=pltpu.CompilerParams(vmem_limit_bytes=12 * 2**20),
         name="plane_messages",
-    )(mine, got, b_two, squares)
+    )(mine, got, late)
     return out.astype(jnp.float16)
 
 
@@ -528,7 +528,7 @@
     side = 8 * w // n
     got = other_core(give)
 
-    got = exchanged(plane_messages(mine, got, b_two, squares, n), ("y", "query"))
+    got = exchanged(plane_messages(mine, got, jnp.concatenate([b_two, squares]), n), ("y", "query"))
     both = plane_total(got.astype(jnp.float32))
     both = summed_in_pairs(both, "z")
     got = total_message(both, side)

time: 176 us -> 174 us (0.989)
  local copies, waits for them, and re-layouts: 10.5 us -> 3.42 us
  waiting for transfers between devices: 29.9 us -> 34.4 us
  starting transfers between devices: 71 us -> 74.5 us
    unnamed x40 -> x24, local copies, waits for them, and re-layouts: 7.81 us -> 2.46 us
    ppermute x25, waiting for transfers between devices: 21.9 us -> 26.2 us  [shift(): return lax.ppermute(x, axis, [(i, (i + k) % n) for i in range(n)])]
    all_to_all x3, starting transfers between devices: 12.6 us -> 16 us  [exchanged(): return lax.all_to_all(x, axis, 0, 0, tiled=True)]
  transfers between devices with their start and end apart: 37 -> 37, of which waited for: 11 -> 9; matrix products, arithmetic and copies ran while one was open for 13% -> 12% of each run, Pallas kernels for 16% -> 16%
where the time goes in v4:
time: 174 us
  starting transfers between devices  74.5 us (43%)
  Pallas kernels  34.8 us (20%)
  waiting for transfers between devices  34.4 us (20%)
  matrix products  11.9 us (7%)
  other arithmetic  11.6 us (7%)
  local copies, waits for them, and re-layouts  3.42 us (2%)
  between operations  2.84 us (2%)
    ppermute x25, starting transfers between devices, shift(): return lax.ppermute(x, axis, [(i, (i + k) % n) for i in range(n)])  33 us
    ppermute x25, waiting for transfers between devices, shift(): return lax.ppermute(x, axis, [(i, (i + k) % n) for i in range(n)])  26.2 us
    ppermute x6, starting transfers between devices, other_core(): return lax.ppermute(x, 'c', [(0, 1), (1, 0)])  17 us
    all_to_all x3, starting transfers between devices, exchanged(): return lax.all_to_all(x, axis, 0, 0, tiled=True)  16 us
    pallas_call x1, Pallas kernels, trunk_backward(): pl.pallas_call(functools.partial(back_kernel, inv_scale=inv_scale), grid_...  11.5 us
    ppermute x3, starting transfers between devices, summed_in_pairs(): x = x + lax.ppermute(x, axis, [(i, i ^ pair) for i in range(n)])  8.6 us
    dot_general x3, matrix products, local(): jnp.dot(sens_y[k], pre_y[k], preferred_element_type=jnp.float32)  6.49 us
    all_to_all x3, waiting for transfers between devices, exchanged(): return lax.all_to_all(x, axis, 0, 0, tiled=True)  6.45 us
  transfers between devices with their start and end apart: 37, of which 9 were waited for; matrix products, arithmetic and copies ran while one was open for 12% of the time, Pallas kernels for 16%

profile of v4, /device:TPU:1, one launch (start us, length us, event | category | flops | bytes accessed | tf_op | source)
XLA Modules:
  0.0 173.5 jit_solution(17976479068382700826)
XLA Ops:
  0.7 1.6 copy-done
  2.2 2.9 %fusion.21 = (bf16[384,256]{1,0:T(8,128)(2,1)S(1)}, f32[384,256]{1,0:T(8,128)S(1)}) fusion(f32[256]{0:T(256)} %param.17, bf16[384,4096]{1,0:T(8,128)(2,1)} %src, bf16[4096,256]{1,0:T(8,128)(2,1)S(1)} %copy-done), kind=kOutput, calls=%fused_computation.41 | convolution fusion | flops 805502976 | bytes 5833728 | tf_op jit(solution)/shard_map/dot_general | solution.py:571
  5.1 2.1 %collective-permute-start = (bf16[384,256]{1,0:T(8,128)(2,1)S(1)}, bf16[384,256]{1,0:T(8,128)(2,1)S(1)}, u32[]{:S(2)}, u32[]{:S(2)}) collective-permute-start(bf16[384,256]{1,0:T(8,128)(2,1)S(1)} %get-tuple-element.74.refs_0_), channel_id=1, source_target_pairs={{0,1},{1,2},{2,3},{3,0},{4,5},{5,6},{6,7},{7,4},{8,9},{9,10},{10,1... | collective-permute-start | bytes 589832 | tf_op jit(solution)/shard_map/ppermute | solution.py:22
  7.2 1.2 collective-permute-start.3
  8.5 1.3 collective-permute-start.4
  9.8 2.0 %collective-permute-start.5 = (bf16[256,512]{1,0:T(8,128)(2,1)S(1)}, bf16[256,512]{1,0:T(8,128)(2,1)S(1)}, u32[]{:S(2)}, u32[]{:S(2)}) collective-permute-start(bf16[256,512]{1,0:T(8,128)(2,1)S(1)} %copy-done.2), channel_id=1, source_target_pairs={{0,3},{1,0},{2,1},{3,2},{4,7},{5,4},{6,5},{7,6},{8,11},{9,8},{10,9... | collective-permute-start | bytes 786440 | tf_op jit(solution)/shard_map/ppermute | solution.py:22
  12.3 2.0 %collective-permute-start.2 = (bf16[384,256]{1,0:T(8,128)(2,1)S(1)}, bf16[384,256]{1,0:T(8,128)(2,1)}, u32[]{:S(2)}, u32[]{:S(2)}) collective-permute-start(bf16[384,256]{1,0:T(8,128)(2,1)S(1)} %get-tuple-element.74.refs_0_), channel_id=1, source_target_pairs={{0,3},{1,0},{2,1},{3,2},{4,7},{5,4},{6,5},{7,6},{8,11},{9,8},{10,9... | collective-permute-start | bytes 589832 | tf_op jit(solution)/shard_map/ppermute | solution.py:22
  14.3 6.2 %trunk_forward.1 = (bf16[2048,512]{1,0:T(8,128)(2,1)}, f32[2048,512]{1,0:T(8,128)}, f32[2048,512]{1,0:T(8,128)}) custom-call(s32[2,2048]{1,0:T(2,128)} %index.3, f32[2,512]{1,0:T(2,128)} %v_one.1, f32[1,512]{1,0:T(1,128)} %bitcast.80, bf16[512,512]{1,0:T(8,128)(2,1)} %v_two.3, f32[1,512]{1,0:T(1,128)} %bitcast.81, bf16[512,512]{1,0:T(8,128)(2,1)} %v_three.3, ...), custom_call_target="tpu_custom_call" | custom-call | flops 2147483648 | bytes 4000000 | tf_op jit(solution)/shard_map/trunk_forward/pallas_call | solution.py:100
  20.5 9.1 %collective-permute-done.1.refs_2_ = bf16[384,256]{1,0:T(8,128)(2,1)} collective-permute-done((bf16[384,256]{1,0:T(8,128)(2,1)S(1)}, bf16[384,256]{1,0:T(8,128)(2,1)}, u32[]{:S(2)}, u32[]{:S(2)}) %collective-permute-start.1) | collective-permute-done | bytes 196640 | tf_op jit(solution)/shard_map/ppermute | solution.py:22
  29.6 0.7 collective-permute-done.2.refs_3_
  30.3 0.7 copy-done.7
  31.2 5.7 %misfit_of.1 = (bf16[384,512]{1,0:T(8,128)(2,1)}, bf16[384,2048]{1,0:T(8,128)(2,1)}, f32[1,512]{1,0:T(1,128)}, f32[384,512]{1,0:T(8,128)}) custom-call(bf16[384,256]{1,0:T(8,128)(2,1)} %copy-done.10, bf16[384,256]{1,0:T(8,128)(2,1)} %copy-done.11, bf16[384,256]{1,0:T(8,128)(2,1)} %collective-permute-done.1.refs_2_, ...), custom_call_target="tpu_custom_call" | custom-call | flops 2013265920 | bytes 8000000 | tf_op jit(solution)/shard_map/misfit_of/pallas_call | solution.py:155
  36.9 4.8 %all-to-all-start = ((f32[4,96,512]{2,1,0:T(8,128)}), f32[4,96,512]{2,1,0:T(8,128)S(1)}, u32[]{:S(2)}, u32[]{:S(2)}) async-start(f32[4,96,512]{2,1,0:T(8,128)} %bitcast.74), calls=%async_computation | async-start | bytes 1572864 | tf_op jit(solution)/shard_map/all_to_all | solution.py:39
  41.7 6.3 %columns_by_y.1 = (bf16[1024,384]{1,0:T(8,128)(2,1)}, bf16[1024,384]{1,0:T(8,128)(2,1)}, bf16[1024,384]{1,0:T(8,128)(2,1)}, bf16[1024,384]{1,0:T(8,128)(2,1)}) custom-call(s32[1]{0:T(128)} %bitcast.1.y, bf16[384,4096]{1,0:T(8,128)(2,1)} %src), custom_call_target="tpu_custom_call" | custom-call | flops 8000000 | bytes 6291456 | tf_op jit(solution)/shard_map/columns_by_y/pallas_call | solution.py:227
  48.0 2.7 %collective-permute-start.27 = (bf16[1024,384]{1,0:T(8,128)(2,1)}, bf16[1024,384]{1,0:T(8,128)(2,1)}, u32[]{:S(2)}, u32[]{:S(2)}) collective-permute-start(bf16[1024,384]{1,0:T(8,128)(2,1)} %get-tuple-element.54), channel_id=1, source_target_pairs={{0,24},{8,0},{16,8},{24,16},{1,25},{9,1},{17,9},{25,17},{2,26},{10... | collective-permute-start | bytes 2359304 | tf_op jit(solution)/shard_map/ppermute | solution.py:22
  51.1 2.1 %all-to-all-done = f32[4,96,512]{2,1,0:T(8,128)S(1)} async-done(((f32[4,96,512]{2,1,0:T(8,128)}), f32[4,96,512]{2,1,0:T(8,128)S(1)}, u32[]{:S(2)}, u32[]{:S(2)}) %all-to-all-start) | async-done | bytes 786464 | tf_op jit(solution)/shard_map/all_to_all | solution.py:39
  53.7 1.8 %collective-permute-start.21 = (bf16[96,512]{1,0:T(8,128)(2,1)S(1)}, bf16[96,512]{1,0:T(8,128)(2,1)S(1)}, u32[]{:S(2)}, u32[]{:S(2)}) collective-permute-start(bf16[96,512]{1,0:T(8,128)(2,1)S(1)} %get-tuple-element.67.refs_0_), channel_id=1, source_target_pairs={{0,2},{1,3},{2,0},{3,1},{4,6},{5,7},{6,4},{7,5},{8,10},{9,11},{10,... | collective-permute-start | bytes 294920 | tf_op jit(solution)/shard_map/ppermute | solution.py:22
  55.5 0.9 collective-permute-start.22
  56.3 11.5 %trunk_backward.1 = (f32[520,512]{1,0:T(8,128)}, f32[520,512]{1,0:T(8,128)}) custom-call(s32[1]{0:T(128)} %bitcast.core, s32[2,2048]{1,0:T(2,128)} %index.3, bf16[384,2048]{1,0:T(8,128)(2,1)} %get-tuple-element.40.misfit, bf16[384,512]{1,0:T(8,128)(2,1)} %get-tuple-element.41.coeffs, f32[2048,512]{1,0:T(8,128)} %get-tuple-element.42.first_act, ...), custom_call_target="tpu_custom_call" | custom-call | flops 6442450944 | bytes 8000000 | tf_op jit(solution)/shard_map/trunk_backward/pallas_call | solution.py:292
  67.8 1.2 collective-permute-start.23
  69.0 2.6 %collective-permute-start.6 = (f32[520,512]{1,0:T(8,128)}, f32[520,512]{1,0:T(8,128)S(1)}, u32[]{:S(2)}, u32[]{:S(2)}) collective-permute-start(f32[520,512]{1,0:T(8,128)} %get-tuple-element.45), channel_id=1, source_target_pairs={{0,4},{4,0},{1,5},{5,1},{2,6},{6,2},{3,7},{7,3},{8,12},{12,8},{9,1... | collective-permute-start | bytes 3194888 | tf_op jit(solution)/shard_map/ppermute | solution.py:43
  72.1 1.9 %collective-permute-start.28 = (bf16[384,256]{1,0:T(8,128)(2,1)S(1)}, bf16[384,256]{1,0:T(8,128)(2,1)S(1)}, u32[]{:S(2)}, u32[]{:S(2)}) collective-permute-start(bf16[384,256]{1,0:T(8,128)(2,1)S(1)} %get-tuple-element.51), channel_id=1, source_target_pairs={{0,24},{8,0},{16,8},{24,16},{1,25},{9,1},{17,9},{25,17},{2,26},{10... | collective-permute-start | bytes 589832 | tf_op jit(solution)/shard_map/ppermute | solution.py:22
  74.1 0.8 fusion.4
  74.9 1.4 collective-permute-start.26
  76.3 12.3 %collective-permute-done.28 = bf16[384,256]{1,0:T(8,128)(2,1)S(1)} collective-permute-done((bf16[384,256]{1,0:T(8,128)(2,1)S(1)}, bf16[384,256]{1,0:T(8,128)(2,1)S(1)}, u32[]{:S(2)}, u32[]{:S(2)}) %collective-permute-start.28) | collective-permute-done | bytes 196640 | tf_op jit(solution)/shard_map/ppermute | solution.py:22
  88.6 3.7 %collective-permute-start.24 = (bf16[384,256]{1,0:T(8,128)(2,1)S(1)}, bf16[384,256]{1,0:T(8,128)(2,1)S(1)}, u32[]{:S(2)}, u32[]{:S(2)}) collective-permute-start(bf16[384,256]{1,0:T(8,128)(2,1)S(1)} %get-tuple-element.51), channel_id=1, source_target_pairs={{0,8},{8,16},{16,24},{24,0},{1,9},{9,17},{17,25},{25,1},{2,10},{10... | collective-permute-start | bytes 589832 | tf_op jit(solution)/shard_map/ppermute | solution.py:22
  92.4 2.5 %fusion.24 = f32[1024,256]{1,0:T(8,128)} fusion(bf16[1024,384]{1,0:T(8,128)(2,1)} %collective-permute-done.27, bf16[384,256]{1,0:T(8,128)(2,1)S(1)} %collective-permute-done.28), kind=kOutput, calls=%fused_computation.44 | convolution fusion | flops 201326592 | bytes 2031616 | tf_op jit(solution)/shard_map/dot_general | solution.py:618
  94.9 0.8 collective-permute-start.30
  95.7 2.5 %fusion.23 = f32[1024,256]{1,0:T(8,128)} fusion(bf16[1024,384]{1,0:T(8,128)(2,1)} %collective-permute-done.25, bf16[384,256]{1,0:T(8,128)(2,1)S(1)} %collective-permute-done.26), kind=kOutput, calls=%fused_computation.43 | convolution fusion | flops 201326592 | bytes 2031616 | tf_op jit(solution)/shard_map/dot_general | solution.py:618
  98.2 1.4 fusion.22
  100.0 1.0 convert_element_type.52
  101.0 7.7 %all-to-all-start.1 = ((f16[16,40,512]{2,1,0:T(8,128)(2,1)}), f16[16,40,512]{2,1,0:T(8,128)(2,1)}, u32[]{:S(2)}, u32[]{:S(2)}) async-start(f16[16,40,512]{2,1,0:T(8,128)(2,1)} %convert_element_type.52), calls=%async_computation.1 | async-start | bytes 1310720 | tf_op jit(solution)/shard_map/all_to_all | solution.py:39
  108.7 2.6 %fusion.1 = f32[1024,256]{1,0:T(8,128)S(1)} fusion(f32[1024,256]{1,0:T(8,128)} %fusion.24, f32[1024,256]{1,0:T(8,128)} %fusion.23, f32[1024,256]{1,0:T(8,128)} %fusion.22, bf16[1024,384]{1,0:T(8,128)(2,1)} %get-tuple-element.50, bf16[384,256]{1,0:T(8,128)(2,1)S(1)} %get-tuple-element.51), kind=kOutput, calls=%fused_computation.2 | convolution fusion | flops 202113024 | bytes 5177344 | tf_op jit(solution)/shard_map/dot_general | solution.py:616
  111.3 1.0 fusion.7
  112.4 0.7 fusion.16
  113.1 2.5 %collective-permute-start.33 = (f32[72,256]{1,0:T(8,128)}, f32[72,256]{1,0:T(8,128)}, u32[]{:S(2)}, u32[]{:S(2)}) collective-permute-start(f32[72,256]{1,0:T(8,128)} %get-tuple-element.71), channel_id=1, source_target_pairs={{0,24},{8,0},{16,8},{24,16},{1,25},{9,1},{17,9},{25,17},{2,26},{10... | collective-permute-start | bytes 221192 | tf_op jit(solution)/shard_map/ppermute | solution.py:22
  116.8 4.4 %all-to-all-done.1 = f16[16,40,512]{2,1,0:T(8,128)(2,1)} async-done(((f16[16,40,512]{2,1,0:T(8,128)(2,1)}), f16[16,40,512]{2,1,0:T(8,128)(2,1)}, u32[]{:S(2)}, u32[]{:S(2)}) %all-to-all-start.1) | async-done | bytes 655392 | tf_op jit(solution)/shard_map/all_to_all | solution.py:39
  121.1 1.2 convert_element_type.53.got
  122.5 1.7 collective-permute-start.7
  124.2 0.8 dynamic-slice_bitcast_fusion
  125.1 2.0 %collective-permute-start.29 = (f32[8,64,256]{2,1,0:T(8,128)}, f32[8,64,256]{2,1,0:T(8,128)}, u32[]{:S(2)}, u32[]{:S(2)}) collective-permute-start(f32[8,64,256]{2,1,0:T(8,128)} %dynamic-slice_bitcast_fusion), channel_id=1, source_target_pairs={{0,4},{4,0},{1,5},{5,1},{2,6},{6,2},{3,7},{7,3},{8,12},{12,8},{9,1... | collective-permute-start | bytes 1572872 | tf_op jit(solution)/shard_map/ppermute | solution.py:43
  127.1 0.9 add.92
  128.0 3.1 %collective-permute-start.8 = (f32[40,512]{1,0:T(8,128)S(1)}, f32[40,512]{1,0:T(8,128)S(1)}, u32[]{:S(2)}, u32[]{:S(2)}) collective-permute-start(f32[40,512]{1,0:T(8,128)S(1)} %add.92), channel_id=1, source_target_pairs={{0,64},{32,96},{64,0},{96,32},{128,192},{160,224},{192,128},{224,1... | collective-permute-start | bytes 245768 | tf_op jit(solution)/shard_map/ppermute | solution.py:330
  131.1 1.0 fusion.14
  132.1 1.7 collective-permute-done.8
  133.8 3.8 %collective-permute-start.9 = (f32[40,512]{1,0:T(8,128)S(1)}, f32[40,512]{1,0:T(8,128)S(1)}, u32[]{:S(2)}, u32[]{:S(2)}) collective-permute-start(f32[40,512]{1,0:T(8,128)S(1)} %add.93), channel_id=1, source_target_pairs={{0,192},{32,224},{64,128},{96,160},{128,64},{160,96},{192,0},{224,... | collective-permute-start | bytes 245768 | tf_op jit(solution)/shard_map/ppermute | solution.py:330
  137.6 1.3 z_messages.1
  138.9 0.8 convert_element_type.65
  139.7 3.4 %all-to-all-start.2 = ((f16[8,80,256]{2,1,0:T(8,128)(2,1)}), f16[8,80,256]{2,1,0:T(8,128)(2,1)S(1)}, u32[]{:S(2)}, u32[]{:S(2)}) async-start(f16[8,80,256]{2,1,0:T(8,128)(2,1)} %convert_element_type.65), calls=%async_computation.2 | async-start | bytes 655360 | tf_op jit(solution)/shard_map/all_to_all | solution.py:39
  143.3 0.7 collective-permute-start.12
  144.0 1.6 collective-permute-start.11
  146.2 2.1 %collective-permute-done.11 = f16[40,512]{1,0:T(8,128)(2,1)S(1)} collective-permute-done((f16[40,512]{1,0:T(8,128)(2,1)S(1)}, f16[40,512]{1,0:T(8,128)(2,1)S(1)}, u32[]{:S(2)}, u32[]{:S(2)}) %collective-permute-start.11) | collective-permute-done | bytes 40992 | tf_op jit(solution)/shard_map/ppermute | solution.py:22
  148.4 1.3 collective-permute-done.10
  149.8 1.5 collective-permute-start.14
  151.3 1.2 collective-permute-start.15
  152.5 6.5 %collective-permute-start.16 = (f16[4,40,512]{2,1,0:T(8,128)(2,1)S(1)}, f16[4,40,512]{2,1,0:T(8,128)(2,1)}, u32[]{:S(2)}, u32[]{:S(2)}) collective-permute-start(f16[4,40,512]{2,1,0:T(8,128)(2,1)S(1)} %get-tuple-element.72), channel_id=1, source_target_pairs={{0,4},{4,0},{1,5},{5,1},{2,6},{6,2},{3,7},{7,3},{8,12},{12,8},{9,1... | collective-permute-start | bytes 491528 | tf_op jit(solution)/shard_map/ppermute | solution.py:43
  159.0 5.0 %collective-permute-start.17 = (f16[4,40,512]{2,1,0:T(8,128)(2,1)S(1)}, f16[4,40,512]{2,1,0:T(8,128)(2,1)}, u32[]{:S(2)}, u32[]{:S(2)}) collective-permute-start(f16[4,40,512]{2,1,0:T(8,128)(2,1)S(1)} %collective-permute-done.13), channel_id=1, source_target_pairs={{0,4},{4,0},{1,5},{5,1},{2,6},{6,2},{3,7},{7,3},{8,12},{12,8},{9,1... | collective-permute-start | bytes 491528 | tf_op jit(solution)/shard_map/ppermute | solution.py:43
  164.0 0.9 collective-permute-start.19
  165.0 0.7 z_finished.1
  165.8 0.9 convert_element_type.60.refs_4_
  166.8 0.9 convert_element_type.61.refs_5_
  167.8 0.9 convert_element_type.62.refs_6_
  168.7 0.9 convert_element_type.63.refs_7_
  169.7 2.1 %finished.1 = (f32[512,512]{1,0:T(8,128)}, f32[512,512]{1,0:T(8,128)}, f32[2,512]{1,0:T(2,128)}, f32[1,512]{1,0:T(1,128)}, f32[1,512]{1,0:T(1,128)}, /*index=5*/...) custom-call(s32[3]{0:T(128)S(1)} %pad_add_fusion.place, f32[4,40,512]{2,1,0:T(8,128)S(1)} %get-tuple-element.73.refs_0_, ...), custom_call_target="tpu_custom_call" | custom-call | tf_op jit(solution)/shard_map/finished/pallas_call | solution.py:485
  (84 shorter events, 5.0 us)
Async XLA Ops:
  0.6 1.6 copy-start
  0.7 6.6 %copy-start.2 = (bf16[256,512]{1,0:T(8,128)(2,1)S(1)}, bf16[256,512]{1,0:T(8,128)(2,1)}, u32[]{:S(2)}) copy-start(bf16[256,512]{1,0:T(8,128)(2,1)} %refs_5_.1) | copy-start | bytes 786436
  5.1 15.3 %copy-start.10 = (bf16[384,256]{1,0:T(8,128)(2,1)}, bf16[384,256]{1,0:T(8,128)(2,1)S(1)}, u32[]{:S(2)}) copy-start(bf16[384,256]{1,0:T(8,128)(2,1)S(1)} %get-tuple-element.74.refs_0_) | copy-start | bytes 589828
  5.1 7.2 %collective-permute-start = (bf16[384,256]{1,0:T(8,128)(2,1)S(1)}, bf16[384,256]{1,0:T(8,128)(2,1)S(1)}, u32[]{:S(2)}, u32[]{:S(2)}) collective-permute-start(bf16[384,256]{1,0:T(8,128)(2,1)S(1)} %get-tuple-element.74.refs_0_), channel_id=1, source_target_pairs={{0,1},{1,2},{2,3},{3,0},{4,5},{5,6},{6,7},{7,4},{8,9},{9,10},{10,1... | collective-permute-start | bytes 589832 | tf_op jit(solution)/shard_map/ppermute | solution.py:22
  7.2 23.0 %collective-permute-start.3 = (bf16[256,512]{1,0:T(8,128)(2,1)S(1)}, bf16[256,512]{1,0:T(8,128)(2,1)S(1)}, u32[]{:S(2)}, u32[]{:S(2)}) collective-permute-start(bf16[256,512]{1,0:T(8,128)(2,1)S(1)} %copy-done.2), channel_id=1, source_target_pairs={{0,1},{1,2},{2,3},{3,0},{4,5},{5,6},{6,7},{7,4},{8,9},{9,10},{10,1... | collective-permute-start | bytes 786440 | tf_op jit(solution)/shard_map/ppermute | solution.py:22
  8.5 21.8 %collective-permute-start.4 = (bf16[256,512]{1,0:T(8,128)(2,1)S(1)}, bf16[256,512]{1,0:T(8,128)(2,1)S(1)}, u32[]{:S(2)}, u32[]{:S(2)}) collective-permute-start(bf16[256,512]{1,0:T(8,128)(2,1)S(1)} %copy-done.2), channel_id=1, source_target_pairs={{0,2},{1,3},{2,0},{3,1},{4,6},{5,7},{6,4},{7,5},{8,10},{9,11},{10,... | collective-permute-start | bytes 786440 | tf_op jit(solution)/shard_map/ppermute | solution.py:22
  9.8 20.5 %collective-permute-start.5 = (bf16[256,512]{1,0:T(8,128)(2,1)S(1)}, bf16[256,512]{1,0:T(8,128)(2,1)S(1)}, u32[]{:S(2)}, u32[]{:S(2)}) collective-permute-start(bf16[256,512]{1,0:T(8,128)(2,1)S(1)} %copy-done.2), channel_id=1, source_target_pairs={{0,3},{1,0},{2,1},{3,2},{4,7},{5,4},{6,5},{7,6},{8,11},{9,8},{10,9... | collective-permute-start | bytes 786440 | tf_op jit(solution)/shard_map/ppermute | solution.py:22
  11.8 17.8 %collective-permute-start.1 = (bf16[384,256]{1,0:T(8,128)(2,1)S(1)}, bf16[384,256]{1,0:T(8,128)(2,1)}, u32[]{:S(2)}, u32[]{:S(2)}) collective-permute-start(bf16[384,256]{1,0:T(8,128)(2,1)S(1)} %get-tuple-element.74.refs_0_), channel_id=1, source_target_pairs={{0,2},{1,3},{2,0},{3,1},{4,6},{5,7},{6,4},{7,5},{8,10},{9,11},{10,... | collective-permute-start | bytes 589832 | tf_op jit(solution)/shard_map/ppermute | solution.py:22
  12.3 8.2 %copy-start.11 = (bf16[384,256]{1,0:T(8,128)(2,1)}, bf16[384,256]{1,0:T(8,128)(2,1)S(1)}, u32[]{:S(2)}) copy-start(bf16[384,256]{1,0:T(8,128)(2,1)S(1)} %collective-permute-done.refs_1_) | copy-start | bytes 589828
  12.3 18.0 %collective-permute-start.2 = (bf16[384,256]{1,0:T(8,128)(2,1)S(1)}, bf16[384,256]{1,0:T(8,128)(2,1)}, u32[]{:S(2)}, u32[]{:S(2)}) collective-permute-start(bf16[384,256]{1,0:T(8,128)(2,1)S(1)} %get-tuple-element.74.refs_0_), channel_id=1, source_target_pairs={{0,3},{1,0},{2,1},{3,2},{4,7},{5,4},{6,5},{7,6},{8,11},{9,8},{10,9... | collective-permute-start | bytes 589832 | tf_op jit(solution)/shard_map/ppermute | solution.py:22
  30.3 0.7 copy-start.7
  30.3 0.8 copy-start.8
  30.3 0.9 copy-start.9
  36.9 16.3 %all-to-all-start = ((f32[4,96,512]{2,1,0:T(8,128)}), f32[4,96,512]{2,1,0:T(8,128)S(1)}, u32[]{:S(2)}, u32[]{:S(2)}) async-start(f32[4,96,512]{2,1,0:T(8,128)} %bitcast.74), calls=%async_computation | async-start | bytes 1572864 | tf_op jit(solution)/shard_map/all_to_all | solution.py:39
  48.0 26.9 %collective-permute-start.27 = (bf16[1024,384]{1,0:T(8,128)(2,1)}, bf16[1024,384]{1,0:T(8,128)(2,1)}, u32[]{:S(2)}, u32[]{:S(2)}) collective-permute-start(bf16[1024,384]{1,0:T(8,128)(2,1)} %get-tuple-element.54), channel_id=1, source_target_pairs={{0,24},{8,0},{16,8},{24,16},{1,25},{9,1},{17,9},{25,17},{2,26},{10... | collective-permute-start | bytes 2359304 | tf_op jit(solution)/shard_map/ppermute | solution.py:22
  50.8 44.1 %collective-permute-start.25 = (bf16[1024,384]{1,0:T(8,128)(2,1)}, bf16[1024,384]{1,0:T(8,128)(2,1)}, u32[]{:S(2)}, u32[]{:S(2)}) collective-permute-start(bf16[1024,384]{1,0:T(8,128)(2,1)} %get-tuple-element.53), channel_id=1, source_target_pairs={{0,16},{8,24},{16,0},{24,8},{1,17},{9,25},{17,1},{25,9},{2,18},{10... | collective-permute-start | bytes 2359304 | tf_op jit(solution)/shard_map/ppermute | solution.py:22
  53.3 14.5 %collective-permute-start.20 = (bf16[96,512]{1,0:T(8,128)(2,1)S(1)}, bf16[96,512]{1,0:T(8,128)(2,1)S(1)}, u32[]{:S(2)}, u32[]{:S(2)}) collective-permute-start(bf16[96,512]{1,0:T(8,128)(2,1)S(1)} %get-tuple-element.67.refs_0_), channel_id=1, source_target_pairs={{0,1},{1,2},{2,3},{3,0},{4,5},{5,6},{6,7},{7,4},{8,9},{9,10},{10,1... | collective-permute-start | bytes 294920 | tf_op jit(solution)/shard_map/ppermute | solution.py:22
  53.7 15.4 %collective-permute-start.21 = (bf16[96,512]{1,0:T(8,128)(2,1)S(1)}, bf16[96,512]{1,0:T(8,128)(2,1)S(1)}, u32[]{:S(2)}, u32[]{:S(2)}) collective-permute-start(bf16[96,512]{1,0:T(8,128)(2,1)S(1)} %get-tuple-element.67.refs_0_), channel_id=1, source_target_pairs={{0,2},{1,3},{2,0},{3,1},{4,6},{5,7},{6,4},{7,5},{8,10},{9,11},{10,... | collective-permute-start | bytes 294920 | tf_op jit(solution)/shard_map/ppermute | solution.py:22
  55.5 16.2 %collective-permute-start.22 = (bf16[96,512]{1,0:T(8,128)(2,1)S(1)}, bf16[96,512]{1,0:T(8,128)(2,1)S(1)}, u32[]{:S(2)}, u32[]{:S(2)}) collective-permute-start(bf16[96,512]{1,0:T(8,128)(2,1)S(1)} %get-tuple-element.67.refs_0_), channel_id=1, source_target_pairs={{0,3},{1,0},{2,1},{3,2},{4,7},{5,4},{6,5},{7,6},{8,11},{9,8},{10,9... | collective-permute-start | bytes 294920 | tf_op jit(solution)/shard_map/ppermute | solution.py:22
  56.3 15.3 %copy-start.3 = (bf16[256,512]{1,0:T(8,128)(2,1)S(1)}, bf16[256,512]{1,0:T(8,128)(2,1)}, u32[]{:S(2)}) copy-start(bf16[256,512]{1,0:T(8,128)(2,1)} %refs_5_.1) | copy-start | bytes 786436
  56.3 17.7 %copy-start.6 = (f32[1,512]{1,0:T(1,128)S(1)}, f32[1,512]{1,0:T(1,128)}, u32[]{:S(2)}) copy-start(f32[1,512]{1,0:T(1,128)} %get-tuple-element.47) | copy-start | bytes 6148
  67.8 30.4 %collective-permute-start.23 = (bf16[1024,384]{1,0:T(8,128)(2,1)}, bf16[1024,384]{1,0:T(8,128)(2,1)S(1)}, u32[]{:S(2)}, u32[]{:S(2)}) collective-permute-start(bf16[1024,384]{1,0:T(8,128)(2,1)} %get-tuple-element.52), channel_id=1, source_target_pairs={{0,8},{8,16},{16,24},{24,0},{1,9},{9,17},{17,25},{25,1},{2,10},{10... | collective-permute-start | bytes 2359304 | tf_op jit(solution)/shard_map/ppermute | solution.py:22
  69.0 30.6 %collective-permute-start.6 = (f32[520,512]{1,0:T(8,128)}, f32[520,512]{1,0:T(8,128)S(1)}, u32[]{:S(2)}, u32[]{:S(2)}) collective-permute-start(f32[520,512]{1,0:T(8,128)} %get-tuple-element.45), channel_id=1, source_target_pairs={{0,4},{4,0},{1,5},{5,1},{2,6},{6,2},{3,7},{7,3},{8,12},{12,8},{9,1... | collective-permute-start | bytes 3194888 | tf_op jit(solution)/shard_map/ppermute | solution.py:43
  72.1 16.5 %collective-permute-start.28 = (bf16[384,256]{1,0:T(8,128)(2,1)S(1)}, bf16[384,256]{1,0:T(8,128)(2,1)S(1)}, u32[]{:S(2)}, u32[]{:S(2)}) collective-permute-start(bf16[384,256]{1,0:T(8,128)(2,1)S(1)} %get-tuple-element.51), channel_id=1, source_target_pairs={{0,24},{8,0},{16,8},{24,16},{1,25},{9,1},{17,9},{25,17},{2,26},{10... | collective-permute-start | bytes 589832 | tf_op jit(solution)/shard_map/ppermute | solution.py:22
  74.1 24.1 %copy-start.4 = (f32[8,4,2,8,256]{4,3,1,0,2:T(8,128)}, f32[8,4,2,8,256]{4,3,1,0,2:T(8,128)S(1)}, u32[]{:S(2)}) copy-start(f32[8,4,2,8,256]{4,3,1,0,2:T(8,128)S(1)} %copy.27) | copy-start | bytes 1572868
  74.9 20.8 %collective-permute-start.26 = (bf16[384,256]{1,0:T(8,128)(2,1)S(1)}, bf16[384,256]{1,0:T(8,128)(2,1)S(1)}, u32[]{:S(2)}, u32[]{:S(2)}) collective-permute-start(bf16[384,256]{1,0:T(8,128)(2,1)S(1)} %get-tuple-element.51), channel_id=1, source_target_pairs={{0,16},{8,24},{16,0},{24,8},{1,17},{9,25},{17,1},{25,9},{2,18},{10... | collective-permute-start | bytes 589832 | tf_op jit(solution)/shard_map/ppermute | solution.py:22
  88.6 9.6 %collective-permute-start.24 = (bf16[384,256]{1,0:T(8,128)(2,1)S(1)}, bf16[384,256]{1,0:T(8,128)(2,1)S(1)}, u32[]{:S(2)}, u32[]{:S(2)}) collective-permute-start(bf16[384,256]{1,0:T(8,128)(2,1)S(1)} %get-tuple-element.51), channel_id=1, source_target_pairs={{0,8},{8,16},{16,24},{24,0},{1,9},{9,17},{17,25},{25,1},{2,10},{10... | collective-permute-start | bytes 589832 | tf_op jit(solution)/shard_map/ppermute | solution.py:22
  94.9 4.8 %copy-start.1 = (f32[520,512]{1,0:T(8,128)S(1)}, f32[520,512]{1,0:T(8,128)}, u32[]{:S(2)}) copy-start(f32[520,512]{1,0:T(8,128)} %get-tuple-element.44.mine) | copy-start | bytes 3194884
  94.9 16.4 %collective-permute-start.30 = (f32[264,256]{1,0:T(8,128)}, f32[264,256]{1,0:T(8,128)}, u32[]{:S(2)}, u32[]{:S(2)}) collective-permute-start(f32[264,256]{1,0:T(8,128)} %fusion.4), channel_id=1, source_target_pairs={{0,4},{4,0},{1,5},{5,1},{2,6},{6,2},{3,7},{7,3},{8,12},{12,8},{9,1... | collective-permute-start | bytes 811016 | tf_op jit(solution)/shard_map/ppermute | solution.py:22
  101.0 20.2 %all-to-all-start.1 = ((f16[16,40,512]{2,1,0:T(8,128)(2,1)}), f16[16,40,512]{2,1,0:T(8,128)(2,1)}, u32[]{:S(2)}, u32[]{:S(2)}) async-start(f16[16,40,512]{2,1,0:T(8,128)(2,1)} %convert_element_type.52), calls=%async_computation.1 | async-start | bytes 1310720 | tf_op jit(solution)/shard_map/all_to_all | solution.py:39
  108.7 2.6 %copy-start.5 = (f32[8,4,2,8,256]{4,3,1,0,2:T(8,128)S(1)}, f32[8,4,2,8,256]{4,3,1,0,2:T(8,128)}, u32[]{:S(2)}) copy-start(f32[8,4,2,8,256]{4,3,1,0,2:T(8,128)} %copy-done.4) | copy-start | bytes 1572868
  113.1 18.0 %collective-permute-start.33 = (f32[72,256]{1,0:T(8,128)}, f32[72,256]{1,0:T(8,128)}, u32[]{:S(2)}, u32[]{:S(2)}) collective-permute-start(f32[72,256]{1,0:T(8,128)} %get-tuple-element.71), channel_id=1, source_target_pairs={{0,24},{8,0},{16,8},{24,16},{1,25},{9,1},{17,9},{25,17},{2,26},{10... | collective-permute-start | bytes 221192 | tf_op jit(solution)/shard_map/ppermute | solution.py:22
  115.6 15.4 %collective-permute-start.32 = (f32[72,256]{1,0:T(8,128)}, f32[72,256]{1,0:T(8,128)}, u32[]{:S(2)}, u32[]{:S(2)}) collective-permute-start(f32[72,256]{1,0:T(8,128)} %get-tuple-element.70), channel_id=1, source_target_pairs={{0,16},{8,24},{16,0},{24,8},{1,17},{9,25},{17,1},{25,9},{2,18},{10... | collective-permute-start | bytes 221192 | tf_op jit(solution)/shard_map/ppermute | solution.py:22
  116.2 14.9 %collective-permute-start.31 = (f32[72,256]{1,0:T(8,128)}, f32[72,256]{1,0:T(8,128)}, u32[]{:S(2)}, u32[]{:S(2)}) collective-permute-start(f32[72,256]{1,0:T(8,128)} %get-tuple-element.69), channel_id=1, source_target_pairs={{0,8},{8,16},{16,24},{24,0},{1,9},{9,17},{17,25},{25,1},{2,10},{10... | collective-permute-start | bytes 221192 | tf_op jit(solution)/shard_map/ppermute | solution.py:22
  122.5 4.6 %collective-permute-start.7 = (f32[40,512]{1,0:T(8,128)S(1)}, f32[40,512]{1,0:T(8,128)}, u32[]{:S(2)}, u32[]{:S(2)}) collective-permute-start(f32[40,512]{1,0:T(8,128)S(1)} %plane_total.1), channel_id=1, source_target_pairs={{0,32},{32,0},{64,96},{96,64},{128,160},{160,128},{192,224},{224,1... | collective-permute-start | bytes 245768 | tf_op jit(solution)/shard_map/ppermute | solution.py:330
  125.1 12.5 %collective-permute-start.29 = (f32[8,64,256]{2,1,0:T(8,128)}, f32[8,64,256]{2,1,0:T(8,128)}, u32[]{:S(2)}, u32[]{:S(2)}) collective-permute-start(f32[8,64,256]{2,1,0:T(8,128)} %dynamic-slice_bitcast_fusion), channel_id=1, source_target_pairs={{0,4},{4,0},{1,5},{5,1},{2,6},{6,2},{3,7},{7,3},{8,12},{12,8},{9,1... | collective-permute-start | bytes 1572872 | tf_op jit(solution)/shard_map/ppermute | solution.py:43
  128.0 5.8 %collective-permute-start.8 = (f32[40,512]{1,0:T(8,128)S(1)}, f32[40,512]{1,0:T(8,128)S(1)}, u32[]{:S(2)}, u32[]{:S(2)}) collective-permute-start(f32[40,512]{1,0:T(8,128)S(1)} %add.92), channel_id=1, source_target_pairs={{0,64},{32,96},{64,0},{96,32},{128,192},{160,224},{192,128},{224,1... | collective-permute-start | bytes 245768 | tf_op jit(solution)/shard_map/ppermute | solution.py:330
  133.8 9.3 %collective-permute-start.9 = (f32[40,512]{1,0:T(8,128)S(1)}, f32[40,512]{1,0:T(8,128)S(1)}, u32[]{:S(2)}, u32[]{:S(2)}) collective-permute-start(f32[40,512]{1,0:T(8,128)S(1)} %add.93), channel_id=1, source_target_pairs={{0,192},{32,224},{64,128},{96,160},{128,64},{160,96},{192,0},{224,... | collective-permute-start | bytes 245768 | tf_op jit(solution)/shard_map/ppermute | solution.py:330
  139.7 25.3 %all-to-all-start.2 = ((f16[8,80,256]{2,1,0:T(8,128)(2,1)}), f16[8,80,256]{2,1,0:T(8,128)(2,1)S(1)}, u32[]{:S(2)}, u32[]{:S(2)}) async-start(f16[8,80,256]{2,1,0:T(8,128)(2,1)} %convert_element_type.65), calls=%async_computation.2 | async-start | bytes 655360 | tf_op jit(solution)/shard_map/all_to_all | solution.py:39
  143.3 2.9 %collective-permute-start.12 = (f16[40,512]{1,0:T(8,128)(2,1)S(1)}, f16[40,512]{1,0:T(8,128)(2,1)S(1)}, u32[]{:S(2)}, u32[]{:S(2)}) collective-permute-start(f16[40,512]{1,0:T(8,128)(2,1)S(1)} %convert_bitcast_fusion), channel_id=1, source_target_pairs={{0,3},{1,0},{2,1},{3,2},{4,7},{5,4},{6,5},{7,6},{8,11},{9,8},{10,9... | collective-permute-start | bytes 122888 | tf_op jit(solution)/shard_map/ppermute | solution.py:22
  144.0 4.4 %collective-permute-start.11 = (f16[40,512]{1,0:T(8,128)(2,1)S(1)}, f16[40,512]{1,0:T(8,128)(2,1)S(1)}, u32[]{:S(2)}, u32[]{:S(2)}) collective-permute-start(f16[40,512]{1,0:T(8,128)(2,1)S(1)} %convert_bitcast_fusion), channel_id=1, source_target_pairs={{0,2},{1,3},{2,0},{3,1},{4,6},{5,7},{6,4},{7,5},{8,10},{9,11},{10,... | collective-permute-start | bytes 122888 | tf_op jit(solution)/shard_map/ppermute | solution.py:22
  145.6 4.1 %collective-permute-start.10 = (f16[40,512]{1,0:T(8,128)(2,1)S(1)}, f16[40,512]{1,0:T(8,128)(2,1)S(1)}, u32[]{:S(2)}, u32[]{:S(2)}) collective-permute-start(f16[40,512]{1,0:T(8,128)(2,1)S(1)} %convert_bitcast_fusion), channel_id=1, source_target_pairs={{0,1},{1,2},{2,3},{3,0},{4,5},{5,6},{6,7},{7,4},{8,9},{9,10},{10,1... | collective-permute-start | bytes 122888 | tf_op jit(solution)/shard_map/ppermute | solution.py:22
  149.8 9.2 %collective-permute-start.13 = (f16[4,40,512]{2,1,0:T(8,128)(2,1)S(1)}, f16[4,40,512]{2,1,0:T(8,128)(2,1)S(1)}, u32[]{:S(2)}, u32[]{:S(2)}) collective-permute-start(f16[4,40,512]{2,1,0:T(8,128)(2,1)S(1)} %get-tuple-element.72), channel_id=1, source_target_pairs={{0,8},{8,16},{16,24},{24,0},{1,9},{9,17},{17,25},{25,1},{2,10},{10... | collective-permute-start | bytes 491528 | tf_op jit(solution)/shard_map/ppermute | solution.py:22
  149.8 14.2 %collective-permute-start.14 = (f16[4,40,512]{2,1,0:T(8,128)(2,1)S(1)}, f16[4,40,512]{2,1,0:T(8,128)(2,1)S(1)}, u32[]{:S(2)}, u32[]{:S(2)}) collective-permute-start(f16[4,40,512]{2,1,0:T(8,128)(2,1)S(1)} %get-tuple-element.72), channel_id=1, source_target_pairs={{0,16},{8,24},{16,0},{24,8},{1,17},{9,25},{17,1},{25,9},{2,18},{10... | collective-permute-start | bytes 491528 | tf_op jit(solution)/shard_map/ppermute | solution.py:22
  151.3 12.7 %collective-permute-start.15 = (f16[4,40,512]{2,1,0:T(8,128)(2,1)S(1)}, f16[4,40,512]{2,1,0:T(8,128)(2,1)S(1)}, u32[]{:S(2)}, u32[]{:S(2)}) collective-permute-start(f16[4,40,512]{2,1,0:T(8,128)(2,1)S(1)} %get-tuple-element.72), channel_id=1, source_target_pairs={{0,24},{8,0},{16,8},{24,16},{1,25},{9,1},{17,9},{25,17},{2,26},{10... | collective-permute-start | bytes 491528 | tf_op jit(solution)/shard_map/ppermute | solution.py:22
  152.5 13.3 %collective-permute-start.16 = (f16[4,40,512]{2,1,0:T(8,128)(2,1)S(1)}, f16[4,40,512]{2,1,0:T(8,128)(2,1)}, u32[]{:S(2)}, u32[]{:S(2)}) collective-permute-start(f16[4,40,512]{2,1,0:T(8,128)(2,1)S(1)} %get-tuple-element.72), channel_id=1, source_target_pairs={{0,4},{4,0},{1,5},{5,1},{2,6},{6,2},{3,7},{7,3},{8,12},{12,8},{9,1... | collective-permute-start | bytes 491528 | tf_op jit(solution)/shard_map/ppermute | solution.py:43
  159.0 7.8 %collective-permute-start.17 = (f16[4,40,512]{2,1,0:T(8,128)(2,1)S(1)}, f16[4,40,512]{2,1,0:T(8,128)(2,1)}, u32[]{:S(2)}, u32[]{:S(2)}) collective-permute-start(f16[4,40,512]{2,1,0:T(8,128)(2,1)S(1)} %collective-permute-done.13), channel_id=1, source_target_pairs={{0,4},{4,0},{1,5},{5,1},{2,6},{6,2},{3,7},{7,3},{8,12},{12,8},{9,1... | collective-permute-start | bytes 491528 | tf_op jit(solution)/shard_map/ppermute | solution.py:43
  164.0 3.8 %collective-permute-start.18 = (f16[4,40,512]{2,1,0:T(8,128)(2,1)S(1)}, f16[4,40,512]{2,1,0:T(8,128)(2,1)}, u32[]{:S(2)}, u32[]{:S(2)}) collective-permute-start(f16[4,40,512]{2,1,0:T(8,128)(2,1)S(1)} %collective-permute-done.14), channel_id=1, source_target_pairs={{0,4},{4,0},{1,5},{5,1},{2,6},{6,2},{3,7},{7,3},{8,12},{12,8},{9,1... | collective-permute-start | bytes 491528 | tf_op jit(solution)/shard_map/ppermute | solution.py:43
  164.0 4.7 %collective-permute-start.19 = (f16[4,40,512]{2,1,0:T(8,128)(2,1)S(1)}, f16[4,40,512]{2,1,0:T(8,128)(2,1)}, u32[]{:S(2)}, u32[]{:S(2)}) collective-permute-start(f16[4,40,512]{2,1,0:T(8,128)(2,1)S(1)} %collective-permute-done.15), channel_id=1, source_target_pairs={{0,4},{4,0},{1,5},{5,1},{2,6},{6,2},{3,7},{7,3},{8,12},{12,8},{9,1... | collective-permute-start | bytes 491528 | tf_op jit(solution)/shard_map/ppermute | solution.py:43
